TPU v7x, 32 devices: a whole 2x2x4 slice. The times are simulated.
32 devices in a mesh: wide: 8 (over z, y), narrow: 4 (over x, core).
Axes of the slice: x: 2, y: 2, z: 4, core: 2. Of those that a mesh axis runs over, the one named last changes fastest.
Arguments:
- queries: bfloat16 [2048, 1024], P(('wide', 'narrow')), may hold values from -16 to 16
- documents: bfloat16 [2048, 1024], P(('wide', 'narrow')), may hold values from -16 to 16
- user_ids: int32 [2048], replicated, may hold values from 0 to 1663, as said below
Outputs:
- query_grad: bfloat16 [2048, 1024], P(('wide', 'narrow'))
- doc_grad: bfloat16 [2048, 1024], P(('wide', 'narrow'))
- loss: float32 [], replicated
Inputs may be any that keep to these rules, and one draw needn't show every extreme that they name: `user_ids`: each user id names at most 4 rows; rows with a common id lie in the same quarter of the 2048 rows.
All inputs are finite; a program needn't handle non-finite values.
Results may differ from a plain program's by a relative error of at most 0.004.
The roundings to bfloat16 on the way count: a program that leaves them out, or rounds other values in their place, can miss the bound.
Values may be sent and summed in bfloat16 or wider, within the bound.
No kernel may reach another device: no remote copies, remote signals or barrier semaphores. Data moves between devices by JAX's collectives and lax.ppermute only.
A program may use at most 64 MiB of HBM per device.

v0:
```python
import functools
import math

import jax
import jax.numpy as jnp
from jax import lax
from jax.experimental import pallas as pl
from jax.experimental.pallas import tpu as pltpu
from jax.sharding import Mesh, PartitionSpec as P


QUARTERS = 4
ALL = ("quarter", "lane", "chip", "core")
PLANE = ("lane", "chip")
DIRECT = 8
CHUNK = 256
F32, BF16 = jnp.float32, jnp.bfloat16


def send_pieces(pieces, axes):
    count = len(pieces)
    if count <= DIRECT:
        out = [pieces[0]] + [None] * (count - 1)
        for k in range(count - 1, 0, -1):
            out[k] = lax.ppermute(pieces[k], axes, [(i, i ^ k) for i in range(count)])
        return out
    order = jnp.bitwise_xor(lax.axis_index(axes), jnp.arange(count))
    placed = jnp.take(jnp.stack(pieces), order, axis=0)
    moved = jnp.take(lax.all_to_all(placed, axes, 0, 0, tiled=True), order, axis=0)
    return [pieces[0]] + [moved[k] for k in range(1, count)]


def swap_cores(array):
    return lax.ppermute(array, "core", [(0, 1), (1, 0)])


def tree_sum(terms):
    while len(terms) > 1:
        terms = [terms[i] + terms[i + 1] for i in range(0, len(terms), 2)]
    return terms[0]


def contract(a, b, da, db):
    return lax.dot_general(a, b, (((da,), (db,)), ((), ())), preferred_element_type=F32)


def call(kernel, outs, *args):
    vmem = pl.BlockSpec(memory_space=pltpu.VMEM)
    return pl.pallas_call(
        kernel,
        out_shape=[jax.ShapeDtypeStruct(shape, dtype) for shape, dtype in outs],
        in_specs=[vmem] * len(args),
        out_specs=[vmem] * len(outs),
    )(*args)


def each_chunk(total, body):
    if total <= 2 * CHUNK:
        for i in range(total // CHUNK):
            body(i * CHUNK)
    else:

        @pl.loop(0, total // CHUNK)
        def _(i):
            body(pl.multiple_of(i * CHUNK, CHUNK))


def score_kernel(scale, rows, docs, queries, positive, scores, stats):
    count = docs.shape[0]
    cols = queries.shape[0]
    peak = jnp.full((1, cols), -jnp.inf, F32)
    pos = jnp.zeros((1, rows), F32)
    stats[...] = jnp.zeros(stats.shape, F32)
    stats[0:1, :cols] = peak
    queries_now = queries[...]

    def first(at):
        part = contract(docs[pl.ds(at, CHUNK), :], queries_now, 1, 1) * scale
        scores[pl.ds(at, CHUNK), :] = part
        stats[0:1, :cols] = jnp.maximum(stats[0:1, :cols], jnp.max(part, 0, keepdims=True))
        chosen = jnp.where(positive[pl.ds(at, CHUNK), :] > 0.0, part[:, :rows], 0.0)
        stats[1:2, :rows] += jnp.sum(chosen, 0, keepdims=True)

    each_chunk(count, first)
    peak = stats[0:1, :cols]

    def second(at):
        stats[2:3, :cols] += jnp.sum(jnp.exp(scores[pl.ds(at, CHUNK), :] - peak), 0, keepdims=True)

    each_chunk(count, second)
    stats[0:1, :cols] = peak + jnp.log(stats[2:3, :cols])


def share_kernel(scale, rows, scores, stats, docs, *outs):
    cols = scores.shape[1]
    lse = stats[0:1, :cols]
    total = None
    for at in range(0, scores.shape[0], 2 * CHUNK):
        probs = jnp.exp(scores[at : at + 2 * CHUNK, :] - lse)
        part = contract(jnp.transpose(probs)[rows:].astype(BF16), docs[at : at + 2 * CHUNK, :], 1, 0)
        total = part if total is None else total + part
    total = (total * scale).astype(BF16)
    for k, out in enumerate(outs):
        out[...] = total[k * rows : (k + 1) * rows]


def weight_kernel(batch_rows, rows, scores, s0, s1, s2, s3, counts, total, positive, *outs):
    w_mine, w_send, gains, loss = outs
    cols = scores.shape[1]
    half = scores.shape[0] // 2
    stats = [s[...] for s in (s0, s1, s2, s3)]
    rest = cols // rows
    lses = [
        jnp.concatenate([s[0:1, (k ^ j) * rows : (k ^ j) * rows + rows] for k in range(rest)], 1)
        for j, s in enumerate(stats)
    ]
    top = functools.reduce(jnp.maximum, lses)
    log_denom = top + jnp.log(tree_sum([jnp.exp(a - top) for a in lses]))
    row_counts = counts[...]
    all_pairs = total[...]

    def fill(out, base):
        def body(at):
            src = pl.ds(base + at, CHUNK)
            raw = row_counts * jnp.exp(scores[src, :] - log_denom)
            own = raw[:, : 2 * rows]
            pad = jnp.concatenate([positive[src, :], jnp.zeros((CHUNK, rows), F32)], 1)
            raw = jnp.concatenate([own - pad, raw[:, 2 * rows :]], 1)
            out[pl.ds(at, CHUNK), :] = (batch_rows * raw / all_pairs).astype(BF16)

        each_chunk(half, body)

    fill(w_send, half)
    fill(w_mine, 0)
    factor = batch_rows * row_counts[:, :rows] / all_pairs[:, :rows]
    lanes = [factor * jnp.exp(a[:, :rows] - log_denom[:, :rows]) for a in lses]
    tall = jnp.concatenate(lanes + lanes, 0)
    gains[...] = jnp.transpose(jnp.concatenate([tall, tall], 1))[:rows]
    terms = row_counts * log_denom
    line = tree_sum(
        [
            jnp.sum(terms[:, k * rows : (k + 1) * rows] - stats[k][1:2, :rows], 1, keepdims=True)
            for k in range(rest)
        ]
    )
    loss[...] = jnp.broadcast_to(line, loss.shape)


def own_kernel(scale, w_mine, w_send, docs, out):
    half = w_mine.shape[0]
    rows = out.shape[0]
    total = None
    for base, ref in ((0, w_mine), (half, w_send)):
        for at in range(0, half, CHUNK):
            w = jnp.transpose(ref[at : at + CHUNK, :].astype(F32))[:rows].astype(BF16)
            part = contract(w, docs[base + at : base + at + CHUNK, :], 1, 0)
            total = part if total is None else total + part
    out[...] = total * scale


def doc_kernel(scale, rows, w_mine, w_in, q_mine, q_other, own, *outs):
    half = w_mine.shape[0]

    def body(at):
        part = contract(w_mine[pl.ds(at, CHUNK), :], q_mine[...], 1, 0)
        part = (part + contract(w_in[pl.ds(at, CHUNK), :], q_other[...], 1, 0)) * scale
        if len(outs) == 1 or half != CHUNK:
            outs[0][pl.ds(at, CHUNK), :] = part.astype(BF16)
            return part
        own[...] = part[:rows]
        for k, out in enumerate(outs, 1):
            out[...] = part[k * rows : (k + 1) * rows].astype(BF16)
        return part

    if half == CHUNK:
        body(0)
    else:
        own[...] = body(0)[:rows]

        @pl.loop(1, half // CHUNK)
        def _(i):
            body(pl.multiple_of(i * CHUNK, CHUNK))


def query_sum_kernel(own, gains, *refs):
    *got, out = refs
    total = own[...]
    for k, ref in enumerate(got, 1):
        total = total + gains[:, k : k + 1] * ref[...].astype(F32)
    out[...] = total.astype(BF16)


def doc_sum_kernel(own, *refs):
    *got, out = refs
    total = own[...]
    for ref in got:
        total = total + ref[...].astype(F32)
    out[...] = total.astype(BF16)


def local(queries, documents, user_ids):
    rows, width = queries.shape
    quarters = lax.axis_size("quarter")
    plane = lax.axis_size("lane") * lax.axis_size("chip")
    devices = quarters * plane * 2
    batch_rows = float(devices * rows)
    scale = 3.0 / math.sqrt(width)
    my_quarter = lax.axis_index("quarter")
    my_plane = lax.axis_index(PLANE)
    my_core = lax.axis_index("core")
    cols = quarters * rows
    half = plane * rows
    piece = ((rows, width), BF16)

    d_parts = send_pieces([documents] * plane, PLANE)
    q_parts = send_pieces([queries] * quarters, "quarter")
    d_mine = jnp.concatenate(d_parts, 0)
    d_other = swap_cores(d_mine)
    q_mine = jnp.concatenate(q_parts, 0)
    docs = jnp.concatenate([d_mine, d_other], 0)

    table = user_ids.reshape(quarters, plane, 2, rows)
    quarter_ids = user_ids.reshape(quarters, plane * 2 * rows)
    total = jnp.sum((quarter_ids[:, :, None] == quarter_ids[:, None, :]).astype(F32))
    total = jnp.broadcast_to(total, (1, cols))
    q_order = jnp.bitwise_xor(my_quarter, jnp.arange(quarters))
    q_ids = lax.dynamic_index_in_dim(
        lax.dynamic_index_in_dim(table, my_plane, 1, False), my_core, 1, False
    )
    row_counts = jnp.sum((q_ids[:, :, None] == quarter_ids[:, None, :]).astype(F32), 2)
    counts = jnp.take(row_counts, q_order, axis=0).reshape(1, -1)
    d_order = jnp.bitwise_xor(my_plane, jnp.arange(plane))
    plane_table = jnp.take(lax.dynamic_index_in_dim(table, my_quarter, 0, False), d_order, axis=0)
    d_ids = jnp.concatenate(
        [
            lax.dynamic_index_in_dim(plane_table, my_core, 1, False).reshape(-1),
            lax.dynamic_index_in_dim(plane_table, 1 - my_core, 1, False).reshape(-1),
        ]
    )
    own_ids = lax.dynamic_index_in_dim(q_ids, my_quarter, 0, False)
    positive = (d_ids[:, None] == own_ids[None, :]).astype(F32)

    scores, stats = call(
        functools.partial(score_kernel, scale, rows),
        [((2 * half, cols), F32), ((8, cols), F32)],
        docs,
        q_mine,
        positive,
    )
    stats_all = send_pieces([stats] * quarters, "quarter")
    q_other = swap_cores(q_mine)
    shares = call(
        functools.partial(share_kernel, scale, rows), [piece] * (quarters - 1), scores, stats, docs
    )
    q_got = send_pieces([None] + list(shares), "quarter")

    w_mine, w_send, gains, line_loss = call(
        functools.partial(weight_kernel, batch_rows, rows),
        [((half, cols), BF16), ((half, cols), BF16), ((rows, 8), F32), ((8, 128), F32)],
        scores,
        *stats_all,
        counts,
        total,
        positive,
    )
    w_in = swap_cores(w_send)
    chip_loss = line_loss + swap_cores(line_loss)
    (own_query,) = call(
        functools.partial(own_kernel, scale), [((rows, width), F32)], w_mine, w_send, docs
    )
    spread = plane <= DIRECT
    own_doc, *d_share = call(
        functools.partial(doc_kernel, scale, rows),
        [((rows, width), F32)] + ([piece] * (plane - 1) if spread else [((half, width), BF16)]),
        w_mine,
        w_in,
        q_mine,
        q_other,
    )
    if not spread:
        d_share = [d_share[0][k * rows : (k + 1) * rows] for k in range(1, plane)]
    d_got = send_pieces([d_share[0]] + list(d_share), PLANE)
    plane_loss = tree_sum(send_pieces([chip_loss] * plane, PLANE))
    loss = plane_loss[0, 0] / total[0, 0]
    (doc_grad,) = call(doc_sum_kernel, [piece], own_doc, *d_got[1:])
    (query_grad,) = call(query_sum_kernel, [piece], own_query, gains, *q_got[1:])
    return query_grad, doc_grad, loss


def solution(mesh):
    wide, narrow = mesh.shape["wide"], mesh.shape["narrow"]
    grid = Mesh(mesh.devices.reshape(QUARTERS, wide // QUARTERS, narrow // 2, 2), ALL)

    return jax.shard_map(
        local,
        mesh=grid,
        in_specs=(P(ALL, None), P(ALL, None), P()),
        out_specs=(P(ALL, None), P(ALL, None), P()),
        check_vma=False,
    )
```

profile of v0, /device:TPU:0, one launch (start us, length us, event | category | flops | bytes accessed | tf_op | source)
XLA Modules:
  0.0 67.4 jit_solution(1803471793911603638)
XLA Ops:
  0.6 0.0 copy-start.3
  0.6 3.0 %collective-permute-start = (bf16[64,1024]{1,0:T(8,128)(2,1)}, bf16[64,1024]{1,0:T(8,128)(2,1)S(1)}, u32[]{:S(2)}, u32[]{:S(2)}) collective-permute-start(bf16[64,1024]{1,0:T(8,128)(2,1)} %param.4), channel_id=1, source_target_pairs={{0,2},{2,0},{4,6},{6,4},{1,3},{3,1},{5,7},{7,5},{8,10},{10,8},{12,... | collective-permute-start | bytes 393224 | tf_op jit(solution)/shard_map/ppermute | solution.py:25
  3.7 1.5 %collective-permute-start.1 = (bf16[64,1024]{1,0:T(8,128)(2,1)}, bf16[64,1024]{1,0:T(8,128)(2,1)S(1)}, u32[]{:S(2)}, u32[]{:S(2)}) collective-permute-start(bf16[64,1024]{1,0:T(8,128)(2,1)} %param.4), channel_id=1, source_target_pairs={{0,4},{2,6},{4,0},{6,2},{1,5},{3,7},{5,1},{7,3},{8,12},{10,14},{12... | collective-permute-start | bytes 393224 | tf_op jit(solution)/shard_map/ppermute | solution.py:25
  5.2 0.0 collective-permute-start.2
  5.2 2.0 %collective-permute-start.4 = (bf16[64,1024]{1,0:T(8,128)(2,1)}, bf16[64,1024]{1,0:T(8,128)(2,1)S(1)}, u32[]{:S(2)}, u32[]{:S(2)}) collective-permute-start(bf16[64,1024]{1,0:T(8,128)(2,1)} %param.3), channel_id=1, source_target_pairs={{0,8},{8,0},{16,24},{24,16},{1,9},{9,1},{17,25},{25,17},{2,10},{10... | collective-permute-start | bytes 393224 | tf_op jit(solution)/shard_map/ppermute | solution.py:25
  7.2 2.6 %collective-permute-start.5 = (bf16[64,1024]{1,0:T(8,128)(2,1)}, bf16[64,1024]{1,0:T(8,128)(2,1)S(1)}, u32[]{:S(2)}, u32[]{:S(2)}) collective-permute-start(bf16[64,1024]{1,0:T(8,128)(2,1)} %param.3), channel_id=1, source_target_pairs={{0,16},{8,24},{16,0},{24,8},{1,17},{9,25},{17,1},{25,9},{2,18},{10... | collective-permute-start | bytes 393224 | tf_op jit(solution)/shard_map/ppermute | solution.py:25
  9.9 0.8 %reshape.92 = s32[4,4,2,64]{3,2,1,0:T(2,128)S(1)} reshape(s32[2048]{0:T(1024)} %param.5) | data formatting | bytes 16384 | tf_op jit(solution)/shard_map/reshape | solution.py:222
  10.6 0.7 %eq.51 = s32[4,512]{1,0:T(4,128)S(1)} reshape(s32[2048]{0:T(1024)} %param.5) | data formatting | bytes 16384 | tf_op jit(solution)/shard_map/eq | solution.py:230
  11.4 0.6 gather_fusion
  12.0 0.1 broadcast_select_fusion
  12.1 0.1 reshape.94
  12.1 0.1 reshape.93
  12.2 0.8 %compare_convert_fusion.positive = f32[512,64]{1,0:T(8,128)} fusion(s32[64]{0:T(128)S(1)} %fusion, s32[512]{0:T(512)S(1)} %pad_add_fusion), kind=kLoop, calls=%fused_computation.5 | loop fusion | flops 65536 | bytes 133376 | tf_op jit(solution)/shard_map/convert_element_type | solution.py:241
  13.1 0.2 convert_reduce_fusion.1
  13.3 0.6 gather_fusion.1
  13.8 0.1 broadcast_select_fusion.1
  13.9 0.9 %constant_dynamic-update-slice_fusion.4 = bf16[512,1024]{1,0:T(8,128)(2,1)S(1)} fusion(bf16[64,1024]{1,0:T(8,128)(2,1)} %param.4), kind=kLoop, calls=%fused_computation.10 | loop fusion | bytes 262144
  14.8 0.9 %constant_dynamic-update-slice_fusion.8 = bf16[256,1024]{1,0:T(8,128)(2,1)S(1)} fusion(bf16[64,1024]{1,0:T(8,128)(2,1)} %param.3), kind=kLoop, calls=%fused_computation.14 | loop fusion | bytes 262144
  15.8 0.0 collective-permute-done
  15.8 0.1 collective-permute-start.6
  15.8 0.0 collective-permute-done.1
  15.9 0.0 collective-permute-done.2
  15.9 0.1 collective-permute-start.3
  16.0 0.0 collective-permute-done.4
  16.0 0.0 collective-permute-done.5
  16.1 6.9 %collective-permute-done.6 = bf16[64,1024]{1,0:T(8,128)(2,1)S(1)} collective-permute-done((bf16[64,1024]{1,0:T(8,128)(2,1)}, bf16[64,1024]{1,0:T(8,128)(2,1)S(1)}, u32[]{:S(2)}, u32[]{:S(2)}) %collective-permute-start.6) | collective-permute-done | bytes 131104 | tf_op jit(solution)/shard_map/ppermute | solution.py:25
  22.9 0.1 collective-permute-start.14
  23.1 0.6 copy-done.1
  23.7 1.0 %copy-done = bf16[512,1024]{1,0:T(8,128)(2,1)} copy-done((bf16[512,1024]{1,0:T(8,128)(2,1)}, bf16[512,1024]{1,0:T(8,128)(2,1)S(1)}, u32[]{:S(2)}) %copy-start) | copy-done | bytes 1048600
  24.7 2.7 %shard_map.58 = (f32[512,256]{1,0:T(8,128)}, f32[8,256]{1,0:T(8,128)}) custom-call(bf16[512,1024]{1,0:T(8,128)(2,1)} %copy-done, bf16[256,1024]{1,0:T(8,128)(2,1)} %copy-done.1, f32[512,64]{1,0:T(8,128)} %compare_convert_fusion.positive), custom_call_target="tpu_custom_call" | custom-call | tf_op jit(solution)/shard_map/pallas_call | solution.py:49
  27.4 0.7 %collective-permute-start.7 = (f32[8,256]{1,0:T(8,128)}, f32[8,256]{1,0:T(8,128)S(1)}, u32[]{:S(2)}, u32[]{:S(2)}) collective-permute-start(f32[8,256]{1,0:T(8,128)} %get-tuple-element.17.s0.stats), channel_id=1, source_target_pairs={{0,8},{8,0},{16,24},{24,16},{1,9},{9,1},{17,25},{25,17},{2,10},{10... | collective-permute-start | bytes 24584 | tf_op jit(solution)/shard_map/ppermute | solution.py:25
  28.2 3.6 %collective-permute-start.9 = (f32[8,256]{1,0:T(8,128)}, f32[8,256]{1,0:T(8,128)S(1)}, u32[]{:S(2)}, u32[]{:S(2)}) collective-permute-start(f32[8,256]{1,0:T(8,128)} %get-tuple-element.17.s0.stats), channel_id=1, source_target_pairs={{0,24},{8,16},{16,8},{24,0},{1,25},{9,17},{17,9},{25,1},{2,26},{10... | collective-permute-start | bytes 24584 | tf_op jit(solution)/shard_map/ppermute | solution.py:25
  31.8 1.8 %convert_reduce_fusion = f32[]{:T(128)} fusion(s32[4,512]{1,0:T(4,128)S(1)} %eq.51), kind=kLoop, calls=%fused_computation.2 | loop fusion | flops 3145727 | bytes 8196 | tf_op jit(solution)/shard_map/reduce_sum | solution.py:224
  33.6 0.6 select_n.86.counts
  34.3 0.0 collective-permute-done.9.s3
  34.3 1.2 %broadcast_in_dim.30.total = f32[1,256]{1,0:T(1,128)} broadcast(f32[]{:T(128)} %convert_reduce_fusion), dimensions={} | broadcast | bytes 1028 | tf_op jit(solution)/shard_map/broadcast_in_dim | solution.py:225
  35.5 2.1 %shard_map.59 = (bf16[256,256]{1,0:T(8,128)(2,1)}, bf16[256,256]{1,0:T(8,128)(2,1)}, f32[64,8]{1,0:T(8,128)}, f32[8,128]{1,0:T(8,128)}) custom-call(f32[512,256]{1,0:T(8,128)} %get-tuple-element.16.scores, f32[8,256]{1,0:T(8,128)} %get-tuple-element.17.s0.stats, f32[8,256]{1,0:T(8,128)} %copy-done.11, f32[8,256]{1,0:T(8,128)} %copy-done.12, ...), custom_call_target="tpu_custom_call" | custom-call | tf_op jit(solution)/shard_map/pallas_call | solution.py:49
  37.6 0.1 collective-permute-start.13
  37.6 2.6 %shard_map.61 = (bf16[64,1024]{1,0:T(8,128)(2,1)}, bf16[64,1024]{1,0:T(8,128)(2,1)}, bf16[64,1024]{1,0:T(8,128)(2,1)}) custom-call(f32[512,256]{1,0:T(8,128)} %get-tuple-element.16.scores, f32[8,256]{1,0:T(8,128)} %get-tuple-element.17.s0.stats, bf16[512,1024]{1,0:T(8,128)(2,1)} %copy-done), custom_call_target="tpu_custom_call" | custom-call | tf_op jit(solution)/shard_map/pallas_call | solution.py:49
  40.2 0.6 collective-permute-start.18
  40.8 0.8 %collective-permute-done.18 = f32[8,128]{1,0:T(8,128)S(1)} collective-permute-done((f32[8,128]{1,0:T(8,128)S(1)}, f32[8,128]{1,0:T(8,128)S(1)}, u32[]{:S(2)}, u32[]{:S(2)}) %collective-permute-start.18) | collective-permute-done | bytes 4128 | tf_op jit(solution)/shard_map/ppermute | solution.py:34
  41.6 1.5 %collective-permute-start.20 = (f32[8,128]{1,0:T(8,128)S(1)}, f32[8,128]{1,0:T(8,128)S(1)}, u32[]{:S(2)}, u32[]{:S(2)}) collective-permute-start(f32[8,128]{1,0:T(8,128)S(1)} %add.81), channel_id=1, source_target_pairs={{0,4},{2,6},{4,0},{6,2},{1,5},{3,7},{5,1},{7,3},{8,12},{10,14},{12... | collective-permute-start | bytes 12296 | tf_op jit(solution)/shard_map/ppermute | solution.py:25
  43.1 1.4 %collective-permute-start.21 = (f32[8,128]{1,0:T(8,128)S(1)}, f32[8,128]{1,0:T(8,128)S(1)}, u32[]{:S(2)}, u32[]{:S(2)}) collective-permute-start(f32[8,128]{1,0:T(8,128)S(1)} %add.81), channel_id=1, source_target_pairs={{0,6},{2,4},{4,2},{6,0},{1,7},{3,5},{5,3},{7,1},{8,14},{10,12},{12... | collective-permute-start | bytes 12296 | tf_op jit(solution)/shard_map/ppermute | solution.py:25
  44.6 0.5 collective-permute-start.19
  45.1 2.4 %shard_map.60.own = f32[64,1024]{1,0:T(8,128)} custom-call(bf16[256,256]{1,0:T(8,128)(2,1)} %get-tuple-element.18.w_mine, bf16[256,256]{1,0:T(8,128)(2,1)} %get-tuple-element.19.w_send, bf16[512,1024]{1,0:T(8,128)(2,1)} %copy-done), custom_call_target="tpu_custom_call" | custom-call | tf_op jit(solution)/shard_map/pallas_call | solution.py:49
  47.5 0.0 collective-permute-done.13.w_in
  47.6 3.6 %collective-permute-start.11 = (bf16[64,1024]{1,0:T(8,128)(2,1)S(1)}, bf16[64,1024]{1,0:T(8,128)(2,1)S(1)}, u32[]{:S(2)}, u32[]{:S(2)}) collective-permute-start(bf16[64,1024]{1,0:T(8,128)(2,1)S(1)} %copy-done.16), channel_id=1, source_target_pairs={{0,16},{8,24},{16,0},{24,8},{1,17},{9,25},{17,1},{25,9},{2,18},{10... | collective-permute-start | bytes 393224 | tf_op jit(solution)/shard_map/ppermute | solution.py:25
  51.2 2.6 %shard_map.63 = (f32[64,1024]{1,0:T(8,128)}, bf16[64,1024]{1,0:T(8,128)(2,1)}, bf16[64,1024]{1,0:T(8,128)(2,1)}, bf16[64,1024]{1,0:T(8,128)(2,1)}) custom-call(bf16[256,256]{1,0:T(8,128)(2,1)} %get-tuple-element.18.w_mine, bf16[256,256]{1,0:T(8,128)(2,1)} %copy-done.6, bf16[256,1024]{1,0:T(8,128)(2,1)} %copy-done.1, bf16[256,1024]{1,0:T(8,128)(2,1)} %copy-done.2), custom_call_target="tpu_custom_call" | custom-call | tf_op jit(solution)/shard_map/pallas_call | solution.py:49
  53.7 0.7 %collective-permute-start.12 = (bf16[64,1024]{1,0:T(8,128)(2,1)S(1)}, bf16[64,1024]{1,0:T(8,128)(2,1)S(1)}, u32[]{:S(2)}, u32[]{:S(2)}) collective-permute-start(bf16[64,1024]{1,0:T(8,128)(2,1)S(1)} %copy-done.15), channel_id=1, source_target_pairs={{0,24},{8,16},{16,8},{24,0},{1,25},{9,17},{17,9},{25,1},{2,26},{10... | collective-permute-start | bytes 393224 | tf_op jit(solution)/shard_map/ppermute | solution.py:25
  54.4 0.0 collective-permute-done.21
  54.4 1.5 %collective-permute-start.15 = (bf16[64,1024]{1,0:T(8,128)(2,1)}, bf16[64,1024]{1,0:T(8,128)(2,1)S(1)}, u32[]{:S(2)}, u32[]{:S(2)}) collective-permute-start(bf16[64,1024]{1,0:T(8,128)(2,1)} %get-tuple-element.25), channel_id=1, source_target_pairs={{0,2},{2,0},{4,6},{6,4},{1,3},{3,1},{5,7},{7,5},{8,10},{10,8},{12,... | collective-permute-start | bytes 393224 | tf_op jit(solution)/shard_map/ppermute | solution.py:25
  55.9 0.0 collective-permute-done.19
  55.9 1.5 %collective-permute-start.16 = (bf16[64,1024]{1,0:T(8,128)(2,1)}, bf16[64,1024]{1,0:T(8,128)(2,1)S(1)}, u32[]{:S(2)}, u32[]{:S(2)}) collective-permute-start(bf16[64,1024]{1,0:T(8,128)(2,1)} %get-tuple-element.26), channel_id=1, source_target_pairs={{0,4},{2,6},{4,0},{6,2},{1,5},{3,7},{5,1},{7,3},{8,12},{10,14},{12... | collective-permute-start | bytes 393224 | tf_op jit(solution)/shard_map/ppermute | solution.py:25
  57.5 0.5 collective-permute-start.17
  57.9 0.5 slice.4
  59.8 0.0 collective-permute-done.11.refs_1_
  59.8 0.7 %collective-permute-done.12.refs_2_ = bf16[64,1024]{1,0:T(8,128)(2,1)S(1)} collective-permute-done((bf16[64,1024]{1,0:T(8,128)(2,1)S(1)}, bf16[64,1024]{1,0:T(8,128)(2,1)S(1)}, u32[]{:S(2)}, u32[]{:S(2)}) %collective-permute-start.12) | collective-permute-done | bytes 131104 | tf_op jit(solution)/shard_map/ppermute | solution.py:25
  60.6 0.7 copy-done.7
  61.2 1.9 %shard_map.62 = bf16[64,1024]{1,0:T(8,128)(2,1)} custom-call(f32[64,1024]{1,0:T(8,128)} %shard_map.60.own, f32[64,8]{1,0:T(8,128)} %get-tuple-element.20.gains, bf16[64,1024]{1,0:T(8,128)(2,1)} %copy-done.4, bf16[64,1024]{1,0:T(8,128)(2,1)} %copy-done.5, bf16[64,1024]{1,0:T(8,128)(2,1)} %copy-done.7), custom_call_target="tpu_custom_call" | custom-call | tf_op jit(solution)/shard_map/pallas_call | solution.py:49
  63.2 0.6 collective-permute-done.16.refs_1_
  63.8 0.0 copy-done.8
  63.8 0.6 copy-done.9
  64.4 0.0 copy-done.10
  64.5 1.8 %shard_map.64 = bf16[64,1024]{1,0:T(8,128)(2,1)} custom-call(f32[64,1024]{1,0:T(8,128)} %get-tuple-element.24.own, bf16[64,1024]{1,0:T(8,128)(2,1)} %copy-done.8, bf16[64,1024]{1,0:T(8,128)(2,1)} %copy-done.9, bf16[64,1024]{1,0:T(8,128)(2,1)} %copy-done.10), custom_call_target="tpu_custom_call" | custom-call | tf_op jit(solution)/shard_map/pallas_call | solution.py:49
  (56 shorter events, 0.3 us)
Async XLA Ops:
  0.6 15.2 %copy-start.3 = (bf16[64,1024]{1,0:T(8,128)(2,1)S(1)}, bf16[64,1024]{1,0:T(8,128)(2,1)}, u32[]{:S(2)}) copy-start(bf16[64,1024]{1,0:T(8,128)(2,1)} %param.4) | copy-start | bytes 393220
  0.6 15.1 %collective-permute-start = (bf16[64,1024]{1,0:T(8,128)(2,1)}, bf16[64,1024]{1,0:T(8,128)(2,1)S(1)}, u32[]{:S(2)}, u32[]{:S(2)}) collective-permute-start(bf16[64,1024]{1,0:T(8,128)(2,1)} %param.4), channel_id=1, source_target_pairs={{0,2},{2,0},{4,6},{6,4},{1,3},{3,1},{5,7},{7,5},{8,10},{10,8},{12,... | collective-permute-start | bytes 393224 | tf_op jit(solution)/shard_map/ppermute | solution.py:25
  3.7 12.2 %collective-permute-start.1 = (bf16[64,1024]{1,0:T(8,128)(2,1)}, bf16[64,1024]{1,0:T(8,128)(2,1)S(1)}, u32[]{:S(2)}, u32[]{:S(2)}) collective-permute-start(bf16[64,1024]{1,0:T(8,128)(2,1)} %param.4), channel_id=1, source_target_pairs={{0,4},{2,6},{4,0},{6,2},{1,5},{3,7},{5,1},{7,3},{8,12},{10,14},{12... | collective-permute-start | bytes 393224 | tf_op jit(solution)/shard_map/ppermute | solution.py:25
  5.2 10.7 %collective-permute-start.2 = (bf16[64,1024]{1,0:T(8,128)(2,1)}, bf16[64,1024]{1,0:T(8,128)(2,1)S(1)}, u32[]{:S(2)}, u32[]{:S(2)}) collective-permute-start(bf16[64,1024]{1,0:T(8,128)(2,1)} %param.4), channel_id=1, source_target_pairs={{0,6},{2,4},{4,2},{6,0},{1,7},{3,5},{5,3},{7,1},{8,14},{10,12},{12... | collective-permute-start | bytes 393224 | tf_op jit(solution)/shard_map/ppermute | solution.py:25
  5.2 10.8 %collective-permute-start.4 = (bf16[64,1024]{1,0:T(8,128)(2,1)}, bf16[64,1024]{1,0:T(8,128)(2,1)S(1)}, u32[]{:S(2)}, u32[]{:S(2)}) collective-permute-start(bf16[64,1024]{1,0:T(8,128)(2,1)} %param.3), channel_id=1, source_target_pairs={{0,8},{8,0},{16,24},{24,16},{1,9},{9,1},{17,25},{25,17},{2,10},{10... | collective-permute-start | bytes 393224 | tf_op jit(solution)/shard_map/ppermute | solution.py:25
  7.2 8.8 %collective-permute-start.5 = (bf16[64,1024]{1,0:T(8,128)(2,1)}, bf16[64,1024]{1,0:T(8,128)(2,1)S(1)}, u32[]{:S(2)}, u32[]{:S(2)}) collective-permute-start(bf16[64,1024]{1,0:T(8,128)(2,1)} %param.3), channel_id=1, source_target_pairs={{0,16},{8,24},{16,0},{24,8},{1,17},{9,25},{17,1},{25,9},{2,18},{10... | collective-permute-start | bytes 393224 | tf_op jit(solution)/shard_map/ppermute | solution.py:25
  15.8 7.1 %collective-permute-start.6 = (bf16[64,1024]{1,0:T(8,128)(2,1)}, bf16[64,1024]{1,0:T(8,128)(2,1)S(1)}, u32[]{:S(2)}, u32[]{:S(2)}) collective-permute-start(bf16[64,1024]{1,0:T(8,128)(2,1)} %param.3), channel_id=1, source_target_pairs={{0,24},{8,16},{16,8},{24,0},{1,25},{9,17},{17,9},{25,1},{2,26},{10... | collective-permute-start | bytes 393224 | tf_op jit(solution)/shard_map/ppermute | solution.py:25
  15.9 7.2 %collective-permute-start.3 = (bf16[256,1024]{1,0:T(8,128)(2,1)S(1)}, bf16[256,1024]{1,0:T(8,128)(2,1)S(1)}, u32[]{:S(2)}, u32[]{:S(2)}) collective-permute-start(bf16[256,1024]{1,0:T(8,128)(2,1)S(1)} %pad_maximum_fusion), channel_id=1, source_target_pairs={{0,1},{1,0},{2,3},{3,2},{4,5},{5,4},{6,7},{7,6},{8,9},{9,8},{10,11... | collective-permute-start | bytes 1572872 | tf_op jit(solution)/shard_map/ppermute | solution.py:34
  22.9 0.8 %copy-start.1 = (bf16[256,1024]{1,0:T(8,128)(2,1)}, bf16[256,1024]{1,0:T(8,128)(2,1)S(1)}, u32[]{:S(2)}) copy-start(bf16[256,1024]{1,0:T(8,128)(2,1)S(1)} %constant_dynamic-update-slice_fusion.5.queries.q_mine) | copy-start | bytes 1572868
  22.9 21.7 %collective-permute-start.14 = (bf16[256,1024]{1,0:T(8,128)(2,1)S(1)}, bf16[256,1024]{1,0:T(8,128)(2,1)S(1)}, u32[]{:S(2)}, u32[]{:S(2)}) collective-permute-start(bf16[256,1024]{1,0:T(8,128)(2,1)S(1)} %constant_dynamic-update-slice_fusion.5.queries.q_mine), channel_id=1, source_target_pairs={{0,1},{1,0},{2,3},{3,2},{4,5},{5,4},{6,7},{7,6},{8,9},{9,8},{10,11... | collective-permute-start | bytes 1572872 | tf_op jit(solution)/shard_map/ppermute | solution.py:34
  23.7 1.0 %copy-start = (bf16[512,1024]{1,0:T(8,128)(2,1)}, bf16[512,1024]{1,0:T(8,128)(2,1)S(1)}, u32[]{:S(2)}) copy-start(bf16[512,1024]{1,0:T(8,128)(2,1)S(1)} %constant_dynamic-update-slice_fusion.docs) | copy-start | bytes 3145732
  27.4 6.8 %collective-permute-start.7 = (f32[8,256]{1,0:T(8,128)}, f32[8,256]{1,0:T(8,128)S(1)}, u32[]{:S(2)}, u32[]{:S(2)}) collective-permute-start(f32[8,256]{1,0:T(8,128)} %get-tuple-element.17.s0.stats), channel_id=1, source_target_pairs={{0,8},{8,0},{16,24},{24,16},{1,9},{9,1},{17,25},{25,17},{2,10},{10... | collective-permute-start | bytes 24584 | tf_op jit(solution)/shard_map/ppermute | solution.py:25
  28.2 6.1 %collective-permute-start.8 = (f32[8,256]{1,0:T(8,128)}, f32[8,256]{1,0:T(8,128)S(1)}, u32[]{:S(2)}, u32[]{:S(2)}) collective-permute-start(f32[8,256]{1,0:T(8,128)} %get-tuple-element.17.s0.stats), channel_id=1, source_target_pairs={{0,16},{8,24},{16,0},{24,8},{1,17},{9,25},{17,1},{25,9},{2,18},{10... | collective-permute-start | bytes 24584 | tf_op jit(solution)/shard_map/ppermute | solution.py:25
  28.2 6.1 %collective-permute-start.9 = (f32[8,256]{1,0:T(8,128)}, f32[8,256]{1,0:T(8,128)S(1)}, u32[]{:S(2)}, u32[]{:S(2)}) collective-permute-start(f32[8,256]{1,0:T(8,128)} %get-tuple-element.17.s0.stats), channel_id=1, source_target_pairs={{0,24},{8,16},{16,8},{24,0},{1,25},{9,17},{17,9},{25,1},{2,26},{10... | collective-permute-start | bytes 24584 | tf_op jit(solution)/shard_map/ppermute | solution.py:25
  34.3 1.2 %copy-start.11 = (f32[8,256]{1,0:T(8,128)}, f32[8,256]{1,0:T(8,128)S(1)}, u32[]{:S(2)}) copy-start(f32[8,256]{1,0:T(8,128)S(1)} %collective-permute-done.7.s1) | copy-start | bytes 24580
  34.3 1.2 %copy-start.12 = (f32[8,256]{1,0:T(8,128)}, f32[8,256]{1,0:T(8,128)S(1)}, u32[]{:S(2)}) copy-start(f32[8,256]{1,0:T(8,128)S(1)} %collective-permute-done.8.s2) | copy-start | bytes 24580
  34.3 1.2 %copy-start.13 = (f32[8,256]{1,0:T(8,128)}, f32[8,256]{1,0:T(8,128)S(1)}, u32[]{:S(2)}) copy-start(f32[8,256]{1,0:T(8,128)S(1)} %collective-permute-done.9.s3) | copy-start | bytes 24580
  37.6 2.7 %copy-start.14 = (f32[8,128]{1,0:T(8,128)S(1)}, f32[8,128]{1,0:T(8,128)}, u32[]{:S(2)}) copy-start(f32[8,128]{1,0:T(8,128)} %get-tuple-element.28) | copy-start | bytes 12292
  37.6 10.0 %collective-permute-start.13 = (bf16[256,256]{1,0:T(8,128)(2,1)}, bf16[256,256]{1,0:T(8,128)(2,1)S(1)}, u32[]{:S(2)}, u32[]{:S(2)}) collective-permute-start(bf16[256,256]{1,0:T(8,128)(2,1)} %get-tuple-element.19.w_send), channel_id=1, source_target_pairs={{0,1},{1,0},{2,3},{3,2},{4,5},{5,4},{6,7},{7,6},{8,9},{9,8},{10,11... | collective-permute-start | bytes 393224 | tf_op jit(solution)/shard_map/ppermute | solution.py:34
  40.2 7.3 %copy-start.16 = (bf16[64,1024]{1,0:T(8,128)(2,1)S(1)}, bf16[64,1024]{1,0:T(8,128)(2,1)}, u32[]{:S(2)}) copy-start(bf16[64,1024]{1,0:T(8,128)(2,1)} %get-tuple-element.22) | copy-start | bytes 393220
  40.2 17.2 %collective-permute-start.10 = (bf16[64,1024]{1,0:T(8,128)(2,1)}, bf16[64,1024]{1,0:T(8,128)(2,1)S(1)}, u32[]{:S(2)}, u32[]{:S(2)}) collective-permute-start(bf16[64,1024]{1,0:T(8,128)(2,1)} %get-tuple-element.21), channel_id=1, source_target_pairs={{0,8},{8,0},{16,24},{24,16},{1,9},{9,1},{17,25},{25,17},{2,10},{10... | collective-permute-start | bytes 393224 | tf_op jit(solution)/shard_map/ppermute | solution.py:25
  40.2 1.4 %collective-permute-start.18 = (f32[8,128]{1,0:T(8,128)S(1)}, f32[8,128]{1,0:T(8,128)S(1)}, u32[]{:S(2)}, u32[]{:S(2)}) collective-permute-start(f32[8,128]{1,0:T(8,128)S(1)} %copy-done.14), channel_id=1, source_target_pairs={{0,1},{1,0},{2,3},{3,2},{4,5},{5,4},{6,7},{7,6},{8,9},{9,8},{10,11... | collective-permute-start | bytes 12296 | tf_op jit(solution)/shard_map/ppermute | solution.py:34
  41.6 12.1 %collective-permute-start.20 = (f32[8,128]{1,0:T(8,128)S(1)}, f32[8,128]{1,0:T(8,128)S(1)}, u32[]{:S(2)}, u32[]{:S(2)}) collective-permute-start(f32[8,128]{1,0:T(8,128)S(1)} %add.81), channel_id=1, source_target_pairs={{0,4},{2,6},{4,0},{6,2},{1,5},{3,7},{5,1},{7,3},{8,12},{10,14},{12... | collective-permute-start | bytes 12296 | tf_op jit(solution)/shard_map/ppermute | solution.py:25
  43.1 11.3 %collective-permute-start.21 = (f32[8,128]{1,0:T(8,128)S(1)}, f32[8,128]{1,0:T(8,128)S(1)}, u32[]{:S(2)}, u32[]{:S(2)}) collective-permute-start(f32[8,128]{1,0:T(8,128)S(1)} %add.81), channel_id=1, source_target_pairs={{0,6},{2,4},{4,2},{6,0},{1,7},{3,5},{5,3},{7,1},{8,14},{10,12},{12... | collective-permute-start | bytes 12296 | tf_op jit(solution)/shard_map/ppermute | solution.py:25
  44.6 6.6 %copy-start.2 = (bf16[256,1024]{1,0:T(8,128)(2,1)}, bf16[256,1024]{1,0:T(8,128)(2,1)S(1)}, u32[]{:S(2)}) copy-start(bf16[256,1024]{1,0:T(8,128)(2,1)S(1)} %collective-permute-done.14.q_other) | copy-start | bytes 1572868
  44.6 11.3 %collective-permute-start.19 = (f32[8,128]{1,0:T(8,128)S(1)}, f32[8,128]{1,0:T(8,128)S(1)}, u32[]{:S(2)}, u32[]{:S(2)}) collective-permute-start(f32[8,128]{1,0:T(8,128)S(1)} %add.81), channel_id=1, source_target_pairs={{0,2},{2,0},{4,6},{6,4},{1,3},{3,1},{5,7},{7,5},{8,10},{10,8},{12,... | collective-permute-start | bytes 12296 | tf_op jit(solution)/shard_map/ppermute | solution.py:25
  47.5 6.2 %copy-start.15 = (bf16[64,1024]{1,0:T(8,128)(2,1)S(1)}, bf16[64,1024]{1,0:T(8,128)(2,1)}, u32[]{:S(2)}) copy-start(bf16[64,1024]{1,0:T(8,128)(2,1)} %get-tuple-element.23) | copy-start | bytes 393220
  47.5 3.6 %copy-start.6 = (bf16[256,256]{1,0:T(8,128)(2,1)}, bf16[256,256]{1,0:T(8,128)(2,1)S(1)}, u32[]{:S(2)}) copy-start(bf16[256,256]{1,0:T(8,128)(2,1)S(1)} %collective-permute-done.13.w_in) | copy-start | bytes 393220
  47.6 12.2 %collective-permute-start.11 = (bf16[64,1024]{1,0:T(8,128)(2,1)S(1)}, bf16[64,1024]{1,0:T(8,128)(2,1)S(1)}, u32[]{:S(2)}, u32[]{:S(2)}) collective-permute-start(bf16[64,1024]{1,0:T(8,128)(2,1)S(1)} %copy-done.16), channel_id=1, source_target_pairs={{0,16},{8,24},{16,0},{24,8},{1,17},{9,25},{17,1},{25,9},{2,18},{10... | collective-permute-start | bytes 393224 | tf_op jit(solution)/shard_map/ppermute | solution.py:25
  53.7 6.8 %collective-permute-start.12 = (bf16[64,1024]{1,0:T(8,128)(2,1)S(1)}, bf16[64,1024]{1,0:T(8,128)(2,1)S(1)}, u32[]{:S(2)}, u32[]{:S(2)}) collective-permute-start(bf16[64,1024]{1,0:T(8,128)(2,1)S(1)} %copy-done.15), channel_id=1, source_target_pairs={{0,24},{8,16},{16,8},{24,0},{1,25},{9,17},{17,9},{25,1},{2,26},{10... | collective-permute-start | bytes 393224 | tf_op jit(solution)/shard_map/ppermute | solution.py:25
  54.4 8.7 %collective-permute-start.15 = (bf16[64,1024]{1,0:T(8,128)(2,1)}, bf16[64,1024]{1,0:T(8,128)(2,1)S(1)}, u32[]{:S(2)}, u32[]{:S(2)}) collective-permute-start(bf16[64,1024]{1,0:T(8,128)(2,1)} %get-tuple-element.25), channel_id=1, source_target_pairs={{0,2},{2,0},{4,6},{6,4},{1,3},{3,1},{5,7},{7,5},{8,10},{10,8},{12,... | collective-permute-start | bytes 393224 | tf_op jit(solution)/shard_map/ppermute | solution.py:25
  55.9 7.8 %collective-permute-start.16 = (bf16[64,1024]{1,0:T(8,128)(2,1)}, bf16[64,1024]{1,0:T(8,128)(2,1)S(1)}, u32[]{:S(2)}, u32[]{:S(2)}) collective-permute-start(bf16[64,1024]{1,0:T(8,128)(2,1)} %get-tuple-element.26), channel_id=1, source_target_pairs={{0,4},{2,6},{4,0},{6,2},{1,5},{3,7},{5,1},{7,3},{8,12},{10,14},{12... | collective-permute-start | bytes 393224 | tf_op jit(solution)/shard_map/ppermute | solution.py:25
  57.5 3.1 %copy-start.4 = (bf16[64,1024]{1,0:T(8,128)(2,1)}, bf16[64,1024]{1,0:T(8,128)(2,1)S(1)}, u32[]{:S(2)}) copy-start(bf16[64,1024]{1,0:T(8,128)(2,1)S(1)} %collective-permute-done.10.refs_0_) | copy-start | bytes 393220
  57.5 6.3 %collective-permute-start.17 = (bf16[64,1024]{1,0:T(8,128)(2,1)}, bf16[64,1024]{1,0:T(8,128)(2,1)S(1)}, u32[]{:S(2)}, u32[]{:S(2)}) collective-permute-start(bf16[64,1024]{1,0:T(8,128)(2,1)} %get-tuple-element.27), channel_id=1, source_target_pairs={{0,6},{2,4},{4,2},{6,0},{1,7},{3,5},{5,3},{7,1},{8,14},{10,12},{12... | collective-permute-start | bytes 393224 | tf_op jit(solution)/shard_map/ppermute | solution.py:25
  59.8 0.8 %copy-start.5 = (bf16[64,1024]{1,0:T(8,128)(2,1)}, bf16[64,1024]{1,0:T(8,128)(2,1)S(1)}, u32[]{:S(2)}) copy-start(bf16[64,1024]{1,0:T(8,128)(2,1)S(1)} %collective-permute-done.11.refs_1_) | copy-start | bytes 393220
  60.6 0.7 copy-start.7
  63.2 0.7 copy-start.8
  63.8 0.7 copy-start.9
  63.8 0.7 %copy-start.10 = (bf16[64,1024]{1,0:T(8,128)(2,1)}, bf16[64,1024]{1,0:T(8,128)(2,1)S(1)}, u32[]{:S(2)}) copy-start(bf16[64,1024]{1,0:T(8,128)(2,1)S(1)} %collective-permute-done.17.refs_2_) | copy-start | bytes 393220
where the time goes:
time: 67.9 us; the launch traced here: 67.4 us
  starting transfers between devices  25.7 us (38%)
  Pallas kernels  16.1 us (24%)
  local copies, waits for them, and re-layouts  10 us (15%)
  waiting for transfers between devices  9.08 us (13%)
  between operations  3.4 us (5%)
  other arithmetic  3.1 us (5%)
    ppermute x18, starting transfers between devices, send_pieces(): out[k] = lax.ppermute(pieces[k], axes, [(i, i ^ k) for i in range(count)])  24.9 us
    pallas_call x7, Pallas kernels, call(): pl.pallas_call(kernel, out_shape=[jax.ShapeDtypeStruct(shape, dtype) for...  16.1 us
    ppermute x18, waiting for transfers between devices, send_pieces(): out[k] = lax.ppermute(pieces[k], axes, [(i, i ^ k) for i in range(count)])  8.25 us
    unnamed x41, local copies, waits for them, and re-layouts  4.87 us
    reduce_sum x1, other arithmetic, local(): jnp.sum((quarter_ids[:, :, None] == quarter_ids[:, None, :]).astype(F32))  1.84 us
  transfers between devices with their start and end apart: 22, of which 4 were waited for; matrix products, arithmetic and copies ran while one was open for 15% of the time, Pallas kernels for 21%

commit v1 on v0

--- a/solution.py
+++ b/solution.py
@@ -44,14 +44,30 @@
     return lax.dot_general(a, b, (((da,), (db,)), ((), ())), preferred_element_type=F32)
 
 
-def call(kernel, outs, *args):
+def call(kernel, outs, *args, scratch=()):
     vmem = pl.BlockSpec(memory_space=pltpu.VMEM)
+    sizes = [a.size * a.dtype.itemsize for a in args]
+    sizes += [math.prod(shape) * jnp.dtype(dtype).itemsize for shape, dtype in outs]
     return pl.pallas_call(
         kernel,
         out_shape=[jax.ShapeDtypeStruct(shape, dtype) for shape, dtype in outs],
         in_specs=[vmem] * len(args),
         out_specs=[vmem] * len(outs),
+        scratch_shapes=list(scratch),
+        compiler_params=pltpu.CompilerParams(vmem_limit_bytes=min(3 * sum(sizes), 40 << 20) + (6 << 20)),
     )(*args)
+
+
+def spread(line, width):
+    lane = lax.broadcasted_iota(jnp.int32, (8, width), 1)
+    parts = [jnp.broadcast_to(part.astype(F32)[:, :1], (8, width)) for part in split3(line)]
+    value = jnp.where(lane == 0, parts[0], jnp.where(lane == 1, parts[1], jnp.where(lane == 2, parts[2], 0.0)))
+    return value.astype(BF16)
+
+
+def gather3(rows):
+    parts = [rows[:, i : i + 1] for i in range(3)]
+    return jnp.broadcast_to(join3(*parts), (8, 128))
 
 
 def each_chunk(total, body):
@@ -63,6 +79,60 @@
         @pl.loop(0, total // CHUNK)
         def _(i):
             body(pl.multiple_of(i * CHUNK, CHUNK))
+
+
+def halves(row, core, rows):
+    low, high = row[:, :rows], row[:, rows:]
+    return jnp.where(core == 0, low, high), jnp.where(core == 0, high, low)
+
+
+def id_kernel(rows, plane, ids, queries, documents, counts, total, positive, q_own, d_own, found):
+    quarters = ids.shape[0] // plane
+    my_quarter, my_core = lax.axis_index("quarter"), lax.axis_index("core")
+    my_plane = lax.axis_index(PLANE)
+    q_own[...] = queries[...]
+    d_own[...] = documents[...]
+    chips, lanes = ids.shape
+    square = ids[...]
+    if chips < lanes:
+        square = jnp.concatenate([square, jnp.zeros((lanes - chips, lanes), square.dtype)], 0)
+    tall = jnp.transpose(square)
+    for z in range(quarters):
+
+        def count(chip):
+            row = ids[pl.ds(chip, 1), :]
+            same = jnp.zeros((lanes, lanes), F32)
+            for other in range(z * plane, (z + 1) * plane):
+                same += (tall[:, other : other + 1] == row).astype(F32)
+            found[pl.ds(chip, 1), :] = jnp.sum(same, 0, keepdims=True)
+
+        if plane <= DIRECT:
+            for chip in range(z * plane, (z + 1) * plane):
+                count(chip)
+        else:
+            pl.loop(z * plane, (z + 1) * plane)(count)
+    total[...] = jnp.broadcast_to(jnp.sum(jnp.sum(found[...], 0, keepdims=True), 1, keepdims=True), total.shape)
+    for k in range(quarters):
+        row = found[pl.ds((my_quarter ^ k) * plane + my_plane, 1), :]
+        counts[:, k * rows : (k + 1) * rows] = halves(row, my_core, rows)[0]
+    own = halves(ids[pl.ds(my_quarter * plane + my_plane, 1), :], my_core, rows)[0]
+    for k in range(plane):
+        row = ids[pl.ds(my_quarter * plane + (my_plane ^ k), 1), :]
+        column = jnp.transpose(jnp.broadcast_to(row, (8, lanes)))[:, :1]
+        low, high = (column[:rows] == own).astype(F32), (column[rows:] == own).astype(F32)
+        positive[k * rows : (k + 1) * rows, :] = jnp.where(my_core == 0, low, high)
+        positive[(plane + k) * rows : (plane + k + 1) * rows, :] = jnp.where(my_core == 0, high, low)
+
+
+def split3(x):
+    high = x.astype(BF16)
+    rest = x - high.astype(F32)
+    middle = rest.astype(BF16)
+    return high, middle, (rest - middle.astype(F32)).astype(BF16)
+
+
+def join3(high, middle, low):
+    return (high.astype(F32) + middle.astype(F32)) + low.astype(F32)
 
 
 def score_kernel(scale, rows, docs, queries, positive, scores, stats):
@@ -106,6 +176,7 @@
 
 def weight_kernel(batch_rows, rows, scores, s0, s1, s2, s3, counts, total, positive, *outs):
     w_mine, w_send, gains, loss = outs
+    tail = w_mine.shape[0]
     cols = scores.shape[1]
     half = scores.shape[0] // 2
     stats = [s[...] for s in (s0, s1, s2, s3)]
@@ -126,13 +197,13 @@
             own = raw[:, : 2 * rows]
             pad = jnp.concatenate([positive[src, :], jnp.zeros((CHUNK, rows), F32)], 1)
             raw = jnp.concatenate([own - pad, raw[:, 2 * rows :]], 1)
-            out[pl.ds(at, CHUNK), :] = (batch_rows * raw / all_pairs).astype(BF16)
+            out[pl.ds(at, CHUNK), :] = (batch_rows * raw / all_pairs[:1]).astype(BF16)
 
         each_chunk(half, body)
 
     fill(w_send, half)
     fill(w_mine, 0)
-    factor = batch_rows * row_counts[:, :rows] / all_pairs[:, :rows]
+    factor = batch_rows * row_counts[:, :rows] / all_pairs[:1, :rows]
     lanes = [factor * jnp.exp(a[:, :rows] - log_denom[:, :rows]) for a in lses]
     tall = jnp.concatenate(lanes + lanes, 0)
     gains[...] = jnp.transpose(jnp.concatenate([tall, tall], 1))[:rows]
@@ -143,7 +214,9 @@
             for k in range(rest)
         ]
     )
-    loss[...] = jnp.broadcast_to(line, loss.shape)
+    line = jnp.broadcast_to(line, loss.shape)
+    loss[...] = line
+    w_send[tail:, :] = spread(line, w_send.shape[1])
 
 
 def own_kernel(scale, w_mine, w_send, docs, out):
@@ -152,34 +225,28 @@
     total = None
     for base, ref in ((0, w_mine), (half, w_send)):
         for at in range(0, half, CHUNK):
-            w = jnp.transpose(ref[at : at + CHUNK, :].astype(F32))[:rows].astype(BF16)
+            w = jnp.transpose(ref[at : at + CHUNK, :128].astype(F32))[:rows].astype(BF16)
             part = contract(w, docs[base + at : base + at + CHUNK, :], 1, 0)
             total = part if total is None else total + part
     out[...] = total * scale
 
 
-def doc_kernel(scale, rows, w_mine, w_in, q_mine, q_other, own, *outs):
+def doc_kernel(scale, rows, w_mine, w_in, q_mine, q_other, loss, own, chip_loss, *outs):
     half = w_mine.shape[0]
-
-    def body(at):
-        part = contract(w_mine[pl.ds(at, CHUNK), :], q_mine[...], 1, 0)
-        part = (part + contract(w_in[pl.ds(at, CHUNK), :], q_other[...], 1, 0)) * scale
-        if len(outs) == 1 or half != CHUNK:
-            outs[0][pl.ds(at, CHUNK), :] = part.astype(BF16)
-            return part
-        own[...] = part[:rows]
-        for k, out in enumerate(outs, 1):
-            out[...] = part[k * rows : (k + 1) * rows].astype(BF16)
-        return part
-
-    if half == CHUNK:
-        body(0)
-    else:
-        own[...] = body(0)[:rows]
-
-        @pl.loop(1, half // CHUNK)
-        def _(i):
-            body(pl.multiple_of(i * CHUNK, CHUNK))
+    line = loss[...] + gather3(w_in[half:, :])
+    chip_loss[...] = line
+    note = spread(line, own.shape[1])
+    for out in outs:
+        out[rows:, :] = note
+    for at in range(0, half, CHUNK):
+        part = contract(w_mine[at : at + CHUNK, :], q_mine[...], 1, 0)
+        part = (part + contract(w_in[at : at + CHUNK, :], q_other[...], 1, 0)) * scale
+        for k in range(at // rows, (at + CHUNK) // rows):
+            share = part[k * rows - at : (k + 1) * rows - at]
+            if k == 0:
+                own[...] = share
+            else:
+                outs[k - 1][:rows, :] = share.astype(BF16)
 
 
 def query_sum_kernel(own, gains, *refs):
@@ -190,12 +257,15 @@
     out[...] = total.astype(BF16)
 
 
-def doc_sum_kernel(own, *refs):
-    *got, out = refs
+def doc_sum_kernel(own, chip_loss, all_pairs, *refs):
+    *got, out, loss = refs
+    rows = own.shape[0]
     total = own[...]
     for ref in got:
-        total = total + ref[...].astype(F32)
+        total = total + ref[:rows, :].astype(F32)
     out[...] = total.astype(BF16)
+    losses = [chip_loss[...]] + [gather3(ref[rows:, :]) for ref in got]
+    loss[...] = (tree_sum(losses) / all_pairs[:, :128])[:1]
 
 
 def local(queries, documents, user_ids):
@@ -205,40 +275,26 @@
     devices = quarters * plane * 2
     batch_rows = float(devices * rows)
     scale = 3.0 / math.sqrt(width)
-    my_quarter = lax.axis_index("quarter")
-    my_plane = lax.axis_index(PLANE)
-    my_core = lax.axis_index("core")
     cols = quarters * rows
     half = plane * rows
     piece = ((rows, width), BF16)
 
     d_parts = send_pieces([documents] * plane, PLANE)
     q_parts = send_pieces([queries] * quarters, "quarter")
+
+    counts, total, positive, q_own, d_own = call(
+        functools.partial(id_kernel, rows, plane),
+        [((1, cols), F32), ((8, cols), F32), ((2 * half, rows), F32), piece, piece],
+        user_ids.reshape(quarters * plane, 2 * rows),
+        queries,
+        documents,
+        scratch=[pltpu.VMEM((quarters * plane, 2 * rows), F32)],
+    )
+    d_parts[0], q_parts[0] = d_own, q_own
     d_mine = jnp.concatenate(d_parts, 0)
     d_other = swap_cores(d_mine)
     q_mine = jnp.concatenate(q_parts, 0)
     docs = jnp.concatenate([d_mine, d_other], 0)
-
-    table = user_ids.reshape(quarters, plane, 2, rows)
-    quarter_ids = user_ids.reshape(quarters, plane * 2 * rows)
-    total = jnp.sum((quarter_ids[:, :, None] == quarter_ids[:, None, :]).astype(F32))
-    total = jnp.broadcast_to(total, (1, cols))
-    q_order = jnp.bitwise_xor(my_quarter, jnp.arange(quarters))
-    q_ids = lax.dynamic_index_in_dim(
-        lax.dynamic_index_in_dim(table, my_plane, 1, False), my_core, 1, False
-    )
-    row_counts = jnp.sum((q_ids[:, :, None] == quarter_ids[:, None, :]).astype(F32), 2)
-    counts = jnp.take(row_counts, q_order, axis=0).reshape(1, -1)
-    d_order = jnp.bitwise_xor(my_plane, jnp.arange(plane))
-    plane_table = jnp.take(lax.dynamic_index_in_dim(table, my_quarter, 0, False), d_order, axis=0)
-    d_ids = jnp.concatenate(
-        [
-            lax.dynamic_index_in_dim(plane_table, my_core, 1, False).reshape(-1),
-            lax.dynamic_index_in_dim(plane_table, 1 - my_core, 1, False).reshape(-1),
-        ]
-    )
-    own_ids = lax.dynamic_index_in_dim(q_ids, my_quarter, 0, False)
-    positive = (d_ids[:, None] == own_ids[None, :]).astype(F32)
 
     scores, stats = call(
         functools.partial(score_kernel, scale, rows),
@@ -249,14 +305,12 @@
     )
     stats_all = send_pieces([stats] * quarters, "quarter")
     q_other = swap_cores(q_mine)
-    shares = call(
-        functools.partial(share_kernel, scale, rows), [piece] * (quarters - 1), scores, stats, docs
-    )
+    shares = call(functools.partial(share_kernel, scale, rows), [piece] * (quarters - 1), scores, stats, docs)
     q_got = send_pieces([None] + list(shares), "quarter")
 
     w_mine, w_send, gains, line_loss = call(
         functools.partial(weight_kernel, batch_rows, rows),
-        [((half, cols), BF16), ((half, cols), BF16), ((rows, 8), F32), ((8, 128), F32)],
+        [((half, cols), BF16), ((half + 8, cols), BF16), ((rows, 8), F32), ((8, 128), F32)],
         scores,
         *stats_all,
         counts,
@@ -264,27 +318,20 @@
         positive,
     )
     w_in = swap_cores(w_send)
-    chip_loss = line_loss + swap_cores(line_loss)
-    (own_query,) = call(
-        functools.partial(own_kernel, scale), [((rows, width), F32)], w_mine, w_send, docs
-    )
-    spread = plane <= DIRECT
-    own_doc, *d_share = call(
+    (own_query,) = call(functools.partial(own_kernel, scale), [((rows, width), F32)], w_mine, w_send, docs)
+    own_doc, chip_loss, *d_share = call(
         functools.partial(doc_kernel, scale, rows),
-        [((rows, width), F32)] + ([piece] * (plane - 1) if spread else [((half, width), BF16)]),
+        [((rows, width), F32), ((8, 128), F32)] + [((rows + 8, width), BF16)] * (plane - 1),
         w_mine,
         w_in,
         q_mine,
         q_other,
-    )
-    if not spread:
-        d_share = [d_share[0][k * rows : (k + 1) * rows] for k in range(1, plane)]
+        line_loss,
+    )
     d_got = send_pieces([d_share[0]] + list(d_share), PLANE)
-    plane_loss = tree_sum(send_pieces([chip_loss] * plane, PLANE))
-    loss = plane_loss[0, 0] / total[0, 0]
-    (doc_grad,) = call(doc_sum_kernel, [piece], own_doc, *d_got[1:])
+    doc_grad, loss = call(doc_sum_kernel, [piece, ((1, 128), F32)], own_doc, chip_loss, total, *d_got[1:])
     (query_grad,) = call(query_sum_kernel, [piece], own_query, gains, *q_got[1:])
-    return query_grad, doc_grad, loss
+    return query_grad, doc_grad, loss[0, 0]
 
 
 def solution(mesh):

time: 67.9 us -> 48.8 us (0.72)
  Pallas kernels: 16.1 us -> 4.74 us
  waiting for transfers between devices: 9.08 us -> 18.1 us
  local copies, waits for them, and re-layouts: 10 us -> 3.49 us
  starting transfers between devices: 25.7 us -> 21.4 us
  other arithmetic: 3.1 us -> 0.04 us
  between operations: 3.4 us -> 0.81 us
    pallas_call x7 -> x8, Pallas kernels: 16.1 us -> 4.74 us  [call(): pl.pallas_call(kernel, out_shape=[jax.ShapeDtypeStruct(shape, dtype) for...]
    ppermute x18 -> x15, waiting for transfers between devices: 8.25 us -> 17.4 us  [send_pieces(): out[k] = lax.ppermute(pieces[k], axes, [(i, i ^ k) for i in range(count)])]
    ppermute x18 -> x15, starting transfers between devices: 24.9 us -> 21.2 us  [send_pieces(): out[k] = lax.ppermute(pieces[k], axes, [(i, i ^ k) for i in range(count)])]
    reduce_sum x2 -> x0, other arithmetic: 2.03 us -> none  [the longest x1 1.84 us: local(): jnp.sum((quarter_ids[:, :, None] == quarter_ids[:, None, :]).astype(F32))]
    unnamed x41 -> x15, local copies, waits for them, and re-layouts: 4.87 us -> 3.45 us
    broadcast_in_dim x1 -> x0, local copies, waits for them, and re-layouts: 1.17 us -> none  [local(): total = jnp.broadcast_to(total, (1, cols))]
    gather x2 -> x0, local copies, waits for them, and re-layouts: 1.13 us -> none  [the longest x1 0.57 us: local(): jnp.take(lax.dynamic_index_in_dim(table, my_quarter, 0, False), d_order,...]
    reshape x3 -> x0, local copies, waits for them, and re-layouts: 0.94 us -> none  [the longest x1 0.78 us: local(): table = user_ids.reshape(quarters, plane, 2, rows)]
  transfers between devices with their start and end apart: 22 -> 18, of which waited for: 4 -> 6; matrix products, arithmetic and copies ran while one was open for 15% -> 0% of each run, Pallas kernels for 21% -> 8%
where the time goes in v1:
time: 48.8 us; the launch traced here: 48.6 us
  starting transfers between devices  21.4 us (44%)
  waiting for transfers between devices  18.1 us (37%)
  Pallas kernels  4.74 us (10%)
  local copies, waits for them, and re-layouts  3.49 us (7%)
  between operations  0.81 us (2%)
    ppermute x15, starting transfers between devices, send_pieces(): out[k] = lax.ppermute(pieces[k], axes, [(i, i ^ k) for i in range(count)])  21.2 us
    ppermute x15, waiting for transfers between devices, send_pieces(): out[k] = lax.ppermute(pieces[k], axes, [(i, i ^ k) for i in range(count)])  17.4 us
    pallas_call x8, Pallas kernels, call(): pl.pallas_call(kernel, out_shape=[jax.ShapeDtypeStruct(shape, dtype) for...  4.74 us
    unnamed x15, local copies, waits for them, and re-layouts  3.45 us
  transfers between devices with their start and end apart: 18, of which 6 were waited for; matrix products, arithmetic and copies ran while one was open for 0% of the time, Pallas kernels for 8%

profile of v1, /device:TPU:0, one launch (start us, length us, event | category | flops | bytes accessed | tf_op | source)
XLA Modules:
  0.0 48.6 jit_solution(15499004033130152920)
XLA Ops:
  0.6 3.0 %collective-permute-start = (bf16[64,1024]{1,0:T(8,128)(2,1)}, bf16[64,1024]{1,0:T(8,128)(2,1)S(1)}, u32[]{:S(2)}, u32[]{:S(2)}) collective-permute-start(bf16[64,1024]{1,0:T(8,128)(2,1)} %documents.1), channel_id=1, source_target_pairs={{0,2},{2,0},{4,6},{6,4},{1,3},{3,1},{5,7},{7,5},{8,10},{10,8},{12,... | collective-permute-start | bytes 393224 | tf_op jit(solution)/shard_map/ppermute | solution.py:25
  3.7 1.5 %collective-permute-start.1 = (bf16[64,1024]{1,0:T(8,128)(2,1)}, bf16[64,1024]{1,0:T(8,128)(2,1)S(1)}, u32[]{:S(2)}, u32[]{:S(2)}) collective-permute-start(bf16[64,1024]{1,0:T(8,128)(2,1)} %documents.1), channel_id=1, source_target_pairs={{0,4},{2,6},{4,0},{6,2},{1,5},{3,7},{5,1},{7,3},{8,12},{10,14},{12... | collective-permute-start | bytes 393224 | tf_op jit(solution)/shard_map/ppermute | solution.py:25
  5.2 0.0 collective-permute-start.2
  5.2 2.0 %collective-permute-start.4 = (bf16[64,1024]{1,0:T(8,128)(2,1)}, bf16[64,1024]{1,0:T(8,128)(2,1)S(1)}, u32[]{:S(2)}, u32[]{:S(2)}) collective-permute-start(bf16[64,1024]{1,0:T(8,128)(2,1)} %queries.1), channel_id=1, source_target_pairs={{0,8},{8,0},{16,24},{24,16},{1,9},{9,1},{17,25},{25,17},{2,10},{10... | collective-permute-start | bytes 393224 | tf_op jit(solution)/shard_map/ppermute | solution.py:25
  7.2 2.6 %collective-permute-start.5 = (bf16[64,1024]{1,0:T(8,128)(2,1)}, bf16[64,1024]{1,0:T(8,128)(2,1)S(1)}, u32[]{:S(2)}, u32[]{:S(2)}) collective-permute-start(bf16[64,1024]{1,0:T(8,128)(2,1)} %queries.1), channel_id=1, source_target_pairs={{0,16},{8,24},{16,0},{24,8},{1,17},{9,25},{17,1},{25,9},{2,18},{10... | collective-permute-start | bytes 393224 | tf_op jit(solution)/shard_map/ppermute | solution.py:25
  9.8 0.0 copy-start
  9.8 0.9 %copy-done = bf16[64,1024]{1,0:T(8,128)(2,1)S(1)} copy-done((bf16[64,1024]{1,0:T(8,128)(2,1)S(1)}, bf16[64,1024]{1,0:T(8,128)(2,1)}, u32[]{:S(2)}) %copy-start) | copy-done | bytes 131096
  10.7 0.0 copy-start.1
  10.7 0.9 %copy-done.1 = bf16[64,1024]{1,0:T(8,128)(2,1)S(1)} copy-done((bf16[64,1024]{1,0:T(8,128)(2,1)S(1)}, bf16[64,1024]{1,0:T(8,128)(2,1)}, u32[]{:S(2)}) %copy-start.1) | copy-done | bytes 131096
  11.6 0.0 copy-start.3
  11.6 0.7 %copy-done.3 = s32[2048]{0:T(1024)S(1)} copy-done((s32[2048]{0:T(1024)S(1)}, s32[2048]{0:T(1024)}, u32[]{:S(2)}) %copy-start.3) | copy-done | bytes 8216
  12.3 0.9 %shard_map.58 = (f32[1,256]{1,0:T(1,128)S(1)}, f32[8,256]{1,0:T(8,128)S(1)}, f32[512,64]{1,0:T(8,128)S(1)}, bf16[64,1024]{1,0:T(8,128)(2,1)S(1)}, bf16[64,1024]{1,0:T(8,128)(2,1)S(1)}) custom-call(s32[16,128]{1,0:T(8,128)S(1)} %bitcast.3, bf16[64,1024]{1,0:T(8,128)(2,1)S(1)} %copy-done.1, bf16[64,1024]{1,0:T(8,128)(2,1)S(1)} %copy-done), custom_call_target="tpu_custom_call" | custom-call | tf_op jit(solution)/shard_map/pallas_call | solution.py:51
  13.3 0.0 copy-start.2
  13.3 0.0 collective-permute-done
  13.3 0.9 %copy-done.2 = bf16[64,1024]{1,0:T(8,128)(2,1)S(1)} copy-done((bf16[64,1024]{1,0:T(8,128)(2,1)S(1)}, bf16[64,1024]{1,0:T(8,128)(2,1)}, u32[]{:S(2)}) %copy-start.2) | copy-done | bytes 131096
  14.2 0.0 collective-permute-start.6
  14.2 0.0 collective-permute-done.1
  14.2 0.0 collective-permute-done.2
  14.3 0.1 collective-permute-start.3
  14.4 0.0 collective-permute-done.4
  14.4 1.1 %collective-permute-done.5 = bf16[64,1024]{1,0:T(8,128)(2,1)S(1)} collective-permute-done((bf16[64,1024]{1,0:T(8,128)(2,1)}, bf16[64,1024]{1,0:T(8,128)(2,1)S(1)}, u32[]{:S(2)}, u32[]{:S(2)}) %collective-permute-start.5) | collective-permute-done | bytes 131104 | tf_op jit(solution)/shard_map/ppermute | solution.py:25
  15.5 5.6 %collective-permute-done.6 = bf16[64,1024]{1,0:T(8,128)(2,1)S(1)} collective-permute-done((bf16[64,1024]{1,0:T(8,128)(2,1)S(1)}, bf16[64,1024]{1,0:T(8,128)(2,1)S(1)}, u32[]{:S(2)}, u32[]{:S(2)}) %collective-permute-start.6) | collective-permute-done | bytes 131104 | tf_op jit(solution)/shard_map/ppermute | solution.py:25
  21.1 0.1 collective-permute-start.14
  21.2 0.0 collective-permute-done.3
  21.3 0.6 %shard_map.59 = (f32[512,256]{1,0:T(8,128)S(1)}, f32[8,256]{1,0:T(8,128)S(1)}) custom-call(bf16[512,1024]{1,0:T(8,128)(2,1)S(1)} %constant_dynamic-update-slice_fusion.docs, bf16[256,1024]{1,0:T(8,128)(2,1)S(1)} %constant_dynamic-update-slice_fusion.5.queries.q_mine, f32[512,64]{1,0:T(8,128)S(1)} %get-tuple-element.26.positive), custom_call_target="tpu_custom_call" | custom-call | tf_op jit(solution)/shard_map/pallas_call | solution.py:51
  21.9 0.8 %collective-permute-start.7 = (f32[8,256]{1,0:T(8,128)S(1)}, f32[8,256]{1,0:T(8,128)S(1)}, u32[]{:S(2)}, u32[]{:S(2)}) collective-permute-start(f32[8,256]{1,0:T(8,128)S(1)} %get-tuple-element.28.s0.stats), channel_id=1, source_target_pairs={{0,8},{8,0},{16,24},{24,16},{1,9},{9,1},{17,25},{25,17},{2,10},{10... | collective-permute-start | bytes 24584 | tf_op jit(solution)/shard_map/ppermute | solution.py:25
  22.7 1.0 %collective-permute-start.8 = (f32[8,256]{1,0:T(8,128)S(1)}, f32[8,256]{1,0:T(8,128)S(1)}, u32[]{:S(2)}, u32[]{:S(2)}) collective-permute-start(f32[8,256]{1,0:T(8,128)S(1)} %get-tuple-element.28.s0.stats), channel_id=1, source_target_pairs={{0,16},{8,24},{16,0},{24,8},{1,17},{9,25},{17,1},{25,9},{2,18},{10... | collective-permute-start | bytes 24584 | tf_op jit(solution)/shard_map/ppermute | solution.py:25
  23.7 2.7 %collective-permute-start.9 = (f32[8,256]{1,0:T(8,128)S(1)}, f32[8,256]{1,0:T(8,128)S(1)}, u32[]{:S(2)}, u32[]{:S(2)}) collective-permute-start(f32[8,256]{1,0:T(8,128)S(1)} %get-tuple-element.28.s0.stats), channel_id=1, source_target_pairs={{0,24},{8,16},{16,8},{24,0},{1,25},{9,17},{17,9},{25,1},{2,26},{10... | collective-permute-start | bytes 24584 | tf_op jit(solution)/shard_map/ppermute | solution.py:25
  26.3 0.0 collective-permute-done.7.s1
  26.3 1.0 %collective-permute-done.8.s2 = f32[8,256]{1,0:T(8,128)S(1)} collective-permute-done((f32[8,256]{1,0:T(8,128)S(1)}, f32[8,256]{1,0:T(8,128)S(1)}, u32[]{:S(2)}, u32[]{:S(2)}) %collective-permute-start.8) | collective-permute-done | bytes 8224 | tf_op jit(solution)/shard_map/ppermute | solution.py:25
  27.3 1.8 %collective-permute-done.9.s3 = f32[8,256]{1,0:T(8,128)S(1)} collective-permute-done((f32[8,256]{1,0:T(8,128)S(1)}, f32[8,256]{1,0:T(8,128)S(1)}, u32[]{:S(2)}, u32[]{:S(2)}) %collective-permute-start.9) | collective-permute-done | bytes 8224 | tf_op jit(solution)/shard_map/ppermute | solution.py:25
  29.1 0.4 shard_map.60
  29.5 0.1 collective-permute-start.13
  29.6 0.5 shard_map.62
  30.0 0.2 collective-permute-start.10
  30.2 0.0 collective-permute-done.14.q_other
  30.2 0.7 %collective-permute-done.13.w_in = bf16[264,256]{1,0:T(8,128)(2,1)S(1)} collective-permute-done((bf16[264,256]{1,0:T(8,128)(2,1)S(1)}, bf16[264,256]{1,0:T(8,128)(2,1)S(1)}, u32[]{:S(2)}, u32[]{:S(2)}) %collective-permute-start.13) | collective-permute-done | bytes 135200 | tf_op jit(solution)/shard_map/ppermute | solution.py:34
  30.9 0.4 shard_map.64
  31.3 1.5 %collective-permute-start.15 = (bf16[72,1024]{1,0:T(8,128)(2,1)S(1)}, bf16[72,1024]{1,0:T(8,128)(2,1)S(1)}, u32[]{:S(2)}, u32[]{:S(2)}) collective-permute-start(bf16[72,1024]{1,0:T(8,128)(2,1)S(1)} %get-tuple-element.40), channel_id=1, source_target_pairs={{0,2},{2,0},{4,6},{6,4},{1,3},{3,1},{5,7},{7,5},{8,10},{10,8},{12,... | collective-permute-start | bytes 442376 | tf_op jit(solution)/shard_map/ppermute | solution.py:25
  32.9 1.5 %collective-permute-start.16 = (bf16[72,1024]{1,0:T(8,128)(2,1)S(1)}, bf16[72,1024]{1,0:T(8,128)(2,1)S(1)}, u32[]{:S(2)}, u32[]{:S(2)}) collective-permute-start(bf16[72,1024]{1,0:T(8,128)(2,1)S(1)} %get-tuple-element.41), channel_id=1, source_target_pairs={{0,4},{2,6},{4,0},{6,2},{1,5},{3,7},{5,1},{7,3},{8,12},{10,14},{12... | collective-permute-start | bytes 442376 | tf_op jit(solution)/shard_map/ppermute | solution.py:25
  34.4 0.5 %collective-permute-start.17 = (bf16[72,1024]{1,0:T(8,128)(2,1)S(1)}, bf16[72,1024]{1,0:T(8,128)(2,1)S(1)}, u32[]{:S(2)}, u32[]{:S(2)}) collective-permute-start(bf16[72,1024]{1,0:T(8,128)(2,1)S(1)} %get-tuple-element.42), channel_id=1, source_target_pairs={{0,6},{2,4},{4,2},{6,0},{1,7},{3,5},{5,3},{7,1},{8,14},{10,12},{12... | collective-permute-start | bytes 442376 | tf_op jit(solution)/shard_map/ppermute | solution.py:25
  34.9 2.4 %collective-permute-start.11 = (bf16[64,1024]{1,0:T(8,128)(2,1)S(1)}, bf16[64,1024]{1,0:T(8,128)(2,1)S(1)}, u32[]{:S(2)}, u32[]{:S(2)}) collective-permute-start(bf16[64,1024]{1,0:T(8,128)(2,1)S(1)} %get-tuple-element.35), channel_id=1, source_target_pairs={{0,16},{8,24},{16,0},{24,8},{1,17},{9,25},{17,1},{25,9},{2,18},{10... | collective-permute-start | bytes 393224 | tf_op jit(solution)/shard_map/ppermute | solution.py:25
  37.3 0.0 collective-permute-done.10.refs_0_
  37.3 1.3 %collective-permute-start.12 = (bf16[64,1024]{1,0:T(8,128)(2,1)S(1)}, bf16[64,1024]{1,0:T(8,128)(2,1)S(1)}, u32[]{:S(2)}, u32[]{:S(2)}) collective-permute-start(bf16[64,1024]{1,0:T(8,128)(2,1)S(1)} %get-tuple-element.36), channel_id=1, source_target_pairs={{0,24},{8,16},{16,8},{24,0},{1,25},{9,17},{17,9},{25,1},{2,26},{10... | collective-permute-start | bytes 393224 | tf_op jit(solution)/shard_map/ppermute | solution.py:25
  38.6 0.3 shard_map.61.own
  39.0 7.9 %collective-permute-done.11.refs_1_ = bf16[64,1024]{1,0:T(8,128)(2,1)S(1)} collective-permute-done((bf16[64,1024]{1,0:T(8,128)(2,1)S(1)}, bf16[64,1024]{1,0:T(8,128)(2,1)S(1)}, u32[]{:S(2)}, u32[]{:S(2)}) %collective-permute-start.11) | collective-permute-done | bytes 131104 | tf_op jit(solution)/shard_map/ppermute | solution.py:25
  46.9 0.0 collective-permute-done.12.refs_2_
  46.9 0.8 %shard_map.63 = bf16[64,1024]{1,0:T(8,128)(2,1)} custom-call(f32[64,1024]{1,0:T(8,128)S(1)} %shard_map.61.own, f32[64,8]{1,0:T(8,128)S(1)} %get-tuple-element.33.gains, bf16[64,1024]{1,0:T(8,128)(2,1)S(1)} %collective-permute-done.10.refs_0_, bf16[64,1024]{1,0:T(8,128)(2,1)S(1)} %collective-permute-done.11.refs_1_, ...), custom_call_target="tpu_custom_call" | custom-call | tf_op jit(solution)/shard_map/pallas_call | solution.py:51
  47.7 0.0 collective-permute-done.15.refs_0_
  47.7 0.0 collective-permute-done.16.refs_1_
  47.7 0.0 collective-permute-done.17.refs_2_
  47.8 0.8 %shard_map.65 = (bf16[64,1024]{1,0:T(8,128)(2,1)}, f32[1,128]{1,0:T(1,128)}) custom-call(f32[64,1024]{1,0:T(8,128)S(1)} %get-tuple-element.38.own, f32[8,128]{1,0:T(8,128)S(1)} %get-tuple-element.39.chip_loss, f32[8,256]{1,0:T(8,128)S(1)} %get-tuple-element.30.total.all_pairs, bf16[72,1024]{1,0:T(8,128)(2,1)S(1)} %collective-permute-done.15.refs_0_, ...), custom_call_target="tpu_custom_call" | custom-call | tf_op jit(solution)/shard_map/pallas_call | solution.py:51
  (10 shorter events, 0.2 us)
Async XLA Ops:
  0.6 12.7 %collective-permute-start = (bf16[64,1024]{1,0:T(8,128)(2,1)}, bf16[64,1024]{1,0:T(8,128)(2,1)S(1)}, u32[]{:S(2)}, u32[]{:S(2)}) collective-permute-start(bf16[64,1024]{1,0:T(8,128)(2,1)} %documents.1), channel_id=1, source_target_pairs={{0,2},{2,0},{4,6},{6,4},{1,3},{3,1},{5,7},{7,5},{8,10},{10,8},{12,... | collective-permute-start | bytes 393224 | tf_op jit(solution)/shard_map/ppermute | solution.py:25
  3.7 10.6 %collective-permute-start.1 = (bf16[64,1024]{1,0:T(8,128)(2,1)}, bf16[64,1024]{1,0:T(8,128)(2,1)S(1)}, u32[]{:S(2)}, u32[]{:S(2)}) collective-permute-start(bf16[64,1024]{1,0:T(8,128)(2,1)} %documents.1), channel_id=1, source_target_pairs={{0,4},{2,6},{4,0},{6,2},{1,5},{3,7},{5,1},{7,3},{8,12},{10,14},{12... | collective-permute-start | bytes 393224 | tf_op jit(solution)/shard_map/ppermute | solution.py:25
  5.2 9.0 %collective-permute-start.2 = (bf16[64,1024]{1,0:T(8,128)(2,1)}, bf16[64,1024]{1,0:T(8,128)(2,1)S(1)}, u32[]{:S(2)}, u32[]{:S(2)}) collective-permute-start(bf16[64,1024]{1,0:T(8,128)(2,1)} %documents.1), channel_id=1, source_target_pairs={{0,6},{2,4},{4,2},{6,0},{1,7},{3,5},{5,3},{7,1},{8,14},{10,12},{12... | collective-permute-start | bytes 393224 | tf_op jit(solution)/shard_map/ppermute | solution.py:25
  5.2 9.2 %collective-permute-start.4 = (bf16[64,1024]{1,0:T(8,128)(2,1)}, bf16[64,1024]{1,0:T(8,128)(2,1)S(1)}, u32[]{:S(2)}, u32[]{:S(2)}) collective-permute-start(bf16[64,1024]{1,0:T(8,128)(2,1)} %queries.1), channel_id=1, source_target_pairs={{0,8},{8,0},{16,24},{24,16},{1,9},{9,1},{17,25},{25,17},{2,10},{10... | collective-permute-start | bytes 393224 | tf_op jit(solution)/shard_map/ppermute | solution.py:25
  7.2 8.2 %collective-permute-start.5 = (bf16[64,1024]{1,0:T(8,128)(2,1)}, bf16[64,1024]{1,0:T(8,128)(2,1)S(1)}, u32[]{:S(2)}, u32[]{:S(2)}) collective-permute-start(bf16[64,1024]{1,0:T(8,128)(2,1)} %queries.1), channel_id=1, source_target_pairs={{0,16},{8,24},{16,0},{24,8},{1,17},{9,25},{17,1},{25,9},{2,18},{10... | collective-permute-start | bytes 393224 | tf_op jit(solution)/shard_map/ppermute | solution.py:25
  9.8 0.9 %copy-start = (bf16[64,1024]{1,0:T(8,128)(2,1)S(1)}, bf16[64,1024]{1,0:T(8,128)(2,1)}, u32[]{:S(2)}) copy-start(bf16[64,1024]{1,0:T(8,128)(2,1)} %documents.1) | copy-start | bytes 393220
  10.7 0.9 %copy-start.1 = (bf16[64,1024]{1,0:T(8,128)(2,1)S(1)}, bf16[64,1024]{1,0:T(8,128)(2,1)}, u32[]{:S(2)}) copy-start(bf16[64,1024]{1,0:T(8,128)(2,1)} %queries.1) | copy-start | bytes 393220
  11.6 0.7 %copy-start.3 = (s32[2048]{0:T(1024)S(1)}, s32[2048]{0:T(1024)}, u32[]{:S(2)}) copy-start(s32[2048]{0:T(1024)} %param.5) | copy-start | bytes 24580
  13.3 0.9 %copy-start.2 = (bf16[64,1024]{1,0:T(8,128)(2,1)S(1)}, bf16[64,1024]{1,0:T(8,128)(2,1)}, u32[]{:S(2)}) copy-start(bf16[64,1024]{1,0:T(8,128)(2,1)} %queries.1) | copy-start | bytes 393220
  14.2 6.9 %collective-permute-start.6 = (bf16[64,1024]{1,0:T(8,128)(2,1)S(1)}, bf16[64,1024]{1,0:T(8,128)(2,1)S(1)}, u32[]{:S(2)}, u32[]{:S(2)}) collective-permute-start(bf16[64,1024]{1,0:T(8,128)(2,1)S(1)} %copy-done.2), channel_id=1, source_target_pairs={{0,24},{8,16},{16,8},{24,0},{1,25},{9,17},{17,9},{25,1},{2,26},{10... | collective-permute-start | bytes 393224 | tf_op jit(solution)/shard_map/ppermute | solution.py:25
  14.3 7.0 %collective-permute-start.3 = (bf16[256,1024]{1,0:T(8,128)(2,1)S(1)}, bf16[256,1024]{1,0:T(8,128)(2,1)S(1)}, u32[]{:S(2)}, u32[]{:S(2)}) collective-permute-start(bf16[256,1024]{1,0:T(8,128)(2,1)S(1)} %pad_maximum_fusion), channel_id=1, source_target_pairs={{0,1},{1,0},{2,3},{3,2},{4,5},{5,4},{6,7},{7,6},{8,9},{9,8},{10,11... | collective-permute-start | bytes 1572872 | tf_op jit(solution)/shard_map/ppermute | solution.py:34
  21.1 9.1 %collective-permute-start.14 = (bf16[256,1024]{1,0:T(8,128)(2,1)S(1)}, bf16[256,1024]{1,0:T(8,128)(2,1)S(1)}, u32[]{:S(2)}, u32[]{:S(2)}) collective-permute-start(bf16[256,1024]{1,0:T(8,128)(2,1)S(1)} %constant_dynamic-update-slice_fusion.5.queries.q_mine), channel_id=1, source_target_pairs={{0,1},{1,0},{2,3},{3,2},{4,5},{5,4},{6,7},{7,6},{8,9},{9,8},{10,11... | collective-permute-start | bytes 1572872 | tf_op jit(solution)/shard_map/ppermute | solution.py:34
  21.9 4.5 %collective-permute-start.7 = (f32[8,256]{1,0:T(8,128)S(1)}, f32[8,256]{1,0:T(8,128)S(1)}, u32[]{:S(2)}, u32[]{:S(2)}) collective-permute-start(f32[8,256]{1,0:T(8,128)S(1)} %get-tuple-element.28.s0.stats), channel_id=1, source_target_pairs={{0,8},{8,0},{16,24},{24,16},{1,9},{9,1},{17,25},{25,17},{2,10},{10... | collective-permute-start | bytes 24584 | tf_op jit(solution)/shard_map/ppermute | solution.py:25
  22.7 4.6 %collective-permute-start.8 = (f32[8,256]{1,0:T(8,128)S(1)}, f32[8,256]{1,0:T(8,128)S(1)}, u32[]{:S(2)}, u32[]{:S(2)}) collective-permute-start(f32[8,256]{1,0:T(8,128)S(1)} %get-tuple-element.28.s0.stats), channel_id=1, source_target_pairs={{0,16},{8,24},{16,0},{24,8},{1,17},{9,25},{17,1},{25,9},{2,18},{10... | collective-permute-start | bytes 24584 | tf_op jit(solution)/shard_map/ppermute | solution.py:25
  23.7 5.4 %collective-permute-start.9 = (f32[8,256]{1,0:T(8,128)S(1)}, f32[8,256]{1,0:T(8,128)S(1)}, u32[]{:S(2)}, u32[]{:S(2)}) collective-permute-start(f32[8,256]{1,0:T(8,128)S(1)} %get-tuple-element.28.s0.stats), channel_id=1, source_target_pairs={{0,24},{8,16},{16,8},{24,0},{1,25},{9,17},{17,9},{25,1},{2,26},{10... | collective-permute-start | bytes 24584 | tf_op jit(solution)/shard_map/ppermute | solution.py:25
  29.5 1.4 %collective-permute-start.13 = (bf16[264,256]{1,0:T(8,128)(2,1)S(1)}, bf16[264,256]{1,0:T(8,128)(2,1)S(1)}, u32[]{:S(2)}, u32[]{:S(2)}) collective-permute-start(bf16[264,256]{1,0:T(8,128)(2,1)S(1)} %get-tuple-element.32.w_send), channel_id=1, source_target_pairs={{0,1},{1,0},{2,3},{3,2},{4,5},{5,4},{6,7},{7,6},{8,9},{9,8},{10,11... | collective-permute-start | bytes 405512 | tf_op jit(solution)/shard_map/ppermute | solution.py:34
  30.0 7.3 %collective-permute-start.10 = (bf16[64,1024]{1,0:T(8,128)(2,1)S(1)}, bf16[64,1024]{1,0:T(8,128)(2,1)S(1)}, u32[]{:S(2)}, u32[]{:S(2)}) collective-permute-start(bf16[64,1024]{1,0:T(8,128)(2,1)S(1)} %get-tuple-element.34), channel_id=1, source_target_pairs={{0,8},{8,0},{16,24},{24,16},{1,9},{9,1},{17,25},{25,17},{2,10},{10... | collective-permute-start | bytes 393224 | tf_op jit(solution)/shard_map/ppermute | solution.py:25
  31.3 16.4 %collective-permute-start.15 = (bf16[72,1024]{1,0:T(8,128)(2,1)S(1)}, bf16[72,1024]{1,0:T(8,128)(2,1)S(1)}, u32[]{:S(2)}, u32[]{:S(2)}) collective-permute-start(bf16[72,1024]{1,0:T(8,128)(2,1)S(1)} %get-tuple-element.40), channel_id=1, source_target_pairs={{0,2},{2,0},{4,6},{6,4},{1,3},{3,1},{5,7},{7,5},{8,10},{10,8},{12,... | collective-permute-start | bytes 442376 | tf_op jit(solution)/shard_map/ppermute | solution.py:25
  32.9 14.9 %collective-permute-start.16 = (bf16[72,1024]{1,0:T(8,128)(2,1)S(1)}, bf16[72,1024]{1,0:T(8,128)(2,1)S(1)}, u32[]{:S(2)}, u32[]{:S(2)}) collective-permute-start(bf16[72,1024]{1,0:T(8,128)(2,1)S(1)} %get-tuple-element.41), channel_id=1, source_target_pairs={{0,4},{2,6},{4,0},{6,2},{1,5},{3,7},{5,1},{7,3},{8,12},{10,14},{12... | collective-permute-start | bytes 442376 | tf_op jit(solution)/shard_map/ppermute | solution.py:25
  34.4 13.4 %collective-permute-start.17 = (bf16[72,1024]{1,0:T(8,128)(2,1)S(1)}, bf16[72,1024]{1,0:T(8,128)(2,1)S(1)}, u32[]{:S(2)}, u32[]{:S(2)}) collective-permute-start(bf16[72,1024]{1,0:T(8,128)(2,1)S(1)} %get-tuple-element.42), channel_id=1, source_target_pairs={{0,6},{2,4},{4,2},{6,0},{1,7},{3,5},{5,3},{7,1},{8,14},{10,12},{12... | collective-permute-start | bytes 442376 | tf_op jit(solution)/shard_map/ppermute | solution.py:25
  34.9 12.0 %collective-permute-start.11 = (bf16[64,1024]{1,0:T(8,128)(2,1)S(1)}, bf16[64,1024]{1,0:T(8,128)(2,1)S(1)}, u32[]{:S(2)}, u32[]{:S(2)}) collective-permute-start(bf16[64,1024]{1,0:T(8,128)(2,1)S(1)} %get-tuple-element.35), channel_id=1, source_target_pairs={{0,16},{8,24},{16,0},{24,8},{1,17},{9,25},{17,1},{25,9},{2,18},{10... | collective-permute-start | bytes 393224 | tf_op jit(solution)/shard_map/ppermute | solution.py:25
  37.3 9.6 %collective-permute-start.12 = (bf16[64,1024]{1,0:T(8,128)(2,1)S(1)}, bf16[64,1024]{1,0:T(8,128)(2,1)S(1)}, u32[]{:S(2)}, u32[]{:S(2)}) collective-permute-start(bf16[64,1024]{1,0:T(8,128)(2,1)S(1)} %get-tuple-element.36), channel_id=1, source_target_pairs={{0,24},{8,16},{16,8},{24,0},{1,25},{9,17},{17,9},{25,1},{2,26},{10... | collective-permute-start | bytes 393224 | tf_op jit(solution)/shard_map/ppermute | solution.py:25

commit v2 on v1

--- a/solution.py
+++ b/solution.py
@@ -14,6 +14,7 @@
 PLANE = ("lane", "chip")
 DIRECT = 8
 CHUNK = 256
+LANES = 128
 F32, BF16 = jnp.float32, jnp.bfloat16
 
 
@@ -235,9 +236,10 @@
     half = w_mine.shape[0]
     line = loss[...] + gather3(w_in[half:, :])
     chip_loss[...] = line
-    note = spread(line, own.shape[1])
+    tiles = own.shape[1] // LANES
+    note = spread(line, LANES)
     for out in outs:
-        out[rows:, :] = note
+        out[tiles * rows :, :] = note
     for at in range(0, half, CHUNK):
         part = contract(w_mine[at : at + CHUNK, :], q_mine[...], 1, 0)
         part = (part + contract(w_in[at : at + CHUNK, :], q_other[...], 1, 0)) * scale
@@ -246,7 +248,8 @@
             if k == 0:
                 own[...] = share
             else:
-                outs[k - 1][:rows, :] = share.astype(BF16)
+                for t in range(tiles):
+                    outs[k - 1][t * rows : (t + 1) * rows, :] = share[:, t * LANES : (t + 1) * LANES].astype(BF16)
 
 
 def query_sum_kernel(own, gains, *refs):
@@ -260,11 +263,13 @@
 def doc_sum_kernel(own, chip_loss, all_pairs, *refs):
     *got, out, loss = refs
     rows = own.shape[0]
-    total = own[...]
-    for ref in got:
-        total = total + ref[:rows, :].astype(F32)
-    out[...] = total.astype(BF16)
-    losses = [chip_loss[...]] + [gather3(ref[rows:, :]) for ref in got]
+    tiles = own.shape[1] // LANES
+    for t in range(tiles):
+        total = own[:, t * LANES : (t + 1) * LANES]
+        for ref in got:
+            total = total + ref[t * rows : (t + 1) * rows, :].astype(F32)
+        out[:, t * LANES : (t + 1) * LANES] = total.astype(BF16)
+    losses = [chip_loss[...]] + [gather3(ref[tiles * rows :, :]) for ref in got]
     loss[...] = (tree_sum(losses) / all_pairs[:, :128])[:1]
 
 
@@ -321,7 +326,7 @@
     (own_query,) = call(functools.partial(own_kernel, scale), [((rows, width), F32)], w_mine, w_send, docs)
     own_doc, chip_loss, *d_share = call(
         functools.partial(doc_kernel, scale, rows),
-        [((rows, width), F32), ((8, 128), F32)] + [((rows + 8, width), BF16)] * (plane - 1),
+        [((rows, width), F32), ((8, 128), F32)] + [((rows * width // LANES + 8, LANES), BF16)] * (plane - 1),
         w_mine,
         w_in,
         q_mine,

time: 48.8 us -> 48.8 us (level)
  no operation moved by 1% of the time
where the time goes in v2:
time: 48.8 us; the launch traced here: 48.5 us
  starting transfers between devices  21.4 us (44%)
  waiting for transfers between devices  18.1 us (37%)
  Pallas kernels  4.73 us (10%)
  local copies, waits for them, and re-layouts  3.49 us (7%)
  between operations  0.81 us (2%)
    ppermute x15, starting transfers between devices, send_pieces(): out[k] = lax.ppermute(pieces[k], axes, [(i, i ^ k) for i in range(count)])  21.2 us
    ppermute x15, waiting for transfers between devices, send_pieces(): out[k] = lax.ppermute(pieces[k], axes, [(i, i ^ k) for i in range(count)])  17.4 us
    pallas_call x8, Pallas kernels, call(): pl.pallas_call(kernel, out_shape=[jax.ShapeDtypeStruct(shape, dtype) for...  4.73 us
    unnamed x15, local copies, waits for them, and re-layouts  3.45 us
  transfers between devices with their start and end apart: 18, of which 6 were waited for; matrix products, arithmetic and copies ran while one was open for 0% of the time, Pallas kernels for 8%

profile of v2, /device:TPU:0, one launch (start us, length us, event | category | flops | bytes accessed | tf_op | source)
XLA Modules:
  0.0 48.5 jit_solution(4037404495352141446)
XLA Ops:
  0.6 3.0 %collective-permute-start = (bf16[64,1024]{1,0:T(8,128)(2,1)}, bf16[64,1024]{1,0:T(8,128)(2,1)S(1)}, u32[]{:S(2)}, u32[]{:S(2)}) collective-permute-start(bf16[64,1024]{1,0:T(8,128)(2,1)} %documents.1), channel_id=1, source_target_pairs={{0,2},{2,0},{4,6},{6,4},{1,3},{3,1},{5,7},{7,5},{8,10},{10,8},{12,... | collective-permute-start | bytes 393224 | tf_op jit(solution)/shard_map/ppermute | solution.py:26
  3.7 1.5 %collective-permute-start.1 = (bf16[64,1024]{1,0:T(8,128)(2,1)}, bf16[64,1024]{1,0:T(8,128)(2,1)S(1)}, u32[]{:S(2)}, u32[]{:S(2)}) collective-permute-start(bf16[64,1024]{1,0:T(8,128)(2,1)} %documents.1), channel_id=1, source_target_pairs={{0,4},{2,6},{4,0},{6,2},{1,5},{3,7},{5,1},{7,3},{8,12},{10,14},{12... | collective-permute-start | bytes 393224 | tf_op jit(solution)/shard_map/ppermute | solution.py:26
  5.2 0.0 collective-permute-start.2
  5.2 2.0 %collective-permute-start.4 = (bf16[64,1024]{1,0:T(8,128)(2,1)}, bf16[64,1024]{1,0:T(8,128)(2,1)S(1)}, u32[]{:S(2)}, u32[]{:S(2)}) collective-permute-start(bf16[64,1024]{1,0:T(8,128)(2,1)} %queries.1), channel_id=1, source_target_pairs={{0,8},{8,0},{16,24},{24,16},{1,9},{9,1},{17,25},{25,17},{2,10},{10... | collective-permute-start | bytes 393224 | tf_op jit(solution)/shard_map/ppermute | solution.py:26
  7.2 2.6 %collective-permute-start.5 = (bf16[64,1024]{1,0:T(8,128)(2,1)}, bf16[64,1024]{1,0:T(8,128)(2,1)S(1)}, u32[]{:S(2)}, u32[]{:S(2)}) collective-permute-start(bf16[64,1024]{1,0:T(8,128)(2,1)} %queries.1), channel_id=1, source_target_pairs={{0,16},{8,24},{16,0},{24,8},{1,17},{9,25},{17,1},{25,9},{2,18},{10... | collective-permute-start | bytes 393224 | tf_op jit(solution)/shard_map/ppermute | solution.py:26
  9.8 0.0 copy-start
  9.8 0.9 %copy-done = bf16[64,1024]{1,0:T(8,128)(2,1)S(1)} copy-done((bf16[64,1024]{1,0:T(8,128)(2,1)S(1)}, bf16[64,1024]{1,0:T(8,128)(2,1)}, u32[]{:S(2)}) %copy-start) | copy-done | bytes 131096
  10.7 0.0 copy-start.1
  10.7 0.9 %copy-done.1 = bf16[64,1024]{1,0:T(8,128)(2,1)S(1)} copy-done((bf16[64,1024]{1,0:T(8,128)(2,1)S(1)}, bf16[64,1024]{1,0:T(8,128)(2,1)}, u32[]{:S(2)}) %copy-start.1) | copy-done | bytes 131096
  11.6 0.0 copy-start.3
  11.6 0.7 %copy-done.3 = s32[2048]{0:T(1024)S(1)} copy-done((s32[2048]{0:T(1024)S(1)}, s32[2048]{0:T(1024)}, u32[]{:S(2)}) %copy-start.3) | copy-done | bytes 8216
  12.3 0.9 %shard_map.58 = (f32[1,256]{1,0:T(1,128)S(1)}, f32[8,256]{1,0:T(8,128)S(1)}, f32[512,64]{1,0:T(8,128)S(1)}, bf16[64,1024]{1,0:T(8,128)(2,1)S(1)}, bf16[64,1024]{1,0:T(8,128)(2,1)S(1)}) custom-call(s32[16,128]{1,0:T(8,128)S(1)} %bitcast.3, bf16[64,1024]{1,0:T(8,128)(2,1)S(1)} %copy-done.1, bf16[64,1024]{1,0:T(8,128)(2,1)S(1)} %copy-done), custom_call_target="tpu_custom_call" | custom-call | tf_op jit(solution)/shard_map/pallas_call | solution.py:52
  13.3 0.0 copy-start.2
  13.3 0.0 collective-permute-done
  13.3 0.9 %copy-done.2 = bf16[64,1024]{1,0:T(8,128)(2,1)S(1)} copy-done((bf16[64,1024]{1,0:T(8,128)(2,1)S(1)}, bf16[64,1024]{1,0:T(8,128)(2,1)}, u32[]{:S(2)}) %copy-start.2) | copy-done | bytes 131096
  14.2 0.0 collective-permute-start.6
  14.2 0.0 collective-permute-done.1
  14.2 0.0 collective-permute-done.2
  14.3 0.1 collective-permute-start.3
  14.4 0.0 collective-permute-done.4
  14.4 1.1 %collective-permute-done.5 = bf16[64,1024]{1,0:T(8,128)(2,1)S(1)} collective-permute-done((bf16[64,1024]{1,0:T(8,128)(2,1)}, bf16[64,1024]{1,0:T(8,128)(2,1)S(1)}, u32[]{:S(2)}, u32[]{:S(2)}) %collective-permute-start.5) | collective-permute-done | bytes 131104 | tf_op jit(solution)/shard_map/ppermute | solution.py:26
  15.5 5.6 %collective-permute-done.6 = bf16[64,1024]{1,0:T(8,128)(2,1)S(1)} collective-permute-done((bf16[64,1024]{1,0:T(8,128)(2,1)S(1)}, bf16[64,1024]{1,0:T(8,128)(2,1)S(1)}, u32[]{:S(2)}, u32[]{:S(2)}) %collective-permute-start.6) | collective-permute-done | bytes 131104 | tf_op jit(solution)/shard_map/ppermute | solution.py:26
  21.1 0.1 collective-permute-start.14
  21.2 0.0 collective-permute-done.3
  21.3 0.6 %shard_map.59 = (f32[512,256]{1,0:T(8,128)S(1)}, f32[8,256]{1,0:T(8,128)S(1)}) custom-call(bf16[512,1024]{1,0:T(8,128)(2,1)S(1)} %constant_dynamic-update-slice_fusion.docs, bf16[256,1024]{1,0:T(8,128)(2,1)S(1)} %constant_dynamic-update-slice_fusion.5.queries.q_mine, f32[512,64]{1,0:T(8,128)S(1)} %get-tuple-element.26.positive), custom_call_target="tpu_custom_call" | custom-call | tf_op jit(solution)/shard_map/pallas_call | solution.py:52
  21.9 0.8 %collective-permute-start.7 = (f32[8,256]{1,0:T(8,128)S(1)}, f32[8,256]{1,0:T(8,128)S(1)}, u32[]{:S(2)}, u32[]{:S(2)}) collective-permute-start(f32[8,256]{1,0:T(8,128)S(1)} %get-tuple-element.28.s0.stats), channel_id=1, source_target_pairs={{0,8},{8,0},{16,24},{24,16},{1,9},{9,1},{17,25},{25,17},{2,10},{10... | collective-permute-start | bytes 24584 | tf_op jit(solution)/shard_map/ppermute | solution.py:26
  22.7 1.0 %collective-permute-start.8 = (f32[8,256]{1,0:T(8,128)S(1)}, f32[8,256]{1,0:T(8,128)S(1)}, u32[]{:S(2)}, u32[]{:S(2)}) collective-permute-start(f32[8,256]{1,0:T(8,128)S(1)} %get-tuple-element.28.s0.stats), channel_id=1, source_target_pairs={{0,16},{8,24},{16,0},{24,8},{1,17},{9,25},{17,1},{25,9},{2,18},{10... | collective-permute-start | bytes 24584 | tf_op jit(solution)/shard_map/ppermute | solution.py:26
  23.7 2.7 %collective-permute-start.9 = (f32[8,256]{1,0:T(8,128)S(1)}, f32[8,256]{1,0:T(8,128)S(1)}, u32[]{:S(2)}, u32[]{:S(2)}) collective-permute-start(f32[8,256]{1,0:T(8,128)S(1)} %get-tuple-element.28.s0.stats), channel_id=1, source_target_pairs={{0,24},{8,16},{16,8},{24,0},{1,25},{9,17},{17,9},{25,1},{2,26},{10... | collective-permute-start | bytes 24584 | tf_op jit(solution)/shard_map/ppermute | solution.py:26
  26.3 0.0 collective-permute-done.7.s1
  26.3 1.0 %collective-permute-done.8.s2 = f32[8,256]{1,0:T(8,128)S(1)} collective-permute-done((f32[8,256]{1,0:T(8,128)S(1)}, f32[8,256]{1,0:T(8,128)S(1)}, u32[]{:S(2)}, u32[]{:S(2)}) %collective-permute-start.8) | collective-permute-done | bytes 8224 | tf_op jit(solution)/shard_map/ppermute | solution.py:26
  27.3 1.8 %collective-permute-done.9.s3 = f32[8,256]{1,0:T(8,128)S(1)} collective-permute-done((f32[8,256]{1,0:T(8,128)S(1)}, f32[8,256]{1,0:T(8,128)S(1)}, u32[]{:S(2)}, u32[]{:S(2)}) %collective-permute-start.9) | collective-permute-done | bytes 8224 | tf_op jit(solution)/shard_map/ppermute | solution.py:26
  29.1 0.4 shard_map.60
  29.5 0.1 collective-permute-start.13
  29.6 0.4 shard_map.62
  30.0 0.2 collective-permute-start.10
  30.2 0.0 collective-permute-done.14.q_other
  30.2 0.7 %collective-permute-done.13.w_in = bf16[264,256]{1,0:T(8,128)(2,1)S(1)} collective-permute-done((bf16[264,256]{1,0:T(8,128)(2,1)S(1)}, bf16[264,256]{1,0:T(8,128)(2,1)S(1)}, u32[]{:S(2)}, u32[]{:S(2)}) %collective-permute-start.13) | collective-permute-done | bytes 135200 | tf_op jit(solution)/shard_map/ppermute | solution.py:35
  30.9 0.4 shard_map.64
  31.3 1.5 %collective-permute-start.15 = (bf16[520,128]{1,0:T(8,128)(2,1)S(1)}, bf16[520,128]{1,0:T(8,128)(2,1)S(1)}, u32[]{:S(2)}, u32[]{:S(2)}) collective-permute-start(bf16[520,128]{1,0:T(8,128)(2,1)S(1)} %get-tuple-element.40), channel_id=1, source_target_pairs={{0,2},{2,0},{4,6},{6,4},{1,3},{3,1},{5,7},{7,5},{8,10},{10,8},{12,... | collective-permute-start | bytes 399368 | tf_op jit(solution)/shard_map/ppermute | solution.py:26
  32.9 1.5 %collective-permute-start.16 = (bf16[520,128]{1,0:T(8,128)(2,1)S(1)}, bf16[520,128]{1,0:T(8,128)(2,1)S(1)}, u32[]{:S(2)}, u32[]{:S(2)}) collective-permute-start(bf16[520,128]{1,0:T(8,128)(2,1)S(1)} %get-tuple-element.41), channel_id=1, source_target_pairs={{0,4},{2,6},{4,0},{6,2},{1,5},{3,7},{5,1},{7,3},{8,12},{10,14},{12... | collective-permute-start | bytes 399368 | tf_op jit(solution)/shard_map/ppermute | solution.py:26
  34.4 0.5 %collective-permute-start.17 = (bf16[520,128]{1,0:T(8,128)(2,1)S(1)}, bf16[520,128]{1,0:T(8,128)(2,1)S(1)}, u32[]{:S(2)}, u32[]{:S(2)}) collective-permute-start(bf16[520,128]{1,0:T(8,128)(2,1)S(1)} %get-tuple-element.42), channel_id=1, source_target_pairs={{0,6},{2,4},{4,2},{6,0},{1,7},{3,5},{5,3},{7,1},{8,14},{10,12},{12... | collective-permute-start | bytes 399368 | tf_op jit(solution)/shard_map/ppermute | solution.py:26
  34.9 2.4 %collective-permute-start.11 = (bf16[64,1024]{1,0:T(8,128)(2,1)S(1)}, bf16[64,1024]{1,0:T(8,128)(2,1)S(1)}, u32[]{:S(2)}, u32[]{:S(2)}) collective-permute-start(bf16[64,1024]{1,0:T(8,128)(2,1)S(1)} %get-tuple-element.35), channel_id=1, source_target_pairs={{0,16},{8,24},{16,0},{24,8},{1,17},{9,25},{17,1},{25,9},{2,18},{10... | collective-permute-start | bytes 393224 | tf_op jit(solution)/shard_map/ppermute | solution.py:26
  37.3 0.0 collective-permute-done.10.refs_0_
  37.3 1.3 %collective-permute-start.12 = (bf16[64,1024]{1,0:T(8,128)(2,1)S(1)}, bf16[64,1024]{1,0:T(8,128)(2,1)S(1)}, u32[]{:S(2)}, u32[]{:S(2)}) collective-permute-start(bf16[64,1024]{1,0:T(8,128)(2,1)S(1)} %get-tuple-element.36), channel_id=1, source_target_pairs={{0,24},{8,16},{16,8},{24,0},{1,25},{9,17},{17,9},{25,1},{2,26},{10... | collective-permute-start | bytes 393224 | tf_op jit(solution)/shard_map/ppermute | solution.py:26
  38.6 0.3 shard_map.61.own
  39.0 7.9 %collective-permute-done.11.refs_1_ = bf16[64,1024]{1,0:T(8,128)(2,1)S(1)} collective-permute-done((bf16[64,1024]{1,0:T(8,128)(2,1)S(1)}, bf16[64,1024]{1,0:T(8,128)(2,1)S(1)}, u32[]{:S(2)}, u32[]{:S(2)}) %collective-permute-start.11) | collective-permute-done | bytes 131104 | tf_op jit(solution)/shard_map/ppermute | solution.py:26
  46.9 0.0 collective-permute-done.12.refs_2_
  46.9 0.8 %shard_map.63 = bf16[64,1024]{1,0:T(8,128)(2,1)} custom-call(f32[64,1024]{1,0:T(8,128)S(1)} %shard_map.61.own, f32[64,8]{1,0:T(8,128)S(1)} %get-tuple-element.33.gains, bf16[64,1024]{1,0:T(8,128)(2,1)S(1)} %collective-permute-done.10.refs_0_, bf16[64,1024]{1,0:T(8,128)(2,1)S(1)} %collective-permute-done.11.refs_1_, ...), custom_call_target="tpu_custom_call" | custom-call | tf_op jit(solution)/shard_map/pallas_call | solution.py:52
  47.7 0.0 collective-permute-done.15.refs_0_
  47.7 0.0 collective-permute-done.16.refs_1_
  47.8 0.0 collective-permute-done.17.refs_2_
  47.8 0.8 %shard_map.65 = (bf16[64,1024]{1,0:T(8,128)(2,1)}, f32[1,128]{1,0:T(1,128)}) custom-call(f32[64,1024]{1,0:T(8,128)S(1)} %get-tuple-element.38.own, f32[8,128]{1,0:T(8,128)S(1)} %get-tuple-element.39.chip_loss, f32[8,256]{1,0:T(8,128)S(1)} %get-tuple-element.30.total.all_pairs, bf16[520,128]{1,0:T(8,128)(2,1)S(1)} %collective-permute-done.15.refs_0_, ...), custom_call_target="tpu_custom_call" | custom-call | tf_op jit(solution)/shard_map/pallas_call | solution.py:52
  (10 shorter events, 0.2 us)
Async XLA Ops:
  0.6 12.7 %collective-permute-start = (bf16[64,1024]{1,0:T(8,128)(2,1)}, bf16[64,1024]{1,0:T(8,128)(2,1)S(1)}, u32[]{:S(2)}, u32[]{:S(2)}) collective-permute-start(bf16[64,1024]{1,0:T(8,128)(2,1)} %documents.1), channel_id=1, source_target_pairs={{0,2},{2,0},{4,6},{6,4},{1,3},{3,1},{5,7},{7,5},{8,10},{10,8},{12,... | collective-permute-start | bytes 393224 | tf_op jit(solution)/shard_map/ppermute | solution.py:26
  3.7 10.6 %collective-permute-start.1 = (bf16[64,1024]{1,0:T(8,128)(2,1)}, bf16[64,1024]{1,0:T(8,128)(2,1)S(1)}, u32[]{:S(2)}, u32[]{:S(2)}) collective-permute-start(bf16[64,1024]{1,0:T(8,128)(2,1)} %documents.1), channel_id=1, source_target_pairs={{0,4},{2,6},{4,0},{6,2},{1,5},{3,7},{5,1},{7,3},{8,12},{10,14},{12... | collective-permute-start | bytes 393224 | tf_op jit(solution)/shard_map/ppermute | solution.py:26
  5.2 9.0 %collective-permute-start.2 = (bf16[64,1024]{1,0:T(8,128)(2,1)}, bf16[64,1024]{1,0:T(8,128)(2,1)S(1)}, u32[]{:S(2)}, u32[]{:S(2)}) collective-permute-start(bf16[64,1024]{1,0:T(8,128)(2,1)} %documents.1), channel_id=1, source_target_pairs={{0,6},{2,4},{4,2},{6,0},{1,7},{3,5},{5,3},{7,1},{8,14},{10,12},{12... | collective-permute-start | bytes 393224 | tf_op jit(solution)/shard_map/ppermute | solution.py:26
  5.2 9.2 %collective-permute-start.4 = (bf16[64,1024]{1,0:T(8,128)(2,1)}, bf16[64,1024]{1,0:T(8,128)(2,1)S(1)}, u32[]{:S(2)}, u32[]{:S(2)}) collective-permute-start(bf16[64,1024]{1,0:T(8,128)(2,1)} %queries.1), channel_id=1, source_target_pairs={{0,8},{8,0},{16,24},{24,16},{1,9},{9,1},{17,25},{25,17},{2,10},{10... | collective-permute-start | bytes 393224 | tf_op jit(solution)/shard_map/ppermute | solution.py:26
  7.2 8.2 %collective-permute-start.5 = (bf16[64,1024]{1,0:T(8,128)(2,1)}, bf16[64,1024]{1,0:T(8,128)(2,1)S(1)}, u32[]{:S(2)}, u32[]{:S(2)}) collective-permute-start(bf16[64,1024]{1,0:T(8,128)(2,1)} %queries.1), channel_id=1, source_target_pairs={{0,16},{8,24},{16,0},{24,8},{1,17},{9,25},{17,1},{25,9},{2,18},{10... | collective-permute-start | bytes 393224 | tf_op jit(solution)/shard_map/ppermute | solution.py:26
  9.8 0.9 %copy-start = (bf16[64,1024]{1,0:T(8,128)(2,1)S(1)}, bf16[64,1024]{1,0:T(8,128)(2,1)}, u32[]{:S(2)}) copy-start(bf16[64,1024]{1,0:T(8,128)(2,1)} %documents.1) | copy-start | bytes 393220
  10.7 0.9 %copy-start.1 = (bf16[64,1024]{1,0:T(8,128)(2,1)S(1)}, bf16[64,1024]{1,0:T(8,128)(2,1)}, u32[]{:S(2)}) copy-start(bf16[64,1024]{1,0:T(8,128)(2,1)} %queries.1) | copy-start | bytes 393220
  11.6 0.7 %copy-start.3 = (s32[2048]{0:T(1024)S(1)}, s32[2048]{0:T(1024)}, u32[]{:S(2)}) copy-start(s32[2048]{0:T(1024)} %param.5) | copy-start | bytes 24580
  13.3 0.9 %copy-start.2 = (bf16[64,1024]{1,0:T(8,128)(2,1)S(1)}, bf16[64,1024]{1,0:T(8,128)(2,1)}, u32[]{:S(2)}) copy-start(bf16[64,1024]{1,0:T(8,128)(2,1)} %queries.1) | copy-start | bytes 393220
  14.2 6.9 %collective-permute-start.6 = (bf16[64,1024]{1,0:T(8,128)(2,1)S(1)}, bf16[64,1024]{1,0:T(8,128)(2,1)S(1)}, u32[]{:S(2)}, u32[]{:S(2)}) collective-permute-start(bf16[64,1024]{1,0:T(8,128)(2,1)S(1)} %copy-done.2), channel_id=1, source_target_pairs={{0,24},{8,16},{16,8},{24,0},{1,25},{9,17},{17,9},{25,1},{2,26},{10... | collective-permute-start | bytes 393224 | tf_op jit(solution)/shard_map/ppermute | solution.py:26
  14.3 7.0 %collective-permute-start.3 = (bf16[256,1024]{1,0:T(8,128)(2,1)S(1)}, bf16[256,1024]{1,0:T(8,128)(2,1)S(1)}, u32[]{:S(2)}, u32[]{:S(2)}) collective-permute-start(bf16[256,1024]{1,0:T(8,128)(2,1)S(1)} %pad_maximum_fusion), channel_id=1, source_target_pairs={{0,1},{1,0},{2,3},{3,2},{4,5},{5,4},{6,7},{7,6},{8,9},{9,8},{10,11... | collective-permute-start | bytes 1572872 | tf_op jit(solution)/shard_map/ppermute | solution.py:35
  21.1 9.1 %collective-permute-start.14 = (bf16[256,1024]{1,0:T(8,128)(2,1)S(1)}, bf16[256,1024]{1,0:T(8,128)(2,1)S(1)}, u32[]{:S(2)}, u32[]{:S(2)}) collective-permute-start(bf16[256,1024]{1,0:T(8,128)(2,1)S(1)} %constant_dynamic-update-slice_fusion.5.queries.q_mine), channel_id=1, source_target_pairs={{0,1},{1,0},{2,3},{3,2},{4,5},{5,4},{6,7},{7,6},{8,9},{9,8},{10,11... | collective-permute-start | bytes 1572872 | tf_op jit(solution)/shard_map/ppermute | solution.py:35
  21.9 4.5 %collective-permute-start.7 = (f32[8,256]{1,0:T(8,128)S(1)}, f32[8,256]{1,0:T(8,128)S(1)}, u32[]{:S(2)}, u32[]{:S(2)}) collective-permute-start(f32[8,256]{1,0:T(8,128)S(1)} %get-tuple-element.28.s0.stats), channel_id=1, source_target_pairs={{0,8},{8,0},{16,24},{24,16},{1,9},{9,1},{17,25},{25,17},{2,10},{10... | collective-permute-start | bytes 24584 | tf_op jit(solution)/shard_map/ppermute | solution.py:26
  22.7 4.6 %collective-permute-start.8 = (f32[8,256]{1,0:T(8,128)S(1)}, f32[8,256]{1,0:T(8,128)S(1)}, u32[]{:S(2)}, u32[]{:S(2)}) collective-permute-start(f32[8,256]{1,0:T(8,128)S(1)} %get-tuple-element.28.s0.stats), channel_id=1, source_target_pairs={{0,16},{8,24},{16,0},{24,8},{1,17},{9,25},{17,1},{25,9},{2,18},{10... | collective-permute-start | bytes 24584 | tf_op jit(solution)/shard_map/ppermute | solution.py:26
  23.7 5.4 %collective-permute-start.9 = (f32[8,256]{1,0:T(8,128)S(1)}, f32[8,256]{1,0:T(8,128)S(1)}, u32[]{:S(2)}, u32[]{:S(2)}) collective-permute-start(f32[8,256]{1,0:T(8,128)S(1)} %get-tuple-element.28.s0.stats), channel_id=1, source_target_pairs={{0,24},{8,16},{16,8},{24,0},{1,25},{9,17},{17,9},{25,1},{2,26},{10... | collective-permute-start | bytes 24584 | tf_op jit(solution)/shard_map/ppermute | solution.py:26
  29.5 1.4 %collective-permute-start.13 = (bf16[264,256]{1,0:T(8,128)(2,1)S(1)}, bf16[264,256]{1,0:T(8,128)(2,1)S(1)}, u32[]{:S(2)}, u32[]{:S(2)}) collective-permute-start(bf16[264,256]{1,0:T(8,128)(2,1)S(1)} %get-tuple-element.32.w_send), channel_id=1, source_target_pairs={{0,1},{1,0},{2,3},{3,2},{4,5},{5,4},{6,7},{7,6},{8,9},{9,8},{10,11... | collective-permute-start | bytes 405512 | tf_op jit(solution)/shard_map/ppermute | solution.py:35
  30.0 7.3 %collective-permute-start.10 = (bf16[64,1024]{1,0:T(8,128)(2,1)S(1)}, bf16[64,1024]{1,0:T(8,128)(2,1)S(1)}, u32[]{:S(2)}, u32[]{:S(2)}) collective-permute-start(bf16[64,1024]{1,0:T(8,128)(2,1)S(1)} %get-tuple-element.34), channel_id=1, source_target_pairs={{0,8},{8,0},{16,24},{24,16},{1,9},{9,1},{17,25},{25,17},{2,10},{10... | collective-permute-start | bytes 393224 | tf_op jit(solution)/shard_map/ppermute | solution.py:26
  31.3 16.4 %collective-permute-start.15 = (bf16[520,128]{1,0:T(8,128)(2,1)S(1)}, bf16[520,128]{1,0:T(8,128)(2,1)S(1)}, u32[]{:S(2)}, u32[]{:S(2)}) collective-permute-start(bf16[520,128]{1,0:T(8,128)(2,1)S(1)} %get-tuple-element.40), channel_id=1, source_target_pairs={{0,2},{2,0},{4,6},{6,4},{1,3},{3,1},{5,7},{7,5},{8,10},{10,8},{12,... | collective-permute-start | bytes 399368 | tf_op jit(solution)/shard_map/ppermute | solution.py:26
  32.9 14.9 %collective-permute-start.16 = (bf16[520,128]{1,0:T(8,128)(2,1)S(1)}, bf16[520,128]{1,0:T(8,128)(2,1)S(1)}, u32[]{:S(2)}, u32[]{:S(2)}) collective-permute-start(bf16[520,128]{1,0:T(8,128)(2,1)S(1)} %get-tuple-element.41), channel_id=1, source_target_pairs={{0,4},{2,6},{4,0},{6,2},{1,5},{3,7},{5,1},{7,3},{8,12},{10,14},{12... | collective-permute-start | bytes 399368 | tf_op jit(solution)/shard_map/ppermute | solution.py:26
  34.4 13.4 %collective-permute-start.17 = (bf16[520,128]{1,0:T(8,128)(2,1)S(1)}, bf16[520,128]{1,0:T(8,128)(2,1)S(1)}, u32[]{:S(2)}, u32[]{:S(2)}) collective-permute-start(bf16[520,128]{1,0:T(8,128)(2,1)S(1)} %get-tuple-element.42), channel_id=1, source_target_pairs={{0,6},{2,4},{4,2},{6,0},{1,7},{3,5},{5,3},{7,1},{8,14},{10,12},{12... | collective-permute-start | bytes 399368 | tf_op jit(solution)/shard_map/ppermute | solution.py:26
  34.9 12.0 %collective-permute-start.11 = (bf16[64,1024]{1,0:T(8,128)(2,1)S(1)}, bf16[64,1024]{1,0:T(8,128)(2,1)S(1)}, u32[]{:S(2)}, u32[]{:S(2)}) collective-permute-start(bf16[64,1024]{1,0:T(8,128)(2,1)S(1)} %get-tuple-element.35), channel_id=1, source_target_pairs={{0,16},{8,24},{16,0},{24,8},{1,17},{9,25},{17,1},{25,9},{2,18},{10... | collective-permute-start | bytes 393224 | tf_op jit(solution)/shard_map/ppermute | solution.py:26
  37.3 9.6 %collective-permute-start.12 = (bf16[64,1024]{1,0:T(8,128)(2,1)S(1)}, bf16[64,1024]{1,0:T(8,128)(2,1)S(1)}, u32[]{:S(2)}, u32[]{:S(2)}) collective-permute-start(bf16[64,1024]{1,0:T(8,128)(2,1)S(1)} %get-tuple-element.36), channel_id=1, source_target_pairs={{0,24},{8,16},{16,8},{24,0},{1,25},{9,17},{17,9},{25,1},{2,26},{10... | collective-permute-start | bytes 393224 | tf_op jit(solution)/shard_map/ppermute | solution.py:26

commit v3 on v2

--- a/solution.py
+++ b/solution.py
@@ -45,14 +45,18 @@
     return lax.dot_general(a, b, (((da,), (db,)), ((), ())), preferred_element_type=F32)
 
 
-def call(kernel, outs, *args, scratch=()):
+def piece_order(plane):
+    return [0] + list(range(plane - 1, 0, -1))
+
+
+def call(kernel, outs, *args, scratch=(), in_hbm=False):
     vmem = pl.BlockSpec(memory_space=pltpu.VMEM)
     sizes = [a.size * a.dtype.itemsize for a in args]
     sizes += [math.prod(shape) * jnp.dtype(dtype).itemsize for shape, dtype in outs]
     return pl.pallas_call(
         kernel,
         out_shape=[jax.ShapeDtypeStruct(shape, dtype) for shape, dtype in outs],
-        in_specs=[vmem] * len(args),
+        in_specs=[pl.BlockSpec(memory_space=pl.ANY) if in_hbm else vmem] * len(args),
         out_specs=[vmem] * len(outs),
         scratch_shapes=list(scratch),
         compiler_params=pltpu.CompilerParams(vmem_limit_bytes=min(3 * sum(sizes), 40 << 20) + (6 << 20)),
@@ -87,12 +91,17 @@
     return jnp.where(core == 0, low, high), jnp.where(core == 0, high, low)
 
 
-def id_kernel(rows, plane, ids, queries, documents, counts, total, positive, q_own, d_own, found):
+def id_kernel(rows, plane, ids_in, queries, documents, counts, total, positive, q_own, d_own, found, ids, sems):
     quarters = ids.shape[0] // plane
     my_quarter, my_core = lax.axis_index("quarter"), lax.axis_index("core")
     my_plane = lax.axis_index(PLANE)
-    q_own[...] = queries[...]
-    d_own[...] = documents[...]
+    copies = [
+        pltpu.make_async_copy(src, dst, sems.at[i])
+        for i, (src, dst) in enumerate(((ids_in, ids), (documents, d_own), (queries, q_own)))
+    ]
+    for copy in copies:
+        copy.start()
+    copies[0].wait()
     chips, lanes = ids.shape
     square = ids[...]
     if chips < lanes:
@@ -117,12 +126,14 @@
         row = found[pl.ds((my_quarter ^ k) * plane + my_plane, 1), :]
         counts[:, k * rows : (k + 1) * rows] = halves(row, my_core, rows)[0]
     own = halves(ids[pl.ds(my_quarter * plane + my_plane, 1), :], my_core, rows)[0]
-    for k in range(plane):
-        row = ids[pl.ds(my_quarter * plane + (my_plane ^ k), 1), :]
+    for k, piece in enumerate(piece_order(plane)):
+        row = ids[pl.ds(my_quarter * plane + (my_plane ^ piece), 1), :]
         column = jnp.transpose(jnp.broadcast_to(row, (8, lanes)))[:, :1]
         low, high = (column[:rows] == own).astype(F32), (column[rows:] == own).astype(F32)
         positive[k * rows : (k + 1) * rows, :] = jnp.where(my_core == 0, low, high)
         positive[(plane + k) * rows : (plane + k + 1) * rows, :] = jnp.where(my_core == 0, high, low)
+    for copy in copies[1:]:
+        copy.wait()
 
 
 def split3(x):
@@ -238,13 +249,15 @@
     chip_loss[...] = line
     tiles = own.shape[1] // LANES
     note = spread(line, LANES)
+    order = piece_order(half // rows)
     for out in outs:
         out[tiles * rows :, :] = note
     for at in range(0, half, CHUNK):
         part = contract(w_mine[at : at + CHUNK, :], q_mine[...], 1, 0)
         part = (part + contract(w_in[at : at + CHUNK, :], q_other[...], 1, 0)) * scale
-        for k in range(at // rows, (at + CHUNK) // rows):
-            share = part[k * rows - at : (k + 1) * rows - at]
+        for j in range(at // rows, (at + CHUNK) // rows):
+            share = part[j * rows - at : (j + 1) * rows - at]
+            k = order[j]
             if k == 0:
                 own[...] = share
             else:
@@ -252,24 +265,23 @@
                     outs[k - 1][t * rows : (t + 1) * rows, :] = share[:, t * LANES : (t + 1) * LANES].astype(BF16)
 
 
-def query_sum_kernel(own, gains, *refs):
-    *got, out = refs
-    total = own[...]
-    for k, ref in enumerate(got, 1):
-        total = total + gains[:, k : k + 1] * ref[...].astype(F32)
-    out[...] = total.astype(BF16)
-
-
-def doc_sum_kernel(own, chip_loss, all_pairs, *refs):
-    *got, out, loss = refs
+def sum_kernel(peers, own_query, gains, own, chip_loss, all_pairs, *refs):
+    *got, query_out, doc_out, loss = refs
+    q_got, d_got = got[:peers], got[peers:]
     rows = own.shape[0]
     tiles = own.shape[1] // LANES
+    gain = [gains[:, k : k + 1] for k in range(peers + 1)]
     for t in range(tiles):
-        total = own[:, t * LANES : (t + 1) * LANES]
-        for ref in got:
+        lanes = slice(t * LANES, (t + 1) * LANES)
+        total = own_query[:, lanes]
+        for k, ref in enumerate(q_got, 1):
+            total = total + gain[k] * ref[:, lanes].astype(F32)
+        query_out[:, lanes] = total.astype(BF16)
+        total = own[:, lanes]
+        for ref in d_got:
             total = total + ref[t * rows : (t + 1) * rows, :].astype(F32)
-        out[:, t * LANES : (t + 1) * LANES] = total.astype(BF16)
-    losses = [chip_loss[...]] + [gather3(ref[tiles * rows :, :]) for ref in got]
+        doc_out[:, lanes] = total.astype(BF16)
+    losses = [chip_loss[...]] + [gather3(ref[tiles * rows :, :]) for ref in d_got]
     loss[...] = (tree_sum(losses) / all_pairs[:, :128])[:1]
 
 
@@ -293,13 +305,20 @@
         user_ids.reshape(quarters * plane, 2 * rows),
         queries,
         documents,
-        scratch=[pltpu.VMEM((quarters * plane, 2 * rows), F32)],
+        scratch=[
+            pltpu.VMEM((quarters * plane, 2 * rows), F32),
+            pltpu.VMEM((quarters * plane, 2 * rows), user_ids.dtype),
+            pltpu.SemaphoreType.DMA((3,)),
+        ],
+        in_hbm=True,
     )
     d_parts[0], q_parts[0] = d_own, q_own
-    d_mine = jnp.concatenate(d_parts, 0)
-    d_other = swap_cores(d_mine)
+    d_parts = [d_parts[k] for k in piece_order(plane)]
+    d_first = jnp.concatenate(d_parts[:-1], 0)
+    first_other = swap_cores(d_first)
+    last_other = swap_cores(d_parts[-1])
     q_mine = jnp.concatenate(q_parts, 0)
-    docs = jnp.concatenate([d_mine, d_other], 0)
+    docs = jnp.concatenate([d_first, d_parts[-1], first_other, last_other], 0)
 
     scores, stats = call(
         functools.partial(score_kernel, scale, rows),
@@ -334,8 +353,17 @@
         line_loss,
     )
     d_got = send_pieces([d_share[0]] + list(d_share), PLANE)
-    doc_grad, loss = call(doc_sum_kernel, [piece, ((1, 128), F32)], own_doc, chip_loss, total, *d_got[1:])
-    (query_grad,) = call(query_sum_kernel, [piece], own_query, gains, *q_got[1:])
+    query_grad, doc_grad, loss = call(
+        functools.partial(sum_kernel, quarters - 1),
+        [piece, piece, ((1, 128), F32)],
+        own_query,
+        gains,
+        own_doc,
+        chip_loss,
+        total,
+        *q_got[1:],
+        *d_got[1:],
+    )
     return query_grad, doc_grad, loss[0, 0]
 
 

time: 48.8 us -> 50 us (1.025)
  starting transfers between devices: 21.4 us -> 22.1 us
  waiting for transfers between devices: 18.1 us -> 18.6 us
    ppermute x3 -> x4, waiting for transfers between devices: 0.67 us -> 1.81 us  [swap_cores(): return lax.ppermute(array, 'core', [(0, 1), (1, 0)])]
    ppermute x15, waiting for transfers between devices: 17.4 us -> 16.8 us  [send_pieces(): out[k] = lax.ppermute(pieces[k], axes, [(i, i ^ k) for i in range(count)])]
    ppermute x3 -> x4, starting transfers between devices: 0.22 us -> 0.77 us  [swap_cores(): return lax.ppermute(array, 'core', [(0, 1), (1, 0)])]
    pallas_call x8 -> x7, Pallas kernels: 4.73 us -> 4.42 us  [call(): pl.pallas_call(kernel, out_shape=[jax.ShapeDtypeStruct(shape, dtype) for...]
    unnamed x15 -> x16, local copies, waits for them, and re-layouts: 3.45 us -> 3.51 us
  transfers between devices with their start and end apart: 18 -> 19, of which waited for: 6 -> 7; matrix products, arithmetic and copies ran while one was open for 0% -> 0% of each run, Pallas kernels for 8% -> 7%
where the time goes in v3:
time: 50 us; the launch traced here: 49.4 us
  starting transfers between devices  22.1 us (44%)
  waiting for transfers between devices  18.6 us (37%)
  Pallas kernels  4.42 us (9%)
  local copies, waits for them, and re-layouts  3.53 us (7%)
  between operations  0.82 us (2%)
    ppermute x15, starting transfers between devices, send_pieces(): out[k] = lax.ppermute(pieces[k], axes, [(i, i ^ k) for i in range(count)])  21.3 us
    ppermute x15, waiting for transfers between devices, send_pieces(): out[k] = lax.ppermute(pieces[k], axes, [(i, i ^ k) for i in range(count)])  16.8 us
    pallas_call x7, Pallas kernels, call(): pl.pallas_call(kernel, out_shape=[jax.ShapeDtypeStruct(shape, dtype) for...  4.42 us
    unnamed x16, local copies, waits for them, and re-layouts  3.51 us
    ppermute x4, waiting for transfers between devices, swap_cores(): return lax.ppermute(array, 'core', [(0, 1), (1, 0)])  1.81 us
  transfers between devices with their start and end apart: 19, of which 7 were waited for; matrix products, arithmetic and copies ran while one was open for 0% of the time, Pallas kernels for 7%

profile of v3, /device:TPU:0, one launch (start us, length us, event | category | flops | bytes accessed | tf_op | source)
XLA Modules:
  0.0 49.4 jit_solution(10863755252568101679)
XLA Ops:
  0.6 4.0 %collective-permute-start = (bf16[64,1024]{1,0:T(8,128)(2,1)}, bf16[64,1024]{1,0:T(8,128)(2,1)S(1)}, u32[]{:S(2)}, u32[]{:S(2)}) collective-permute-start(bf16[64,1024]{1,0:T(8,128)(2,1)} %documents.1), channel_id=1, source_target_pairs={{0,6},{2,4},{4,2},{6,0},{1,7},{3,5},{5,3},{7,1},{8,14},{10,12},{12... | collective-permute-start | bytes 393224 | tf_op jit(solution)/shard_map/ppermute | solution.py:26
  4.6 0.5 %collective-permute-start.1 = (bf16[64,1024]{1,0:T(8,128)(2,1)}, bf16[64,1024]{1,0:T(8,128)(2,1)S(1)}, u32[]{:S(2)}, u32[]{:S(2)}) collective-permute-start(bf16[64,1024]{1,0:T(8,128)(2,1)} %documents.1), channel_id=1, source_target_pairs={{0,4},{2,6},{4,0},{6,2},{1,5},{3,7},{5,1},{7,3},{8,12},{10,14},{12... | collective-permute-start | bytes 393224 | tf_op jit(solution)/shard_map/ppermute | solution.py:26
  5.1 0.1 collective-permute-start.2
  5.3 2.0 %collective-permute-start.5 = (bf16[64,1024]{1,0:T(8,128)(2,1)}, bf16[64,1024]{1,0:T(8,128)(2,1)S(1)}, u32[]{:S(2)}, u32[]{:S(2)}) collective-permute-start(bf16[64,1024]{1,0:T(8,128)(2,1)} %queries.1), channel_id=1, source_target_pairs={{0,8},{8,0},{16,24},{24,16},{1,9},{9,1},{17,25},{25,17},{2,10},{10... | collective-permute-start | bytes 393224 | tf_op jit(solution)/shard_map/ppermute | solution.py:26
  7.2 2.6 %collective-permute-start.6 = (bf16[64,1024]{1,0:T(8,128)(2,1)}, bf16[64,1024]{1,0:T(8,128)(2,1)S(1)}, u32[]{:S(2)}, u32[]{:S(2)}) collective-permute-start(bf16[64,1024]{1,0:T(8,128)(2,1)} %queries.1), channel_id=1, source_target_pairs={{0,16},{8,24},{16,0},{24,8},{1,17},{9,25},{17,1},{25,9},{2,18},{10... | collective-permute-start | bytes 393224 | tf_op jit(solution)/shard_map/ppermute | solution.py:26
  9.8 0.0 copy-start
  9.8 0.9 %copy-done = bf16[64,1024]{1,0:T(8,128)(2,1)S(1)} copy-done((bf16[64,1024]{1,0:T(8,128)(2,1)S(1)}, bf16[64,1024]{1,0:T(8,128)(2,1)}, u32[]{:S(2)}) %copy-start) | copy-done | bytes 131096
  10.8 0.0 copy-start.2
  10.8 0.9 %copy-done.2 = bf16[64,1024]{1,0:T(8,128)(2,1)S(1)} copy-done((bf16[64,1024]{1,0:T(8,128)(2,1)S(1)}, bf16[64,1024]{1,0:T(8,128)(2,1)}, u32[]{:S(2)}) %copy-start.2) | copy-done | bytes 131096
  11.7 0.0 copy-start.3
  11.7 0.7 %copy-done.3 = s32[2048]{0:T(1024)S(1)} copy-done((s32[2048]{0:T(1024)S(1)}, s32[2048]{0:T(1024)}, u32[]{:S(2)}) %copy-start.3) | copy-done | bytes 8216
  12.4 1.3 %shard_map.58 = (f32[1,256]{1,0:T(1,128)S(1)}, f32[8,256]{1,0:T(8,128)S(1)}, f32[512,64]{1,0:T(8,128)S(1)}, bf16[64,1024]{1,0:T(8,128)(2,1)S(1)}, bf16[64,1024]{1,0:T(8,128)(2,1)S(1)}) custom-call(s32[16,128]{1,0:T(8,128)S(1)} %bitcast.3, bf16[64,1024]{1,0:T(8,128)(2,1)S(1)} %copy-done, bf16[64,1024]{1,0:T(8,128)(2,1)S(1)} %copy-done.2), custom_call_target="tpu_custom_call" | custom-call | tf_op jit(solution)/shard_map/pallas_call | solution.py:56
  13.7 0.0 copy-start.1
  13.8 0.0 collective-permute-done
  13.8 0.9 %copy-done.1 = bf16[64,1024]{1,0:T(8,128)(2,1)S(1)} copy-done((bf16[64,1024]{1,0:T(8,128)(2,1)S(1)}, bf16[64,1024]{1,0:T(8,128)(2,1)}, u32[]{:S(2)}) %copy-start.1) | copy-done | bytes 131096
  14.6 0.0 collective-permute-start.7
  14.6 0.0 collective-permute-done.1
  14.7 0.1 collective-permute-start.3
  14.8 0.0 collective-permute-done.5
  14.8 0.5 %collective-permute-done.6 = bf16[64,1024]{1,0:T(8,128)(2,1)S(1)} collective-permute-done((bf16[64,1024]{1,0:T(8,128)(2,1)}, bf16[64,1024]{1,0:T(8,128)(2,1)S(1)}, u32[]{:S(2)}, u32[]{:S(2)}) %collective-permute-start.6) | collective-permute-done | bytes 131104 | tf_op jit(solution)/shard_map/ppermute | solution.py:26
  15.4 6.2 %collective-permute-done.7 = bf16[64,1024]{1,0:T(8,128)(2,1)S(1)} collective-permute-done((bf16[64,1024]{1,0:T(8,128)(2,1)S(1)}, bf16[64,1024]{1,0:T(8,128)(2,1)S(1)}, u32[]{:S(2)}, u32[]{:S(2)}) %collective-permute-start.7) | collective-permute-done | bytes 131104 | tf_op jit(solution)/shard_map/ppermute | solution.py:26
  21.5 0.1 collective-permute-start.12
  21.6 0.0 collective-permute-done.2
  21.7 0.6 %collective-permute-start.4 = (bf16[64,1024]{1,0:T(8,128)(2,1)S(1)}, bf16[64,1024]{1,0:T(8,128)(2,1)S(1)}, u32[]{:S(2)}, u32[]{:S(2)}) collective-permute-start(bf16[64,1024]{1,0:T(8,128)(2,1)S(1)} %collective-permute-done.2), channel_id=1, source_target_pairs={{0,1},{1,0},{2,3},{3,2},{4,5},{5,4},{6,7},{7,6},{8,9},{9,8},{10,11... | collective-permute-start | bytes 393224 | tf_op jit(solution)/shard_map/ppermute | solution.py:35
  22.2 0.0 collective-permute-done.3
  22.3 1.4 %collective-permute-done.4 = bf16[64,1024]{1,0:T(8,128)(2,1)S(1)} collective-permute-done((bf16[64,1024]{1,0:T(8,128)(2,1)S(1)}, bf16[64,1024]{1,0:T(8,128)(2,1)S(1)}, u32[]{:S(2)}, u32[]{:S(2)}) %collective-permute-start.4) | collective-permute-done | bytes 131104 | tf_op jit(solution)/shard_map/ppermute | solution.py:35
  23.7 0.6 %shard_map.59 = (f32[512,256]{1,0:T(8,128)S(1)}, f32[8,256]{1,0:T(8,128)S(1)}) custom-call(bf16[512,1024]{1,0:T(8,128)(2,1)S(1)} %constant_dynamic-update-slice_fusion.docs, bf16[256,1024]{1,0:T(8,128)(2,1)S(1)} %constant_dynamic-update-slice_fusion.6.queries.q_mine, f32[512,64]{1,0:T(8,128)S(1)} %get-tuple-element.27.positive), custom_call_target="tpu_custom_call" | custom-call | tf_op jit(solution)/shard_map/pallas_call | solution.py:56
  24.3 0.2 collective-permute-start.10
  24.5 1.6 %collective-permute-start.8 = (f32[8,256]{1,0:T(8,128)S(1)}, f32[8,256]{1,0:T(8,128)S(1)}, u32[]{:S(2)}, u32[]{:S(2)}) collective-permute-start(f32[8,256]{1,0:T(8,128)S(1)} %get-tuple-element.29.s0.stats), channel_id=1, source_target_pairs={{0,8},{8,0},{16,24},{24,16},{1,9},{9,1},{17,25},{25,17},{2,10},{10... | collective-permute-start | bytes 24584 | tf_op jit(solution)/shard_map/ppermute | solution.py:26
  26.1 2.6 %collective-permute-start.9 = (f32[8,256]{1,0:T(8,128)S(1)}, f32[8,256]{1,0:T(8,128)S(1)}, u32[]{:S(2)}, u32[]{:S(2)}) collective-permute-start(f32[8,256]{1,0:T(8,128)S(1)} %get-tuple-element.29.s0.stats), channel_id=1, source_target_pairs={{0,16},{8,24},{16,0},{24,8},{1,17},{9,25},{17,1},{25,9},{2,18},{10... | collective-permute-start | bytes 24584 | tf_op jit(solution)/shard_map/ppermute | solution.py:26
  28.8 1.1 %collective-permute-done.10.s3 = f32[8,256]{1,0:T(8,128)S(1)} collective-permute-done((f32[8,256]{1,0:T(8,128)S(1)}, f32[8,256]{1,0:T(8,128)S(1)}, u32[]{:S(2)}, u32[]{:S(2)}) %collective-permute-start.10) | collective-permute-done | bytes 8224 | tf_op jit(solution)/shard_map/ppermute | solution.py:26
  29.8 0.0 collective-permute-done.8.s1
  29.8 0.9 %collective-permute-done.9.s2 = f32[8,256]{1,0:T(8,128)S(1)} collective-permute-done((f32[8,256]{1,0:T(8,128)S(1)}, f32[8,256]{1,0:T(8,128)S(1)}, u32[]{:S(2)}, u32[]{:S(2)}) %collective-permute-start.9) | collective-permute-done | bytes 8224 | tf_op jit(solution)/shard_map/ppermute | solution.py:26
  30.7 0.4 shard_map.60
  31.0 0.1 collective-permute-start.11
  31.1 0.4 shard_map.63
  31.6 0.5 %collective-permute-start.13 = (bf16[64,1024]{1,0:T(8,128)(2,1)S(1)}, bf16[64,1024]{1,0:T(8,128)(2,1)S(1)}, u32[]{:S(2)}, u32[]{:S(2)}) collective-permute-start(bf16[64,1024]{1,0:T(8,128)(2,1)S(1)} %get-tuple-element.38), channel_id=1, source_target_pairs={{0,8},{8,0},{16,24},{24,16},{1,9},{9,1},{17,25},{25,17},{2,10},{10... | collective-permute-start | bytes 393224 | tf_op jit(solution)/shard_map/ppermute | solution.py:26
  32.1 0.0 collective-permute-done.12.q_other
  32.1 0.4 collective-permute-done.11.w_in
  32.5 0.4 shard_map.62
  32.9 1.6 %collective-permute-start.16 = (bf16[520,128]{1,0:T(8,128)(2,1)S(1)}, bf16[520,128]{1,0:T(8,128)(2,1)S(1)}, u32[]{:S(2)}, u32[]{:S(2)}) collective-permute-start(bf16[520,128]{1,0:T(8,128)(2,1)S(1)} %get-tuple-element.41), channel_id=1, source_target_pairs={{0,2},{2,0},{4,6},{6,4},{1,3},{3,1},{5,7},{7,5},{8,10},{10,8},{12,... | collective-permute-start | bytes 399368 | tf_op jit(solution)/shard_map/ppermute | solution.py:26
  34.5 1.5 %collective-permute-start.17 = (bf16[520,128]{1,0:T(8,128)(2,1)S(1)}, bf16[520,128]{1,0:T(8,128)(2,1)S(1)}, u32[]{:S(2)}, u32[]{:S(2)}) collective-permute-start(bf16[520,128]{1,0:T(8,128)(2,1)S(1)} %get-tuple-element.42), channel_id=1, source_target_pairs={{0,4},{2,6},{4,0},{6,2},{1,5},{3,7},{5,1},{7,3},{8,12},{10,14},{12... | collective-permute-start | bytes 399368 | tf_op jit(solution)/shard_map/ppermute | solution.py:26
  36.0 0.5 collective-permute-start.18
  36.5 2.6 %collective-permute-start.14 = (bf16[64,1024]{1,0:T(8,128)(2,1)S(1)}, bf16[64,1024]{1,0:T(8,128)(2,1)S(1)}, u32[]{:S(2)}, u32[]{:S(2)}) collective-permute-start(bf16[64,1024]{1,0:T(8,128)(2,1)S(1)} %get-tuple-element.39), channel_id=1, source_target_pairs={{0,16},{8,24},{16,0},{24,8},{1,17},{9,25},{17,1},{25,9},{2,18},{10... | collective-permute-start | bytes 393224 | tf_op jit(solution)/shard_map/ppermute | solution.py:26
  39.1 0.0 collective-permute-done.13.refs_0_
  39.1 0.9 %collective-permute-start.15 = (bf16[64,1024]{1,0:T(8,128)(2,1)S(1)}, bf16[64,1024]{1,0:T(8,128)(2,1)S(1)}, u32[]{:S(2)}, u32[]{:S(2)}) collective-permute-start(bf16[64,1024]{1,0:T(8,128)(2,1)S(1)} %get-tuple-element.40), channel_id=1, source_target_pairs={{0,24},{8,16},{16,8},{24,0},{1,25},{9,17},{17,9},{25,1},{2,26},{10... | collective-permute-start | bytes 393224 | tf_op jit(solution)/shard_map/ppermute | solution.py:26
  40.0 0.3 shard_map.61.own_query
  40.4 8.1 %collective-permute-done.14.refs_1_ = bf16[64,1024]{1,0:T(8,128)(2,1)S(1)} collective-permute-done((bf16[64,1024]{1,0:T(8,128)(2,1)S(1)}, bf16[64,1024]{1,0:T(8,128)(2,1)S(1)}, u32[]{:S(2)}, u32[]{:S(2)}) %collective-permute-start.14) | collective-permute-done | bytes 131104 | tf_op jit(solution)/shard_map/ppermute | solution.py:26
  48.5 0.0 collective-permute-done.15.refs_2_
  48.5 0.0 collective-permute-done.16.refs_3_
  48.5 0.0 collective-permute-done.17.refs_4_
  48.5 0.0 collective-permute-done.18.refs_5_
  48.5 0.9 %shard_map.64 = (bf16[64,1024]{1,0:T(8,128)(2,1)}, bf16[64,1024]{1,0:T(8,128)(2,1)}, f32[1,128]{1,0:T(1,128)}) custom-call(f32[64,1024]{1,0:T(8,128)S(1)} %shard_map.61.own_query, f32[64,8]{1,0:T(8,128)S(1)} %get-tuple-element.34.gains, f32[64,1024]{1,0:T(8,128)S(1)} %get-tuple-element.36.own, f32[8,128]{1,0:T(8,128)S(1)} %get-tuple-element.37.chip_loss, ...), custom_call_target="tpu_custom_call" | custom-call | tf_op jit(solution)/shard_map/pallas_call | solution.py:56
  (11 shorter events, 0.1 us)
Async XLA Ops:
  0.6 13.1 %collective-permute-start = (bf16[64,1024]{1,0:T(8,128)(2,1)}, bf16[64,1024]{1,0:T(8,128)(2,1)S(1)}, u32[]{:S(2)}, u32[]{:S(2)}) collective-permute-start(bf16[64,1024]{1,0:T(8,128)(2,1)} %documents.1), channel_id=1, source_target_pairs={{0,6},{2,4},{4,2},{6,0},{1,7},{3,5},{5,3},{7,1},{8,14},{10,12},{12... | collective-permute-start | bytes 393224 | tf_op jit(solution)/shard_map/ppermute | solution.py:26
  4.6 10.0 %collective-permute-start.1 = (bf16[64,1024]{1,0:T(8,128)(2,1)}, bf16[64,1024]{1,0:T(8,128)(2,1)S(1)}, u32[]{:S(2)}, u32[]{:S(2)}) collective-permute-start(bf16[64,1024]{1,0:T(8,128)(2,1)} %documents.1), channel_id=1, source_target_pairs={{0,4},{2,6},{4,0},{6,2},{1,5},{3,7},{5,1},{7,3},{8,12},{10,14},{12... | collective-permute-start | bytes 393224 | tf_op jit(solution)/shard_map/ppermute | solution.py:26
  5.1 16.5 %collective-permute-start.2 = (bf16[64,1024]{1,0:T(8,128)(2,1)}, bf16[64,1024]{1,0:T(8,128)(2,1)S(1)}, u32[]{:S(2)}, u32[]{:S(2)}) collective-permute-start(bf16[64,1024]{1,0:T(8,128)(2,1)} %documents.1), channel_id=1, source_target_pairs={{0,2},{2,0},{4,6},{6,4},{1,3},{3,1},{5,7},{7,5},{8,10},{10,8},{12,... | collective-permute-start | bytes 393224 | tf_op jit(solution)/shard_map/ppermute | solution.py:26
  5.3 9.5 %collective-permute-start.5 = (bf16[64,1024]{1,0:T(8,128)(2,1)}, bf16[64,1024]{1,0:T(8,128)(2,1)S(1)}, u32[]{:S(2)}, u32[]{:S(2)}) collective-permute-start(bf16[64,1024]{1,0:T(8,128)(2,1)} %queries.1), channel_id=1, source_target_pairs={{0,8},{8,0},{16,24},{24,16},{1,9},{9,1},{17,25},{25,17},{2,10},{10... | collective-permute-start | bytes 393224 | tf_op jit(solution)/shard_map/ppermute | solution.py:26
  7.2 8.1 %collective-permute-start.6 = (bf16[64,1024]{1,0:T(8,128)(2,1)}, bf16[64,1024]{1,0:T(8,128)(2,1)S(1)}, u32[]{:S(2)}, u32[]{:S(2)}) collective-permute-start(bf16[64,1024]{1,0:T(8,128)(2,1)} %queries.1), channel_id=1, source_target_pairs={{0,16},{8,24},{16,0},{24,8},{1,17},{9,25},{17,1},{25,9},{2,18},{10... | collective-permute-start | bytes 393224 | tf_op jit(solution)/shard_map/ppermute | solution.py:26
  9.8 0.9 %copy-start = (bf16[64,1024]{1,0:T(8,128)(2,1)S(1)}, bf16[64,1024]{1,0:T(8,128)(2,1)}, u32[]{:S(2)}) copy-start(bf16[64,1024]{1,0:T(8,128)(2,1)} %queries.1) | copy-start | bytes 393220
  10.8 0.9 %copy-start.2 = (bf16[64,1024]{1,0:T(8,128)(2,1)S(1)}, bf16[64,1024]{1,0:T(8,128)(2,1)}, u32[]{:S(2)}) copy-start(bf16[64,1024]{1,0:T(8,128)(2,1)} %documents.1) | copy-start | bytes 393220
  11.7 0.7 %copy-start.3 = (s32[2048]{0:T(1024)S(1)}, s32[2048]{0:T(1024)}, u32[]{:S(2)}) copy-start(s32[2048]{0:T(1024)} %param.5) | copy-start | bytes 24580
  13.7 0.9 %copy-start.1 = (bf16[64,1024]{1,0:T(8,128)(2,1)S(1)}, bf16[64,1024]{1,0:T(8,128)(2,1)}, u32[]{:S(2)}) copy-start(bf16[64,1024]{1,0:T(8,128)(2,1)} %queries.1) | copy-start | bytes 393220
  14.6 6.9 %collective-permute-start.7 = (bf16[64,1024]{1,0:T(8,128)(2,1)S(1)}, bf16[64,1024]{1,0:T(8,128)(2,1)S(1)}, u32[]{:S(2)}, u32[]{:S(2)}) collective-permute-start(bf16[64,1024]{1,0:T(8,128)(2,1)S(1)} %copy-done.1), channel_id=1, source_target_pairs={{0,24},{8,16},{16,8},{24,0},{1,25},{9,17},{17,9},{25,1},{2,26},{10... | collective-permute-start | bytes 393224 | tf_op jit(solution)/shard_map/ppermute | solution.py:26
  14.7 7.5 %collective-permute-start.3 = (bf16[192,1024]{1,0:T(8,128)(2,1)S(1)}, bf16[192,1024]{1,0:T(8,128)(2,1)S(1)}, u32[]{:S(2)}, u32[]{:S(2)}) collective-permute-start(bf16[192,1024]{1,0:T(8,128)(2,1)S(1)} %pad_maximum_fusion), channel_id=1, source_target_pairs={{0,1},{1,0},{2,3},{3,2},{4,5},{5,4},{6,7},{7,6},{8,9},{9,8},{10,11... | collective-permute-start | bytes 1179656 | tf_op jit(solution)/shard_map/ppermute | solution.py:35
  21.5 10.6 %collective-permute-start.12 = (bf16[256,1024]{1,0:T(8,128)(2,1)S(1)}, bf16[256,1024]{1,0:T(8,128)(2,1)S(1)}, u32[]{:S(2)}, u32[]{:S(2)}) collective-permute-start(bf16[256,1024]{1,0:T(8,128)(2,1)S(1)} %constant_dynamic-update-slice_fusion.6.queries.q_mine), channel_id=1, source_target_pairs={{0,1},{1,0},{2,3},{3,2},{4,5},{5,4},{6,7},{7,6},{8,9},{9,8},{10,11... | collective-permute-start | bytes 1572872 | tf_op jit(solution)/shard_map/ppermute | solution.py:35
  21.7 2.0 %collective-permute-start.4 = (bf16[64,1024]{1,0:T(8,128)(2,1)S(1)}, bf16[64,1024]{1,0:T(8,128)(2,1)S(1)}, u32[]{:S(2)}, u32[]{:S(2)}) collective-permute-start(bf16[64,1024]{1,0:T(8,128)(2,1)S(1)} %collective-permute-done.2), channel_id=1, source_target_pairs={{0,1},{1,0},{2,3},{3,2},{4,5},{5,4},{6,7},{7,6},{8,9},{9,8},{10,11... | collective-permute-start | bytes 393224 | tf_op jit(solution)/shard_map/ppermute | solution.py:35
  24.3 5.5 %collective-permute-start.10 = (f32[8,256]{1,0:T(8,128)S(1)}, f32[8,256]{1,0:T(8,128)S(1)}, u32[]{:S(2)}, u32[]{:S(2)}) collective-permute-start(f32[8,256]{1,0:T(8,128)S(1)} %get-tuple-element.29.s0.stats), channel_id=1, source_target_pairs={{0,24},{8,16},{16,8},{24,0},{1,25},{9,17},{17,9},{25,1},{2,26},{10... | collective-permute-start | bytes 24584 | tf_op jit(solution)/shard_map/ppermute | solution.py:26
  24.5 5.3 %collective-permute-start.8 = (f32[8,256]{1,0:T(8,128)S(1)}, f32[8,256]{1,0:T(8,128)S(1)}, u32[]{:S(2)}, u32[]{:S(2)}) collective-permute-start(f32[8,256]{1,0:T(8,128)S(1)} %get-tuple-element.29.s0.stats), channel_id=1, source_target_pairs={{0,8},{8,0},{16,24},{24,16},{1,9},{9,1},{17,25},{25,17},{2,10},{10... | collective-permute-start | bytes 24584 | tf_op jit(solution)/shard_map/ppermute | solution.py:26
  26.1 4.5 %collective-permute-start.9 = (f32[8,256]{1,0:T(8,128)S(1)}, f32[8,256]{1,0:T(8,128)S(1)}, u32[]{:S(2)}, u32[]{:S(2)}) collective-permute-start(f32[8,256]{1,0:T(8,128)S(1)} %get-tuple-element.29.s0.stats), channel_id=1, source_target_pairs={{0,16},{8,24},{16,0},{24,8},{1,17},{9,25},{17,1},{25,9},{2,18},{10... | collective-permute-start | bytes 24584 | tf_op jit(solution)/shard_map/ppermute | solution.py:26
  31.0 1.4 %collective-permute-start.11 = (bf16[264,256]{1,0:T(8,128)(2,1)S(1)}, bf16[264,256]{1,0:T(8,128)(2,1)S(1)}, u32[]{:S(2)}, u32[]{:S(2)}) collective-permute-start(bf16[264,256]{1,0:T(8,128)(2,1)S(1)} %get-tuple-element.33.w_send), channel_id=1, source_target_pairs={{0,1},{1,0},{2,3},{3,2},{4,5},{5,4},{6,7},{7,6},{8,9},{9,8},{10,11... | collective-permute-start | bytes 405512 | tf_op jit(solution)/shard_map/ppermute | solution.py:35
  31.6 7.5 %collective-permute-start.13 = (bf16[64,1024]{1,0:T(8,128)(2,1)S(1)}, bf16[64,1024]{1,0:T(8,128)(2,1)S(1)}, u32[]{:S(2)}, u32[]{:S(2)}) collective-permute-start(bf16[64,1024]{1,0:T(8,128)(2,1)S(1)} %get-tuple-element.38), channel_id=1, source_target_pairs={{0,8},{8,0},{16,24},{24,16},{1,9},{9,1},{17,25},{25,17},{2,10},{10... | collective-permute-start | bytes 393224 | tf_op jit(solution)/shard_map/ppermute | solution.py:26
  32.9 15.6 %collective-permute-start.16 = (bf16[520,128]{1,0:T(8,128)(2,1)S(1)}, bf16[520,128]{1,0:T(8,128)(2,1)S(1)}, u32[]{:S(2)}, u32[]{:S(2)}) collective-permute-start(bf16[520,128]{1,0:T(8,128)(2,1)S(1)} %get-tuple-element.41), channel_id=1, source_target_pairs={{0,2},{2,0},{4,6},{6,4},{1,3},{3,1},{5,7},{7,5},{8,10},{10,8},{12,... | collective-permute-start | bytes 399368 | tf_op jit(solution)/shard_map/ppermute | solution.py:26
  34.5 14.0 %collective-permute-start.17 = (bf16[520,128]{1,0:T(8,128)(2,1)S(1)}, bf16[520,128]{1,0:T(8,128)(2,1)S(1)}, u32[]{:S(2)}, u32[]{:S(2)}) collective-permute-start(bf16[520,128]{1,0:T(8,128)(2,1)S(1)} %get-tuple-element.42), channel_id=1, source_target_pairs={{0,4},{2,6},{4,0},{6,2},{1,5},{3,7},{5,1},{7,3},{8,12},{10,14},{12... | collective-permute-start | bytes 399368 | tf_op jit(solution)/shard_map/ppermute | solution.py:26
  36.0 12.5 %collective-permute-start.18 = (bf16[520,128]{1,0:T(8,128)(2,1)S(1)}, bf16[520,128]{1,0:T(8,128)(2,1)S(1)}, u32[]{:S(2)}, u32[]{:S(2)}) collective-permute-start(bf16[520,128]{1,0:T(8,128)(2,1)S(1)} %get-tuple-element.43), channel_id=1, source_target_pairs={{0,6},{2,4},{4,2},{6,0},{1,7},{3,5},{5,3},{7,1},{8,14},{10,12},{12... | collective-permute-start | bytes 399368 | tf_op jit(solution)/shard_map/ppermute | solution.py:26
  36.5 12.0 %collective-permute-start.14 = (bf16[64,1024]{1,0:T(8,128)(2,1)S(1)}, bf16[64,1024]{1,0:T(8,128)(2,1)S(1)}, u32[]{:S(2)}, u32[]{:S(2)}) collective-permute-start(bf16[64,1024]{1,0:T(8,128)(2,1)S(1)} %get-tuple-element.39), channel_id=1, source_target_pairs={{0,16},{8,24},{16,0},{24,8},{1,17},{9,25},{17,1},{25,9},{2,18},{10... | collective-permute-start | bytes 393224 | tf_op jit(solution)/shard_map/ppermute | solution.py:26
  39.1 9.4 %collective-permute-start.15 = (bf16[64,1024]{1,0:T(8,128)(2,1)S(1)}, bf16[64,1024]{1,0:T(8,128)(2,1)S(1)}, u32[]{:S(2)}, u32[]{:S(2)}) collective-permute-start(bf16[64,1024]{1,0:T(8,128)(2,1)S(1)} %get-tuple-element.40), channel_id=1, source_target_pairs={{0,24},{8,16},{16,8},{24,0},{1,25},{9,17},{17,9},{25,1},{2,26},{10... | collective-permute-start | bytes 393224 | tf_op jit(solution)/shard_map/ppermute | solution.py:26

commit v4 on v3

--- a/solution.py
+++ b/solution.py
@@ -200,7 +200,7 @@
     top = functools.reduce(jnp.maximum, lses)
     log_denom = top + jnp.log(tree_sum([jnp.exp(a - top) for a in lses]))
     row_counts = counts[...]
-    all_pairs = total[...]
+    per_pair = batch_rows / total[:1, :]
 
     def fill(out, base):
         def body(at):
@@ -209,13 +209,13 @@
             own = raw[:, : 2 * rows]
             pad = jnp.concatenate([positive[src, :], jnp.zeros((CHUNK, rows), F32)], 1)
             raw = jnp.concatenate([own - pad, raw[:, 2 * rows :]], 1)
-            out[pl.ds(at, CHUNK), :] = (batch_rows * raw / all_pairs[:1]).astype(BF16)
+            out[pl.ds(at, CHUNK), :] = (raw * per_pair).astype(BF16)
 
         each_chunk(half, body)
 
     fill(w_send, half)
     fill(w_mine, 0)
-    factor = batch_rows * row_counts[:, :rows] / all_pairs[:1, :rows]
+    factor = row_counts[:, :rows] * per_pair[:, :rows]
     lanes = [factor * jnp.exp(a[:, :rows] - log_denom[:, :rows]) for a in lses]
     tall = jnp.concatenate(lanes + lanes, 0)
     gains[...] = jnp.transpose(jnp.concatenate([tall, tall], 1))[:rows]

time: 50 us -> 50 us (level)
  no operation moved by 1% of the time
where the time goes in v4:
time: 50 us; the launch traced here: 49.4 us
  starting transfers between devices  22.1 us (44%)
  waiting for transfers between devices  18.6 us (37%)
  Pallas kernels  4.39 us (9%)
  local copies, waits for them, and re-layouts  3.53 us (7%)
  between operations  0.82 us (2%)
    ppermute x15, starting transfers between devices, send_pieces(): out[k] = lax.ppermute(pieces[k], axes, [(i, i ^ k) for i in range(count)])  21.3 us
    ppermute x15, waiting for transfers between devices, send_pieces(): out[k] = lax.ppermute(pieces[k], axes, [(i, i ^ k) for i in range(count)])  16.8 us
    pallas_call x7, Pallas kernels, call(): pl.pallas_call(kernel, out_shape=[jax.ShapeDtypeStruct(shape, dtype) for...  4.39 us
    unnamed x16, local copies, waits for them, and re-layouts  3.51 us
    ppermute x4, waiting for transfers between devices, swap_cores(): return lax.ppermute(array, 'core', [(0, 1), (1, 0)])  1.81 us
  transfers between devices with their start and end apart: 19, of which 7 were waited for; matrix products, arithmetic and copies ran while one was open for 0% of the time, Pallas kernels for 7%

profile of v4, /device:TPU:0, one launch (start us, length us, event | category | flops | bytes accessed | tf_op | source)
XLA Modules:
  0.0 49.4 jit_solution(7203489636515516549)
XLA Ops:
  0.6 4.0 %collective-permute-start = (bf16[64,1024]{1,0:T(8,128)(2,1)}, bf16[64,1024]{1,0:T(8,128)(2,1)S(1)}, u32[]{:S(2)}, u32[]{:S(2)}) collective-permute-start(bf16[64,1024]{1,0:T(8,128)(2,1)} %documents.1), channel_id=1, source_target_pairs={{0,6},{2,4},{4,2},{6,0},{1,7},{3,5},{5,3},{7,1},{8,14},{10,12},{12... | collective-permute-start | bytes 393224 | tf_op jit(solution)/shard_map/ppermute | solution.py:26
  4.6 0.5 %collective-permute-start.1 = (bf16[64,1024]{1,0:T(8,128)(2,1)}, bf16[64,1024]{1,0:T(8,128)(2,1)S(1)}, u32[]{:S(2)}, u32[]{:S(2)}) collective-permute-start(bf16[64,1024]{1,0:T(8,128)(2,1)} %documents.1), channel_id=1, source_target_pairs={{0,4},{2,6},{4,0},{6,2},{1,5},{3,7},{5,1},{7,3},{8,12},{10,14},{12... | collective-permute-start | bytes 393224 | tf_op jit(solution)/shard_map/ppermute | solution.py:26
  5.1 0.1 collective-permute-start.2
  5.3 2.0 %collective-permute-start.5 = (bf16[64,1024]{1,0:T(8,128)(2,1)}, bf16[64,1024]{1,0:T(8,128)(2,1)S(1)}, u32[]{:S(2)}, u32[]{:S(2)}) collective-permute-start(bf16[64,1024]{1,0:T(8,128)(2,1)} %queries.1), channel_id=1, source_target_pairs={{0,8},{8,0},{16,24},{24,16},{1,9},{9,1},{17,25},{25,17},{2,10},{10... | collective-permute-start | bytes 393224 | tf_op jit(solution)/shard_map/ppermute | solution.py:26
  7.2 2.6 %collective-permute-start.6 = (bf16[64,1024]{1,0:T(8,128)(2,1)}, bf16[64,1024]{1,0:T(8,128)(2,1)S(1)}, u32[]{:S(2)}, u32[]{:S(2)}) collective-permute-start(bf16[64,1024]{1,0:T(8,128)(2,1)} %queries.1), channel_id=1, source_target_pairs={{0,16},{8,24},{16,0},{24,8},{1,17},{9,25},{17,1},{25,9},{2,18},{10... | collective-permute-start | bytes 393224 | tf_op jit(solution)/shard_map/ppermute | solution.py:26
  9.8 0.0 copy-start
  9.8 0.9 %copy-done = bf16[64,1024]{1,0:T(8,128)(2,1)S(1)} copy-done((bf16[64,1024]{1,0:T(8,128)(2,1)S(1)}, bf16[64,1024]{1,0:T(8,128)(2,1)}, u32[]{:S(2)}) %copy-start) | copy-done | bytes 131096
  10.8 0.0 copy-start.2
  10.8 0.9 %copy-done.2 = bf16[64,1024]{1,0:T(8,128)(2,1)S(1)} copy-done((bf16[64,1024]{1,0:T(8,128)(2,1)S(1)}, bf16[64,1024]{1,0:T(8,128)(2,1)}, u32[]{:S(2)}) %copy-start.2) | copy-done | bytes 131096
  11.7 0.0 copy-start.3
  11.7 0.7 %copy-done.3 = s32[2048]{0:T(1024)S(1)} copy-done((s32[2048]{0:T(1024)S(1)}, s32[2048]{0:T(1024)}, u32[]{:S(2)}) %copy-start.3) | copy-done | bytes 8216
  12.4 1.3 %shard_map.58 = (f32[1,256]{1,0:T(1,128)S(1)}, f32[8,256]{1,0:T(8,128)S(1)}, f32[512,64]{1,0:T(8,128)S(1)}, bf16[64,1024]{1,0:T(8,128)(2,1)S(1)}, bf16[64,1024]{1,0:T(8,128)(2,1)S(1)}) custom-call(s32[16,128]{1,0:T(8,128)S(1)} %bitcast.3, bf16[64,1024]{1,0:T(8,128)(2,1)S(1)} %copy-done, bf16[64,1024]{1,0:T(8,128)(2,1)S(1)} %copy-done.2), custom_call_target="tpu_custom_call" | custom-call | tf_op jit(solution)/shard_map/pallas_call | solution.py:56
  13.7 0.0 copy-start.1
  13.8 0.0 collective-permute-done
  13.8 0.9 %copy-done.1 = bf16[64,1024]{1,0:T(8,128)(2,1)S(1)} copy-done((bf16[64,1024]{1,0:T(8,128)(2,1)S(1)}, bf16[64,1024]{1,0:T(8,128)(2,1)}, u32[]{:S(2)}) %copy-start.1) | copy-done | bytes 131096
  14.6 0.0 collective-permute-start.7
  14.6 0.0 collective-permute-done.1
  14.7 0.1 collective-permute-start.3
  14.8 0.0 collective-permute-done.5
  14.8 0.5 %collective-permute-done.6 = bf16[64,1024]{1,0:T(8,128)(2,1)S(1)} collective-permute-done((bf16[64,1024]{1,0:T(8,128)(2,1)}, bf16[64,1024]{1,0:T(8,128)(2,1)S(1)}, u32[]{:S(2)}, u32[]{:S(2)}) %collective-permute-start.6) | collective-permute-done | bytes 131104 | tf_op jit(solution)/shard_map/ppermute | solution.py:26
  15.4 6.2 %collective-permute-done.7 = bf16[64,1024]{1,0:T(8,128)(2,1)S(1)} collective-permute-done((bf16[64,1024]{1,0:T(8,128)(2,1)S(1)}, bf16[64,1024]{1,0:T(8,128)(2,1)S(1)}, u32[]{:S(2)}, u32[]{:S(2)}) %collective-permute-start.7) | collective-permute-done | bytes 131104 | tf_op jit(solution)/shard_map/ppermute | solution.py:26
  21.5 0.1 collective-permute-start.12
  21.6 0.0 collective-permute-done.2
  21.7 0.6 %collective-permute-start.4 = (bf16[64,1024]{1,0:T(8,128)(2,1)S(1)}, bf16[64,1024]{1,0:T(8,128)(2,1)S(1)}, u32[]{:S(2)}, u32[]{:S(2)}) collective-permute-start(bf16[64,1024]{1,0:T(8,128)(2,1)S(1)} %collective-permute-done.2), channel_id=1, source_target_pairs={{0,1},{1,0},{2,3},{3,2},{4,5},{5,4},{6,7},{7,6},{8,9},{9,8},{10,11... | collective-permute-start | bytes 393224 | tf_op jit(solution)/shard_map/ppermute | solution.py:35
  22.2 0.0 collective-permute-done.3
  22.3 1.4 %collective-permute-done.4 = bf16[64,1024]{1,0:T(8,128)(2,1)S(1)} collective-permute-done((bf16[64,1024]{1,0:T(8,128)(2,1)S(1)}, bf16[64,1024]{1,0:T(8,128)(2,1)S(1)}, u32[]{:S(2)}, u32[]{:S(2)}) %collective-permute-start.4) | collective-permute-done | bytes 131104 | tf_op jit(solution)/shard_map/ppermute | solution.py:35
  23.7 0.6 %shard_map.59 = (f32[512,256]{1,0:T(8,128)S(1)}, f32[8,256]{1,0:T(8,128)S(1)}) custom-call(bf16[512,1024]{1,0:T(8,128)(2,1)S(1)} %constant_dynamic-update-slice_fusion.docs, bf16[256,1024]{1,0:T(8,128)(2,1)S(1)} %constant_dynamic-update-slice_fusion.6.queries.q_mine, f32[512,64]{1,0:T(8,128)S(1)} %get-tuple-element.27.positive), custom_call_target="tpu_custom_call" | custom-call | tf_op jit(solution)/shard_map/pallas_call | solution.py:56
  24.3 0.2 collective-permute-start.10
  24.5 1.6 %collective-permute-start.8 = (f32[8,256]{1,0:T(8,128)S(1)}, f32[8,256]{1,0:T(8,128)S(1)}, u32[]{:S(2)}, u32[]{:S(2)}) collective-permute-start(f32[8,256]{1,0:T(8,128)S(1)} %get-tuple-element.29.s0.stats), channel_id=1, source_target_pairs={{0,8},{8,0},{16,24},{24,16},{1,9},{9,1},{17,25},{25,17},{2,10},{10... | collective-permute-start | bytes 24584 | tf_op jit(solution)/shard_map/ppermute | solution.py:26
  26.1 2.6 %collective-permute-start.9 = (f32[8,256]{1,0:T(8,128)S(1)}, f32[8,256]{1,0:T(8,128)S(1)}, u32[]{:S(2)}, u32[]{:S(2)}) collective-permute-start(f32[8,256]{1,0:T(8,128)S(1)} %get-tuple-element.29.s0.stats), channel_id=1, source_target_pairs={{0,16},{8,24},{16,0},{24,8},{1,17},{9,25},{17,1},{25,9},{2,18},{10... | collective-permute-start | bytes 24584 | tf_op jit(solution)/shard_map/ppermute | solution.py:26
  28.8 1.1 %collective-permute-done.10.s3 = f32[8,256]{1,0:T(8,128)S(1)} collective-permute-done((f32[8,256]{1,0:T(8,128)S(1)}, f32[8,256]{1,0:T(8,128)S(1)}, u32[]{:S(2)}, u32[]{:S(2)}) %collective-permute-start.10) | collective-permute-done | bytes 8224 | tf_op jit(solution)/shard_map/ppermute | solution.py:26
  29.8 0.0 collective-permute-done.8.s1
  29.8 0.9 %collective-permute-done.9.s2 = f32[8,256]{1,0:T(8,128)S(1)} collective-permute-done((f32[8,256]{1,0:T(8,128)S(1)}, f32[8,256]{1,0:T(8,128)S(1)}, u32[]{:S(2)}, u32[]{:S(2)}) %collective-permute-start.9) | collective-permute-done | bytes 8224 | tf_op jit(solution)/shard_map/ppermute | solution.py:26
  30.7 0.3 shard_map.60
  31.0 0.1 collective-permute-start.11
  31.1 0.5 shard_map.63
  31.5 0.5 %collective-permute-start.13 = (bf16[64,1024]{1,0:T(8,128)(2,1)S(1)}, bf16[64,1024]{1,0:T(8,128)(2,1)S(1)}, u32[]{:S(2)}, u32[]{:S(2)}) collective-permute-start(bf16[64,1024]{1,0:T(8,128)(2,1)S(1)} %get-tuple-element.38), channel_id=1, source_target_pairs={{0,8},{8,0},{16,24},{24,16},{1,9},{9,1},{17,25},{25,17},{2,10},{10... | collective-permute-start | bytes 393224 | tf_op jit(solution)/shard_map/ppermute | solution.py:26
  32.0 0.0 collective-permute-done.12.q_other
  32.0 0.4 collective-permute-done.11.w_in
  32.4 0.4 shard_map.62
  32.9 1.6 %collective-permute-start.16 = (bf16[520,128]{1,0:T(8,128)(2,1)S(1)}, bf16[520,128]{1,0:T(8,128)(2,1)S(1)}, u32[]{:S(2)}, u32[]{:S(2)}) collective-permute-start(bf16[520,128]{1,0:T(8,128)(2,1)S(1)} %get-tuple-element.41), channel_id=1, source_target_pairs={{0,2},{2,0},{4,6},{6,4},{1,3},{3,1},{5,7},{7,5},{8,10},{10,8},{12,... | collective-permute-start | bytes 399368 | tf_op jit(solution)/shard_map/ppermute | solution.py:26
  34.4 1.5 %collective-permute-start.17 = (bf16[520,128]{1,0:T(8,128)(2,1)S(1)}, bf16[520,128]{1,0:T(8,128)(2,1)S(1)}, u32[]{:S(2)}, u32[]{:S(2)}) collective-permute-start(bf16[520,128]{1,0:T(8,128)(2,1)S(1)} %get-tuple-element.42), channel_id=1, source_target_pairs={{0,4},{2,6},{4,0},{6,2},{1,5},{3,7},{5,1},{7,3},{8,12},{10,14},{12... | collective-permute-start | bytes 399368 | tf_op jit(solution)/shard_map/ppermute | solution.py:26
  36.0 0.5 collective-permute-start.18
  36.4 2.6 %collective-permute-start.14 = (bf16[64,1024]{1,0:T(8,128)(2,1)S(1)}, bf16[64,1024]{1,0:T(8,128)(2,1)S(1)}, u32[]{:S(2)}, u32[]{:S(2)}) collective-permute-start(bf16[64,1024]{1,0:T(8,128)(2,1)S(1)} %get-tuple-element.39), channel_id=1, source_target_pairs={{0,16},{8,24},{16,0},{24,8},{1,17},{9,25},{17,1},{25,9},{2,18},{10... | collective-permute-start | bytes 393224 | tf_op jit(solution)/shard_map/ppermute | solution.py:26
  39.1 0.0 collective-permute-done.13.refs_0_
  39.1 0.9 %collective-permute-start.15 = (bf16[64,1024]{1,0:T(8,128)(2,1)S(1)}, bf16[64,1024]{1,0:T(8,128)(2,1)S(1)}, u32[]{:S(2)}, u32[]{:S(2)}) collective-permute-start(bf16[64,1024]{1,0:T(8,128)(2,1)S(1)} %get-tuple-element.40), channel_id=1, source_target_pairs={{0,24},{8,16},{16,8},{24,0},{1,25},{9,17},{17,9},{25,1},{2,26},{10... | collective-permute-start | bytes 393224 | tf_op jit(solution)/shard_map/ppermute | solution.py:26
  40.0 0.3 shard_map.61.own_query
  40.4 8.1 %collective-permute-done.14.refs_1_ = bf16[64,1024]{1,0:T(8,128)(2,1)S(1)} collective-permute-done((bf16[64,1024]{1,0:T(8,128)(2,1)S(1)}, bf16[64,1024]{1,0:T(8,128)(2,1)S(1)}, u32[]{:S(2)}, u32[]{:S(2)}) %collective-permute-start.14) | collective-permute-done | bytes 131104 | tf_op jit(solution)/shard_map/ppermute | solution.py:26
  48.5 0.0 collective-permute-done.15.refs_2_
  48.5 0.0 collective-permute-done.16.refs_3_
  48.5 0.0 collective-permute-done.17.refs_4_
  48.5 0.0 collective-permute-done.18.refs_5_
  48.5 0.9 %shard_map.64 = (bf16[64,1024]{1,0:T(8,128)(2,1)}, bf16[64,1024]{1,0:T(8,128)(2,1)}, f32[1,128]{1,0:T(1,128)}) custom-call(f32[64,1024]{1,0:T(8,128)S(1)} %shard_map.61.own_query, f32[64,8]{1,0:T(8,128)S(1)} %get-tuple-element.34.gains, f32[64,1024]{1,0:T(8,128)S(1)} %get-tuple-element.36.own, f32[8,128]{1,0:T(8,128)S(1)} %get-tuple-element.37.chip_loss, ...), custom_call_target="tpu_custom_call" | custom-call | tf_op jit(solution)/shard_map/pallas_call | solution.py:56
  (11 shorter events, 0.1 us)
Async XLA Ops:
  0.6 13.1 %collective-permute-start = (bf16[64,1024]{1,0:T(8,128)(2,1)}, bf16[64,1024]{1,0:T(8,128)(2,1)S(1)}, u32[]{:S(2)}, u32[]{:S(2)}) collective-permute-start(bf16[64,1024]{1,0:T(8,128)(2,1)} %documents.1), channel_id=1, source_target_pairs={{0,6},{2,4},{4,2},{6,0},{1,7},{3,5},{5,3},{7,1},{8,14},{10,12},{12... | collective-permute-start | bytes 393224 | tf_op jit(solution)/shard_map/ppermute | solution.py:26
  4.6 10.0 %collective-permute-start.1 = (bf16[64,1024]{1,0:T(8,128)(2,1)}, bf16[64,1024]{1,0:T(8,128)(2,1)S(1)}, u32[]{:S(2)}, u32[]{:S(2)}) collective-permute-start(bf16[64,1024]{1,0:T(8,128)(2,1)} %documents.1), channel_id=1, source_target_pairs={{0,4},{2,6},{4,0},{6,2},{1,5},{3,7},{5,1},{7,3},{8,12},{10,14},{12... | collective-permute-start | bytes 393224 | tf_op jit(solution)/shard_map/ppermute | solution.py:26
  5.1 16.5 %collective-permute-start.2 = (bf16[64,1024]{1,0:T(8,128)(2,1)}, bf16[64,1024]{1,0:T(8,128)(2,1)S(1)}, u32[]{:S(2)}, u32[]{:S(2)}) collective-permute-start(bf16[64,1024]{1,0:T(8,128)(2,1)} %documents.1), channel_id=1, source_target_pairs={{0,2},{2,0},{4,6},{6,4},{1,3},{3,1},{5,7},{7,5},{8,10},{10,8},{12,... | collective-permute-start | bytes 393224 | tf_op jit(solution)/shard_map/ppermute | solution.py:26
  5.3 9.5 %collective-permute-start.5 = (bf16[64,1024]{1,0:T(8,128)(2,1)}, bf16[64,1024]{1,0:T(8,128)(2,1)S(1)}, u32[]{:S(2)}, u32[]{:S(2)}) collective-permute-start(bf16[64,1024]{1,0:T(8,128)(2,1)} %queries.1), channel_id=1, source_target_pairs={{0,8},{8,0},{16,24},{24,16},{1,9},{9,1},{17,25},{25,17},{2,10},{10... | collective-permute-start | bytes 393224 | tf_op jit(solution)/shard_map/ppermute | solution.py:26
  7.2 8.1 %collective-permute-start.6 = (bf16[64,1024]{1,0:T(8,128)(2,1)}, bf16[64,1024]{1,0:T(8,128)(2,1)S(1)}, u32[]{:S(2)}, u32[]{:S(2)}) collective-permute-start(bf16[64,1024]{1,0:T(8,128)(2,1)} %queries.1), channel_id=1, source_target_pairs={{0,16},{8,24},{16,0},{24,8},{1,17},{9,25},{17,1},{25,9},{2,18},{10... | collective-permute-start | bytes 393224 | tf_op jit(solution)/shard_map/ppermute | solution.py:26
  9.8 0.9 %copy-start = (bf16[64,1024]{1,0:T(8,128)(2,1)S(1)}, bf16[64,1024]{1,0:T(8,128)(2,1)}, u32[]{:S(2)}) copy-start(bf16[64,1024]{1,0:T(8,128)(2,1)} %queries.1) | copy-start | bytes 393220
  10.8 0.9 %copy-start.2 = (bf16[64,1024]{1,0:T(8,128)(2,1)S(1)}, bf16[64,1024]{1,0:T(8,128)(2,1)}, u32[]{:S(2)}) copy-start(bf16[64,1024]{1,0:T(8,128)(2,1)} %documents.1) | copy-start | bytes 393220
  11.7 0.7 %copy-start.3 = (s32[2048]{0:T(1024)S(1)}, s32[2048]{0:T(1024)}, u32[]{:S(2)}) copy-start(s32[2048]{0:T(1024)} %param.5) | copy-start | bytes 24580
  13.7 0.9 %copy-start.1 = (bf16[64,1024]{1,0:T(8,128)(2,1)S(1)}, bf16[64,1024]{1,0:T(8,128)(2,1)}, u32[]{:S(2)}) copy-start(bf16[64,1024]{1,0:T(8,128)(2,1)} %queries.1) | copy-start | bytes 393220
  14.6 6.9 %collective-permute-start.7 = (bf16[64,1024]{1,0:T(8,128)(2,1)S(1)}, bf16[64,1024]{1,0:T(8,128)(2,1)S(1)}, u32[]{:S(2)}, u32[]{:S(2)}) collective-permute-start(bf16[64,1024]{1,0:T(8,128)(2,1)S(1)} %copy-done.1), channel_id=1, source_target_pairs={{0,24},{8,16},{16,8},{24,0},{1,25},{9,17},{17,9},{25,1},{2,26},{10... | collective-permute-start | bytes 393224 | tf_op jit(solution)/shard_map/ppermute | solution.py:26
  14.7 7.5 %collective-permute-start.3 = (bf16[192,1024]{1,0:T(8,128)(2,1)S(1)}, bf16[192,1024]{1,0:T(8,128)(2,1)S(1)}, u32[]{:S(2)}, u32[]{:S(2)}) collective-permute-start(bf16[192,1024]{1,0:T(8,128)(2,1)S(1)} %pad_maximum_fusion), channel_id=1, source_target_pairs={{0,1},{1,0},{2,3},{3,2},{4,5},{5,4},{6,7},{7,6},{8,9},{9,8},{10,11... | collective-permute-start | bytes 1179656 | tf_op jit(solution)/shard_map/ppermute | solution.py:35
  21.5 10.5 %collective-permute-start.12 = (bf16[256,1024]{1,0:T(8,128)(2,1)S(1)}, bf16[256,1024]{1,0:T(8,128)(2,1)S(1)}, u32[]{:S(2)}, u32[]{:S(2)}) collective-permute-start(bf16[256,1024]{1,0:T(8,128)(2,1)S(1)} %constant_dynamic-update-slice_fusion.6.queries.q_mine), channel_id=1, source_target_pairs={{0,1},{1,0},{2,3},{3,2},{4,5},{5,4},{6,7},{7,6},{8,9},{9,8},{10,11... | collective-permute-start | bytes 1572872 | tf_op jit(solution)/shard_map/ppermute | solution.py:35
  21.7 2.0 %collective-permute-start.4 = (bf16[64,1024]{1,0:T(8,128)(2,1)S(1)}, bf16[64,1024]{1,0:T(8,128)(2,1)S(1)}, u32[]{:S(2)}, u32[]{:S(2)}) collective-permute-start(bf16[64,1024]{1,0:T(8,128)(2,1)S(1)} %collective-permute-done.2), channel_id=1, source_target_pairs={{0,1},{1,0},{2,3},{3,2},{4,5},{5,4},{6,7},{7,6},{8,9},{9,8},{10,11... | collective-permute-start | bytes 393224 | tf_op jit(solution)/shard_map/ppermute | solution.py:35
  24.3 5.5 %collective-permute-start.10 = (f32[8,256]{1,0:T(8,128)S(1)}, f32[8,256]{1,0:T(8,128)S(1)}, u32[]{:S(2)}, u32[]{:S(2)}) collective-permute-start(f32[8,256]{1,0:T(8,128)S(1)} %get-tuple-element.29.s0.stats), channel_id=1, source_target_pairs={{0,24},{8,16},{16,8},{24,0},{1,25},{9,17},{17,9},{25,1},{2,26},{10... | collective-permute-start | bytes 24584 | tf_op jit(solution)/shard_map/ppermute | solution.py:26
  24.5 5.3 %collective-permute-start.8 = (f32[8,256]{1,0:T(8,128)S(1)}, f32[8,256]{1,0:T(8,128)S(1)}, u32[]{:S(2)}, u32[]{:S(2)}) collective-permute-start(f32[8,256]{1,0:T(8,128)S(1)} %get-tuple-element.29.s0.stats), channel_id=1, source_target_pairs={{0,8},{8,0},{16,24},{24,16},{1,9},{9,1},{17,25},{25,17},{2,10},{10... | collective-permute-start | bytes 24584 | tf_op jit(solution)/shard_map/ppermute | solution.py:26
  26.1 4.5 %collective-permute-start.9 = (f32[8,256]{1,0:T(8,128)S(1)}, f32[8,256]{1,0:T(8,128)S(1)}, u32[]{:S(2)}, u32[]{:S(2)}) collective-permute-start(f32[8,256]{1,0:T(8,128)S(1)} %get-tuple-element.29.s0.stats), channel_id=1, source_target_pairs={{0,16},{8,24},{16,0},{24,8},{1,17},{9,25},{17,1},{25,9},{2,18},{10... | collective-permute-start | bytes 24584 | tf_op jit(solution)/shard_map/ppermute | solution.py:26
  31.0 1.4 %collective-permute-start.11 = (bf16[264,256]{1,0:T(8,128)(2,1)S(1)}, bf16[264,256]{1,0:T(8,128)(2,1)S(1)}, u32[]{:S(2)}, u32[]{:S(2)}) collective-permute-start(bf16[264,256]{1,0:T(8,128)(2,1)S(1)} %get-tuple-element.33.w_send), channel_id=1, source_target_pairs={{0,1},{1,0},{2,3},{3,2},{4,5},{5,4},{6,7},{7,6},{8,9},{9,8},{10,11... | collective-permute-start | bytes 405512 | tf_op jit(solution)/shard_map/ppermute | solution.py:35
  31.5 7.5 %collective-permute-start.13 = (bf16[64,1024]{1,0:T(8,128)(2,1)S(1)}, bf16[64,1024]{1,0:T(8,128)(2,1)S(1)}, u32[]{:S(2)}, u32[]{:S(2)}) collective-permute-start(bf16[64,1024]{1,0:T(8,128)(2,1)S(1)} %get-tuple-element.38), channel_id=1, source_target_pairs={{0,8},{8,0},{16,24},{24,16},{1,9},{9,1},{17,25},{25,17},{2,10},{10... | collective-permute-start | bytes 393224 | tf_op jit(solution)/shard_map/ppermute | solution.py:26
  32.9 15.6 %collective-permute-start.16 = (bf16[520,128]{1,0:T(8,128)(2,1)S(1)}, bf16[520,128]{1,0:T(8,128)(2,1)S(1)}, u32[]{:S(2)}, u32[]{:S(2)}) collective-permute-start(bf16[520,128]{1,0:T(8,128)(2,1)S(1)} %get-tuple-element.41), channel_id=1, source_target_pairs={{0,2},{2,0},{4,6},{6,4},{1,3},{3,1},{5,7},{7,5},{8,10},{10,8},{12,... | collective-permute-start | bytes 399368 | tf_op jit(solution)/shard_map/ppermute | solution.py:26
  34.4 14.0 %collective-permute-start.17 = (bf16[520,128]{1,0:T(8,128)(2,1)S(1)}, bf16[520,128]{1,0:T(8,128)(2,1)S(1)}, u32[]{:S(2)}, u32[]{:S(2)}) collective-permute-start(bf16[520,128]{1,0:T(8,128)(2,1)S(1)} %get-tuple-element.42), channel_id=1, source_target_pairs={{0,4},{2,6},{4,0},{6,2},{1,5},{3,7},{5,1},{7,3},{8,12},{10,14},{12... | collective-permute-start | bytes 399368 | tf_op jit(solution)/shard_map/ppermute | solution.py:26
  36.0 12.5 %collective-permute-start.18 = (bf16[520,128]{1,0:T(8,128)(2,1)S(1)}, bf16[520,128]{1,0:T(8,128)(2,1)S(1)}, u32[]{:S(2)}, u32[]{:S(2)}) collective-permute-start(bf16[520,128]{1,0:T(8,128)(2,1)S(1)} %get-tuple-element.43), channel_id=1, source_target_pairs={{0,6},{2,4},{4,2},{6,0},{1,7},{3,5},{5,3},{7,1},{8,14},{10,12},{12... | collective-permute-start | bytes 399368 | tf_op jit(solution)/shard_map/ppermute | solution.py:26
  36.4 12.0 %collective-permute-start.14 = (bf16[64,1024]{1,0:T(8,128)(2,1)S(1)}, bf16[64,1024]{1,0:T(8,128)(2,1)S(1)}, u32[]{:S(2)}, u32[]{:S(2)}) collective-permute-start(bf16[64,1024]{1,0:T(8,128)(2,1)S(1)} %get-tuple-element.39), channel_id=1, source_target_pairs={{0,16},{8,24},{16,0},{24,8},{1,17},{9,25},{17,1},{25,9},{2,18},{10... | collective-permute-start | bytes 393224 | tf_op jit(solution)/shard_map/ppermute | solution.py:26
  39.1 9.4 %collective-permute-start.15 = (bf16[64,1024]{1,0:T(8,128)(2,1)S(1)}, bf16[64,1024]{1,0:T(8,128)(2,1)S(1)}, u32[]{:S(2)}, u32[]{:S(2)}) collective-permute-start(bf16[64,1024]{1,0:T(8,128)(2,1)S(1)} %get-tuple-element.40), channel_id=1, source_target_pairs={{0,24},{8,16},{16,8},{24,0},{1,25},{9,17},{17,9},{25,1},{2,26},{10... | collective-permute-start | bytes 393224 | tf_op jit(solution)/shard_map/ppermute | solution.py:26

commit v5 on v4

--- a/solution.py
+++ b/solution.py
@@ -147,30 +147,29 @@
     return (high.astype(F32) + middle.astype(F32)) + low.astype(F32)
 
 
-def score_kernel(scale, rows, docs, queries, positive, scores, stats):
+def score_kernel(scale, rows, docs, queries, positive, scores, stats, run):
     count = docs.shape[0]
     cols = queries.shape[0]
-    peak = jnp.full((1, cols), -jnp.inf, F32)
-    pos = jnp.zeros((1, rows), F32)
-    stats[...] = jnp.zeros(stats.shape, F32)
-    stats[0:1, :cols] = peak
+    run[...] = jnp.zeros(run.shape, F32)
+    run[0:1, :] = jnp.full((1, cols), -jnp.inf, F32)
     queries_now = queries[...]
 
     def first(at):
         part = contract(docs[pl.ds(at, CHUNK), :], queries_now, 1, 1) * scale
         scores[pl.ds(at, CHUNK), :] = part
-        stats[0:1, :cols] = jnp.maximum(stats[0:1, :cols], jnp.max(part, 0, keepdims=True))
+        run[0:1, :] = jnp.maximum(run[0:1, :], jnp.max(part, 0, keepdims=True))
         chosen = jnp.where(positive[pl.ds(at, CHUNK), :] > 0.0, part[:, :rows], 0.0)
-        stats[1:2, :rows] += jnp.sum(chosen, 0, keepdims=True)
+        run[1:2, :rows] += jnp.sum(chosen, 0, keepdims=True)
 
     each_chunk(count, first)
-    peak = stats[0:1, :cols]
+    peak = run[0:1, :]
 
     def second(at):
-        stats[2:3, :cols] += jnp.sum(jnp.exp(scores[pl.ds(at, CHUNK), :] - peak), 0, keepdims=True)
+        run[2:3, :] += jnp.sum(jnp.exp(scores[pl.ds(at, CHUNK), :] - peak), 0, keepdims=True)
 
     each_chunk(count, second)
-    stats[0:1, :cols] = peak + jnp.log(stats[2:3, :cols])
+    stats[:, :cols] = peak + jnp.log(run[2:3, :])
+    stats[:, cols:] = jnp.broadcast_to(jnp.sum(run[1:2, :rows], 1, keepdims=True), (1, LANES))
 
 
 def share_kernel(scale, rows, scores, stats, docs, *outs):
@@ -222,7 +221,7 @@
     terms = row_counts * log_denom
     line = tree_sum(
         [
-            jnp.sum(terms[:, k * rows : (k + 1) * rows] - stats[k][1:2, :rows], 1, keepdims=True)
+            jnp.sum(terms[:, k * rows : (k + 1) * rows], 1, keepdims=True) - stats[k][:, cols : cols + 1]
             for k in range(rest)
         ]
     )
@@ -322,10 +321,11 @@
 
     scores, stats = call(
         functools.partial(score_kernel, scale, rows),
-        [((2 * half, cols), F32), ((8, cols), F32)],
+        [((2 * half, cols), F32), ((1, cols + LANES), F32)],
         docs,
         q_mine,
         positive,
+        scratch=[pltpu.VMEM((8, cols), F32)],
     )
     stats_all = send_pieces([stats] * quarters, "quarter")
     q_other = swap_cores(q_mine)

time: 50 us -> 49.9 us (level)
  no operation moved by 1% of the time
where the time goes in v5:
time: 49.9 us; the launch traced here: 49.3 us
  starting transfers between devices  22 us (44%)
  waiting for transfers between devices  18.5 us (37%)
  Pallas kernels  4.42 us (9%)
  local copies, waits for them, and re-layouts  3.53 us (7%)
  between operations  0.82 us (2%)
    ppermute x15, starting transfers between devices, send_pieces(): out[k] = lax.ppermute(pieces[k], axes, [(i, i ^ k) for i in range(count)])  21.3 us
    ppermute x15, waiting for transfers between devices, send_pieces(): out[k] = lax.ppermute(pieces[k], axes, [(i, i ^ k) for i in range(count)])  16.7 us
    pallas_call x7, Pallas kernels, call(): pl.pallas_call(kernel, out_shape=[jax.ShapeDtypeStruct(shape, dtype) for...  4.42 us
    unnamed x16, local copies, waits for them, and re-layouts  3.51 us
    ppermute x4, waiting for transfers between devices, swap_cores(): return lax.ppermute(array, 'core', [(0, 1), (1, 0)])  1.81 us
  transfers between devices with their start and end apart: 19, of which 7 were waited for; matrix products, arithmetic and copies ran while one was open for 0% of the time, Pallas kernels for 7%

profile of v5, /device:TPU:0, one launch (start us, length us, event | category | flops | bytes accessed | tf_op | source)
XLA Modules:
  0.0 49.3 jit_solution(8951523934036988211)
XLA Ops:
  0.6 4.0 %collective-permute-start = (bf16[64,1024]{1,0:T(8,128)(2,1)}, bf16[64,1024]{1,0:T(8,128)(2,1)S(1)}, u32[]{:S(2)}, u32[]{:S(2)}) collective-permute-start(bf16[64,1024]{1,0:T(8,128)(2,1)} %documents.1), channel_id=1, source_target_pairs={{0,6},{2,4},{4,2},{6,0},{1,7},{3,5},{5,3},{7,1},{8,14},{10,12},{12... | collective-permute-start | bytes 393224 | tf_op jit(solution)/shard_map/ppermute | solution.py:26
  4.6 0.5 %collective-permute-start.1 = (bf16[64,1024]{1,0:T(8,128)(2,1)}, bf16[64,1024]{1,0:T(8,128)(2,1)S(1)}, u32[]{:S(2)}, u32[]{:S(2)}) collective-permute-start(bf16[64,1024]{1,0:T(8,128)(2,1)} %documents.1), channel_id=1, source_target_pairs={{0,4},{2,6},{4,0},{6,2},{1,5},{3,7},{5,1},{7,3},{8,12},{10,14},{12... | collective-permute-start | bytes 393224 | tf_op jit(solution)/shard_map/ppermute | solution.py:26
  5.1 0.1 collective-permute-start.2
  5.3 2.0 %collective-permute-start.5 = (bf16[64,1024]{1,0:T(8,128)(2,1)}, bf16[64,1024]{1,0:T(8,128)(2,1)S(1)}, u32[]{:S(2)}, u32[]{:S(2)}) collective-permute-start(bf16[64,1024]{1,0:T(8,128)(2,1)} %queries.1), channel_id=1, source_target_pairs={{0,8},{8,0},{16,24},{24,16},{1,9},{9,1},{17,25},{25,17},{2,10},{10... | collective-permute-start | bytes 393224 | tf_op jit(solution)/shard_map/ppermute | solution.py:26
  7.2 2.6 %collective-permute-start.6 = (bf16[64,1024]{1,0:T(8,128)(2,1)}, bf16[64,1024]{1,0:T(8,128)(2,1)S(1)}, u32[]{:S(2)}, u32[]{:S(2)}) collective-permute-start(bf16[64,1024]{1,0:T(8,128)(2,1)} %queries.1), channel_id=1, source_target_pairs={{0,16},{8,24},{16,0},{24,8},{1,17},{9,25},{17,1},{25,9},{2,18},{10... | collective-permute-start | bytes 393224 | tf_op jit(solution)/shard_map/ppermute | solution.py:26
  9.8 0.0 copy-start
  9.8 0.9 %copy-done = bf16[64,1024]{1,0:T(8,128)(2,1)S(1)} copy-done((bf16[64,1024]{1,0:T(8,128)(2,1)S(1)}, bf16[64,1024]{1,0:T(8,128)(2,1)}, u32[]{:S(2)}) %copy-start) | copy-done | bytes 131096
  10.8 0.0 copy-start.2
  10.8 0.9 %copy-done.2 = bf16[64,1024]{1,0:T(8,128)(2,1)S(1)} copy-done((bf16[64,1024]{1,0:T(8,128)(2,1)S(1)}, bf16[64,1024]{1,0:T(8,128)(2,1)}, u32[]{:S(2)}) %copy-start.2) | copy-done | bytes 131096
  11.7 0.0 copy-start.3
  11.7 0.7 %copy-done.3 = s32[2048]{0:T(1024)S(1)} copy-done((s32[2048]{0:T(1024)S(1)}, s32[2048]{0:T(1024)}, u32[]{:S(2)}) %copy-start.3) | copy-done | bytes 8216
  12.4 1.3 %shard_map.58 = (f32[1,256]{1,0:T(1,128)S(1)}, f32[8,256]{1,0:T(8,128)S(1)}, f32[512,64]{1,0:T(8,128)S(1)}, bf16[64,1024]{1,0:T(8,128)(2,1)S(1)}, bf16[64,1024]{1,0:T(8,128)(2,1)S(1)}) custom-call(s32[16,128]{1,0:T(8,128)S(1)} %bitcast.3, bf16[64,1024]{1,0:T(8,128)(2,1)S(1)} %copy-done, bf16[64,1024]{1,0:T(8,128)(2,1)S(1)} %copy-done.2), custom_call_target="tpu_custom_call" | custom-call | tf_op jit(solution)/shard_map/pallas_call | solution.py:56
  13.7 0.0 copy-start.1
  13.8 0.0 collective-permute-done
  13.8 0.9 %copy-done.1 = bf16[64,1024]{1,0:T(8,128)(2,1)S(1)} copy-done((bf16[64,1024]{1,0:T(8,128)(2,1)S(1)}, bf16[64,1024]{1,0:T(8,128)(2,1)}, u32[]{:S(2)}) %copy-start.1) | copy-done | bytes 131096
  14.6 0.0 collective-permute-start.7
  14.6 0.0 collective-permute-done.1
  14.7 0.1 collective-permute-start.3
  14.8 0.0 collective-permute-done.5
  14.8 0.5 %collective-permute-done.6 = bf16[64,1024]{1,0:T(8,128)(2,1)S(1)} collective-permute-done((bf16[64,1024]{1,0:T(8,128)(2,1)}, bf16[64,1024]{1,0:T(8,128)(2,1)S(1)}, u32[]{:S(2)}, u32[]{:S(2)}) %collective-permute-start.6) | collective-permute-done | bytes 131104 | tf_op jit(solution)/shard_map/ppermute | solution.py:26
  15.4 6.2 %collective-permute-done.7 = bf16[64,1024]{1,0:T(8,128)(2,1)S(1)} collective-permute-done((bf16[64,1024]{1,0:T(8,128)(2,1)S(1)}, bf16[64,1024]{1,0:T(8,128)(2,1)S(1)}, u32[]{:S(2)}, u32[]{:S(2)}) %collective-permute-start.7) | collective-permute-done | bytes 131104 | tf_op jit(solution)/shard_map/ppermute | solution.py:26
  21.5 0.1 collective-permute-start.12
  21.6 0.0 collective-permute-done.2
  21.7 0.6 %collective-permute-start.4 = (bf16[64,1024]{1,0:T(8,128)(2,1)S(1)}, bf16[64,1024]{1,0:T(8,128)(2,1)S(1)}, u32[]{:S(2)}, u32[]{:S(2)}) collective-permute-start(bf16[64,1024]{1,0:T(8,128)(2,1)S(1)} %collective-permute-done.2), channel_id=1, source_target_pairs={{0,1},{1,0},{2,3},{3,2},{4,5},{5,4},{6,7},{7,6},{8,9},{9,8},{10,11... | collective-permute-start | bytes 393224 | tf_op jit(solution)/shard_map/ppermute | solution.py:35
  22.2 0.0 collective-permute-done.3
  22.3 1.4 %collective-permute-done.4 = bf16[64,1024]{1,0:T(8,128)(2,1)S(1)} collective-permute-done((bf16[64,1024]{1,0:T(8,128)(2,1)S(1)}, bf16[64,1024]{1,0:T(8,128)(2,1)S(1)}, u32[]{:S(2)}, u32[]{:S(2)}) %collective-permute-start.4) | collective-permute-done | bytes 131104 | tf_op jit(solution)/shard_map/ppermute | solution.py:35
  23.7 0.6 %shard_map.59 = (f32[512,256]{1,0:T(8,128)S(1)}, f32[1,384]{1,0:T(1,128)S(1)}) custom-call(bf16[512,1024]{1,0:T(8,128)(2,1)S(1)} %constant_dynamic-update-slice_fusion.docs, bf16[256,1024]{1,0:T(8,128)(2,1)S(1)} %constant_dynamic-update-slice_fusion.6.queries.q_mine, f32[512,64]{1,0:T(8,128)S(1)} %get-tuple-element.27.positive), custom_call_target="tpu_custom_call" | custom-call | tf_op jit(solution)/shard_map/pallas_call | solution.py:56
  24.3 0.2 collective-permute-start.10
  24.5 1.6 %collective-permute-start.8 = (f32[1,384]{1,0:T(1,128)S(1)}, f32[1,384]{1,0:T(1,128)S(1)}, u32[]{:S(2)}, u32[]{:S(2)}) collective-permute-start(f32[1,384]{1,0:T(1,128)S(1)} %get-tuple-element.29.s0.stats), channel_id=1, source_target_pairs={{0,8},{8,0},{16,24},{24,16},{1,9},{9,1},{17,25},{25,17},{2,10},{10... | collective-permute-start | bytes 4616 | tf_op jit(solution)/shard_map/ppermute | solution.py:26
  26.1 2.6 %collective-permute-start.9 = (f32[1,384]{1,0:T(1,128)S(1)}, f32[1,384]{1,0:T(1,128)S(1)}, u32[]{:S(2)}, u32[]{:S(2)}) collective-permute-start(f32[1,384]{1,0:T(1,128)S(1)} %get-tuple-element.29.s0.stats), channel_id=1, source_target_pairs={{0,16},{8,24},{16,0},{24,8},{1,17},{9,25},{17,1},{25,9},{2,18},{10... | collective-permute-start | bytes 4616 | tf_op jit(solution)/shard_map/ppermute | solution.py:26
  28.8 1.0 %collective-permute-done.10.s3 = f32[1,384]{1,0:T(1,128)S(1)} collective-permute-done((f32[1,384]{1,0:T(1,128)S(1)}, f32[1,384]{1,0:T(1,128)S(1)}, u32[]{:S(2)}, u32[]{:S(2)}) %collective-permute-start.10) | collective-permute-done | bytes 1568 | tf_op jit(solution)/shard_map/ppermute | solution.py:26
  29.7 0.0 collective-permute-done.8.s1
  29.8 0.9 %collective-permute-done.9.s2 = f32[1,384]{1,0:T(1,128)S(1)} collective-permute-done((f32[1,384]{1,0:T(1,128)S(1)}, f32[1,384]{1,0:T(1,128)S(1)}, u32[]{:S(2)}, u32[]{:S(2)}) %collective-permute-start.9) | collective-permute-done | bytes 1568 | tf_op jit(solution)/shard_map/ppermute | solution.py:26
  30.6 0.4 shard_map.60
  31.0 0.1 collective-permute-start.11
  31.0 0.4 shard_map.63
  31.5 0.5 %collective-permute-start.13 = (bf16[64,1024]{1,0:T(8,128)(2,1)S(1)}, bf16[64,1024]{1,0:T(8,128)(2,1)S(1)}, u32[]{:S(2)}, u32[]{:S(2)}) collective-permute-start(bf16[64,1024]{1,0:T(8,128)(2,1)S(1)} %get-tuple-element.38), channel_id=1, source_target_pairs={{0,8},{8,0},{16,24},{24,16},{1,9},{9,1},{17,25},{25,17},{2,10},{10... | collective-permute-start | bytes 393224 | tf_op jit(solution)/shard_map/ppermute | solution.py:26
  32.0 0.0 collective-permute-done.12.q_other
  32.0 0.4 collective-permute-done.11.w_in
  32.4 0.4 shard_map.62
  32.8 1.5 %collective-permute-start.16 = (bf16[520,128]{1,0:T(8,128)(2,1)S(1)}, bf16[520,128]{1,0:T(8,128)(2,1)S(1)}, u32[]{:S(2)}, u32[]{:S(2)}) collective-permute-start(bf16[520,128]{1,0:T(8,128)(2,1)S(1)} %get-tuple-element.41), channel_id=1, source_target_pairs={{0,2},{2,0},{4,6},{6,4},{1,3},{3,1},{5,7},{7,5},{8,10},{10,8},{12,... | collective-permute-start | bytes 399368 | tf_op jit(solution)/shard_map/ppermute | solution.py:26
  34.4 1.5 %collective-permute-start.17 = (bf16[520,128]{1,0:T(8,128)(2,1)S(1)}, bf16[520,128]{1,0:T(8,128)(2,1)S(1)}, u32[]{:S(2)}, u32[]{:S(2)}) collective-permute-start(bf16[520,128]{1,0:T(8,128)(2,1)S(1)} %get-tuple-element.42), channel_id=1, source_target_pairs={{0,4},{2,6},{4,0},{6,2},{1,5},{3,7},{5,1},{7,3},{8,12},{10,14},{12... | collective-permute-start | bytes 399368 | tf_op jit(solution)/shard_map/ppermute | solution.py:26
  35.9 0.5 collective-permute-start.18
  36.4 2.6 %collective-permute-start.14 = (bf16[64,1024]{1,0:T(8,128)(2,1)S(1)}, bf16[64,1024]{1,0:T(8,128)(2,1)S(1)}, u32[]{:S(2)}, u32[]{:S(2)}) collective-permute-start(bf16[64,1024]{1,0:T(8,128)(2,1)S(1)} %get-tuple-element.39), channel_id=1, source_target_pairs={{0,16},{8,24},{16,0},{24,8},{1,17},{9,25},{17,1},{25,9},{2,18},{10... | collective-permute-start | bytes 393224 | tf_op jit(solution)/shard_map/ppermute | solution.py:26
  39.0 0.0 collective-permute-done.13.refs_0_
  39.0 0.9 %collective-permute-start.15 = (bf16[64,1024]{1,0:T(8,128)(2,1)S(1)}, bf16[64,1024]{1,0:T(8,128)(2,1)S(1)}, u32[]{:S(2)}, u32[]{:S(2)}) collective-permute-start(bf16[64,1024]{1,0:T(8,128)(2,1)S(1)} %get-tuple-element.40), channel_id=1, source_target_pairs={{0,24},{8,16},{16,8},{24,0},{1,25},{9,17},{17,9},{25,1},{2,26},{10... | collective-permute-start | bytes 393224 | tf_op jit(solution)/shard_map/ppermute | solution.py:26
  39.9 0.3 shard_map.61.own_query
  40.3 8.1 %collective-permute-done.14.refs_1_ = bf16[64,1024]{1,0:T(8,128)(2,1)S(1)} collective-permute-done((bf16[64,1024]{1,0:T(8,128)(2,1)S(1)}, bf16[64,1024]{1,0:T(8,128)(2,1)S(1)}, u32[]{:S(2)}, u32[]{:S(2)}) %collective-permute-start.14) | collective-permute-done | bytes 131104 | tf_op jit(solution)/shard_map/ppermute | solution.py:26
  48.4 0.0 collective-permute-done.15.refs_2_
  48.4 0.0 collective-permute-done.16.refs_3_
  48.4 0.0 collective-permute-done.17.refs_4_
  48.4 0.0 collective-permute-done.18.refs_5_
  48.4 0.9 %shard_map.64 = (bf16[64,1024]{1,0:T(8,128)(2,1)}, bf16[64,1024]{1,0:T(8,128)(2,1)}, f32[1,128]{1,0:T(1,128)}) custom-call(f32[64,1024]{1,0:T(8,128)S(1)} %shard_map.61.own_query, f32[64,8]{1,0:T(8,128)S(1)} %get-tuple-element.34.gains, f32[64,1024]{1,0:T(8,128)S(1)} %get-tuple-element.36.own, f32[8,128]{1,0:T(8,128)S(1)} %get-tuple-element.37.chip_loss, ...), custom_call_target="tpu_custom_call" | custom-call | tf_op jit(solution)/shard_map/pallas_call | solution.py:56
  (11 shorter events, 0.1 us)
Async XLA Ops:
  0.6 13.1 %collective-permute-start = (bf16[64,1024]{1,0:T(8,128)(2,1)}, bf16[64,1024]{1,0:T(8,128)(2,1)S(1)}, u32[]{:S(2)}, u32[]{:S(2)}) collective-permute-start(bf16[64,1024]{1,0:T(8,128)(2,1)} %documents.1), channel_id=1, source_target_pairs={{0,6},{2,4},{4,2},{6,0},{1,7},{3,5},{5,3},{7,1},{8,14},{10,12},{12... | collective-permute-start | bytes 393224 | tf_op jit(solution)/shard_map/ppermute | solution.py:26
  4.6 10.0 %collective-permute-start.1 = (bf16[64,1024]{1,0:T(8,128)(2,1)}, bf16[64,1024]{1,0:T(8,128)(2,1)S(1)}, u32[]{:S(2)}, u32[]{:S(2)}) collective-permute-start(bf16[64,1024]{1,0:T(8,128)(2,1)} %documents.1), channel_id=1, source_target_pairs={{0,4},{2,6},{4,0},{6,2},{1,5},{3,7},{5,1},{7,3},{8,12},{10,14},{12... | collective-permute-start | bytes 393224 | tf_op jit(solution)/shard_map/ppermute | solution.py:26
  5.1 16.5 %collective-permute-start.2 = (bf16[64,1024]{1,0:T(8,128)(2,1)}, bf16[64,1024]{1,0:T(8,128)(2,1)S(1)}, u32[]{:S(2)}, u32[]{:S(2)}) collective-permute-start(bf16[64,1024]{1,0:T(8,128)(2,1)} %documents.1), channel_id=1, source_target_pairs={{0,2},{2,0},{4,6},{6,4},{1,3},{3,1},{5,7},{7,5},{8,10},{10,8},{12,... | collective-permute-start | bytes 393224 | tf_op jit(solution)/shard_map/ppermute | solution.py:26
  5.3 9.5 %collective-permute-start.5 = (bf16[64,1024]{1,0:T(8,128)(2,1)}, bf16[64,1024]{1,0:T(8,128)(2,1)S(1)}, u32[]{:S(2)}, u32[]{:S(2)}) collective-permute-start(bf16[64,1024]{1,0:T(8,128)(2,1)} %queries.1), channel_id=1, source_target_pairs={{0,8},{8,0},{16,24},{24,16},{1,9},{9,1},{17,25},{25,17},{2,10},{10... | collective-permute-start | bytes 393224 | tf_op jit(solution)/shard_map/ppermute | solution.py:26
  7.2 8.1 %collective-permute-start.6 = (bf16[64,1024]{1,0:T(8,128)(2,1)}, bf16[64,1024]{1,0:T(8,128)(2,1)S(1)}, u32[]{:S(2)}, u32[]{:S(2)}) collective-permute-start(bf16[64,1024]{1,0:T(8,128)(2,1)} %queries.1), channel_id=1, source_target_pairs={{0,16},{8,24},{16,0},{24,8},{1,17},{9,25},{17,1},{25,9},{2,18},{10... | collective-permute-start | bytes 393224 | tf_op jit(solution)/shard_map/ppermute | solution.py:26
  9.8 0.9 %copy-start = (bf16[64,1024]{1,0:T(8,128)(2,1)S(1)}, bf16[64,1024]{1,0:T(8,128)(2,1)}, u32[]{:S(2)}) copy-start(bf16[64,1024]{1,0:T(8,128)(2,1)} %queries.1) | copy-start | bytes 393220
  10.8 0.9 %copy-start.2 = (bf16[64,1024]{1,0:T(8,128)(2,1)S(1)}, bf16[64,1024]{1,0:T(8,128)(2,1)}, u32[]{:S(2)}) copy-start(bf16[64,1024]{1,0:T(8,128)(2,1)} %documents.1) | copy-start | bytes 393220
  11.7 0.7 %copy-start.3 = (s32[2048]{0:T(1024)S(1)}, s32[2048]{0:T(1024)}, u32[]{:S(2)}) copy-start(s32[2048]{0:T(1024)} %param.5) | copy-start | bytes 24580
  13.7 0.9 %copy-start.1 = (bf16[64,1024]{1,0:T(8,128)(2,1)S(1)}, bf16[64,1024]{1,0:T(8,128)(2,1)}, u32[]{:S(2)}) copy-start(bf16[64,1024]{1,0:T(8,128)(2,1)} %queries.1) | copy-start | bytes 393220
  14.6 6.9 %collective-permute-start.7 = (bf16[64,1024]{1,0:T(8,128)(2,1)S(1)}, bf16[64,1024]{1,0:T(8,128)(2,1)S(1)}, u32[]{:S(2)}, u32[]{:S(2)}) collective-permute-start(bf16[64,1024]{1,0:T(8,128)(2,1)S(1)} %copy-done.1), channel_id=1, source_target_pairs={{0,24},{8,16},{16,8},{24,0},{1,25},{9,17},{17,9},{25,1},{2,26},{10... | collective-permute-start | bytes 393224 | tf_op jit(solution)/shard_map/ppermute | solution.py:26
  14.7 7.5 %collective-permute-start.3 = (bf16[192,1024]{1,0:T(8,128)(2,1)S(1)}, bf16[192,1024]{1,0:T(8,128)(2,1)S(1)}, u32[]{:S(2)}, u32[]{:S(2)}) collective-permute-start(bf16[192,1024]{1,0:T(8,128)(2,1)S(1)} %pad_maximum_fusion), channel_id=1, source_target_pairs={{0,1},{1,0},{2,3},{3,2},{4,5},{5,4},{6,7},{7,6},{8,9},{9,8},{10,11... | collective-permute-start | bytes 1179656 | tf_op jit(solution)/shard_map/ppermute | solution.py:35
  21.5 10.5 %collective-permute-start.12 = (bf16[256,1024]{1,0:T(8,128)(2,1)S(1)}, bf16[256,1024]{1,0:T(8,128)(2,1)S(1)}, u32[]{:S(2)}, u32[]{:S(2)}) collective-permute-start(bf16[256,1024]{1,0:T(8,128)(2,1)S(1)} %constant_dynamic-update-slice_fusion.6.queries.q_mine), channel_id=1, source_target_pairs={{0,1},{1,0},{2,3},{3,2},{4,5},{5,4},{6,7},{7,6},{8,9},{9,8},{10,11... | collective-permute-start | bytes 1572872 | tf_op jit(solution)/shard_map/ppermute | solution.py:35
  21.7 2.0 %collective-permute-start.4 = (bf16[64,1024]{1,0:T(8,128)(2,1)S(1)}, bf16[64,1024]{1,0:T(8,128)(2,1)S(1)}, u32[]{:S(2)}, u32[]{:S(2)}) collective-permute-start(bf16[64,1024]{1,0:T(8,128)(2,1)S(1)} %collective-permute-done.2), channel_id=1, source_target_pairs={{0,1},{1,0},{2,3},{3,2},{4,5},{5,4},{6,7},{7,6},{8,9},{9,8},{10,11... | collective-permute-start | bytes 393224 | tf_op jit(solution)/shard_map/ppermute | solution.py:35
  24.3 5.4 %collective-permute-start.10 = (f32[1,384]{1,0:T(1,128)S(1)}, f32[1,384]{1,0:T(1,128)S(1)}, u32[]{:S(2)}, u32[]{:S(2)}) collective-permute-start(f32[1,384]{1,0:T(1,128)S(1)} %get-tuple-element.29.s0.stats), channel_id=1, source_target_pairs={{0,24},{8,16},{16,8},{24,0},{1,25},{9,17},{17,9},{25,1},{2,26},{10... | collective-permute-start | bytes 4616 | tf_op jit(solution)/shard_map/ppermute | solution.py:26
  24.5 5.2 %collective-permute-start.8 = (f32[1,384]{1,0:T(1,128)S(1)}, f32[1,384]{1,0:T(1,128)S(1)}, u32[]{:S(2)}, u32[]{:S(2)}) collective-permute-start(f32[1,384]{1,0:T(1,128)S(1)} %get-tuple-element.29.s0.stats), channel_id=1, source_target_pairs={{0,8},{8,0},{16,24},{24,16},{1,9},{9,1},{17,25},{25,17},{2,10},{10... | collective-permute-start | bytes 4616 | tf_op jit(solution)/shard_map/ppermute | solution.py:26
  26.1 4.5 %collective-permute-start.9 = (f32[1,384]{1,0:T(1,128)S(1)}, f32[1,384]{1,0:T(1,128)S(1)}, u32[]{:S(2)}, u32[]{:S(2)}) collective-permute-start(f32[1,384]{1,0:T(1,128)S(1)} %get-tuple-element.29.s0.stats), channel_id=1, source_target_pairs={{0,16},{8,24},{16,0},{24,8},{1,17},{9,25},{17,1},{25,9},{2,18},{10... | collective-permute-start | bytes 4616 | tf_op jit(solution)/shard_map/ppermute | solution.py:26
  31.0 1.4 %collective-permute-start.11 = (bf16[264,256]{1,0:T(8,128)(2,1)S(1)}, bf16[264,256]{1,0:T(8,128)(2,1)S(1)}, u32[]{:S(2)}, u32[]{:S(2)}) collective-permute-start(bf16[264,256]{1,0:T(8,128)(2,1)S(1)} %get-tuple-element.33.w_send), channel_id=1, source_target_pairs={{0,1},{1,0},{2,3},{3,2},{4,5},{5,4},{6,7},{7,6},{8,9},{9,8},{10,11... | collective-permute-start | bytes 405512 | tf_op jit(solution)/shard_map/ppermute | solution.py:35
  31.5 7.5 %collective-permute-start.13 = (bf16[64,1024]{1,0:T(8,128)(2,1)S(1)}, bf16[64,1024]{1,0:T(8,128)(2,1)S(1)}, u32[]{:S(2)}, u32[]{:S(2)}) collective-permute-start(bf16[64,1024]{1,0:T(8,128)(2,1)S(1)} %get-tuple-element.38), channel_id=1, source_target_pairs={{0,8},{8,0},{16,24},{24,16},{1,9},{9,1},{17,25},{25,17},{2,10},{10... | collective-permute-start | bytes 393224 | tf_op jit(solution)/shard_map/ppermute | solution.py:26
  32.8 15.6 %collective-permute-start.16 = (bf16[520,128]{1,0:T(8,128)(2,1)S(1)}, bf16[520,128]{1,0:T(8,128)(2,1)S(1)}, u32[]{:S(2)}, u32[]{:S(2)}) collective-permute-start(bf16[520,128]{1,0:T(8,128)(2,1)S(1)} %get-tuple-element.41), channel_id=1, source_target_pairs={{0,2},{2,0},{4,6},{6,4},{1,3},{3,1},{5,7},{7,5},{8,10},{10,8},{12,... | collective-permute-start | bytes 399368 | tf_op jit(solution)/shard_map/ppermute | solution.py:26
  34.4 14.1 %collective-permute-start.17 = (bf16[520,128]{1,0:T(8,128)(2,1)S(1)}, bf16[520,128]{1,0:T(8,128)(2,1)S(1)}, u32[]{:S(2)}, u32[]{:S(2)}) collective-permute-start(bf16[520,128]{1,0:T(8,128)(2,1)S(1)} %get-tuple-element.42), channel_id=1, source_target_pairs={{0,4},{2,6},{4,0},{6,2},{1,5},{3,7},{5,1},{7,3},{8,12},{10,14},{12... | collective-permute-start | bytes 399368 | tf_op jit(solution)/shard_map/ppermute | solution.py:26
  35.9 12.5 %collective-permute-start.18 = (bf16[520,128]{1,0:T(8,128)(2,1)S(1)}, bf16[520,128]{1,0:T(8,128)(2,1)S(1)}, u32[]{:S(2)}, u32[]{:S(2)}) collective-permute-start(bf16[520,128]{1,0:T(8,128)(2,1)S(1)} %get-tuple-element.43), channel_id=1, source_target_pairs={{0,6},{2,4},{4,2},{6,0},{1,7},{3,5},{5,3},{7,1},{8,14},{10,12},{12... | collective-permute-start | bytes 399368 | tf_op jit(solution)/shard_map/ppermute | solution.py:26
  36.4 12.0 %collective-permute-start.14 = (bf16[64,1024]{1,0:T(8,128)(2,1)S(1)}, bf16[64,1024]{1,0:T(8,128)(2,1)S(1)}, u32[]{:S(2)}, u32[]{:S(2)}) collective-permute-start(bf16[64,1024]{1,0:T(8,128)(2,1)S(1)} %get-tuple-element.39), channel_id=1, source_target_pairs={{0,16},{8,24},{16,0},{24,8},{1,17},{9,25},{17,1},{25,9},{2,18},{10... | collective-permute-start | bytes 393224 | tf_op jit(solution)/shard_map/ppermute | solution.py:26
  39.0 9.4 %collective-permute-start.15 = (bf16[64,1024]{1,0:T(8,128)(2,1)S(1)}, bf16[64,1024]{1,0:T(8,128)(2,1)S(1)}, u32[]{:S(2)}, u32[]{:S(2)}) collective-permute-start(bf16[64,1024]{1,0:T(8,128)(2,1)S(1)} %get-tuple-element.40), channel_id=1, source_target_pairs={{0,24},{8,16},{16,8},{24,0},{1,25},{9,17},{17,9},{25,1},{2,26},{10... | collective-permute-start | bytes 393224 | tf_op jit(solution)/shard_map/ppermute | solution.py:26

commit v6 on v5

--- a/solution.py
+++ b/solution.py
@@ -172,17 +172,19 @@
     stats[:, cols:] = jnp.broadcast_to(jnp.sum(run[1:2, :rows], 1, keepdims=True), (1, LANES))
 
 
-def share_kernel(scale, rows, scores, stats, docs, *outs):
-    cols = scores.shape[1]
-    lse = stats[0:1, :cols]
+def share_kernel(scale, rows, blocks, scores, stats, docs, *outs):
+    low = min(blocks) // 2 * 2 * rows
+    high = (max(blocks) // 2 + 1) * 2 * rows
+    lse = stats[0:1, low:high]
     total = None
     for at in range(0, scores.shape[0], 2 * CHUNK):
-        probs = jnp.exp(scores[at : at + 2 * CHUNK, :] - lse)
-        part = contract(jnp.transpose(probs)[rows:].astype(BF16), docs[at : at + 2 * CHUNK, :], 1, 0)
+        probs = jnp.transpose(jnp.exp(scores[at : at + 2 * CHUNK, low:high] - lse)).astype(BF16)
+        probs = jnp.concatenate([probs[k * rows - low : (k + 1) * rows - low] for k in blocks], 0)
+        part = contract(probs, docs[at : at + 2 * CHUNK, :], 1, 0)
         total = part if total is None else total + part
     total = (total * scale).astype(BF16)
-    for k, out in enumerate(outs):
-        out[...] = total[k * rows : (k + 1) * rows]
+    for i, out in enumerate(outs):
+        out[...] = total[i * rows : (i + 1) * rows]
 
 
 def weight_kernel(batch_rows, rows, scores, s0, s1, s2, s3, counts, total, positive, *outs):
@@ -329,8 +331,12 @@
     )
     stats_all = send_pieces([stats] * quarters, "quarter")
     q_other = swap_cores(q_mine)
-    shares = call(functools.partial(share_kernel, scale, rows), [piece] * (quarters - 1), scores, stats, docs)
-    q_got = send_pieces([None] + list(shares), "quarter")
+    shares = [None] * quarters
+    for blocks in ((2,), tuple(k for k in range(1, quarters) if k != 2)):
+        outs = call(functools.partial(share_kernel, scale, rows, blocks), [piece] * len(blocks), scores, stats, docs)
+        for k, out in zip(blocks, outs):
+            shares[k] = out
+    q_got = send_pieces(shares, "quarter")
 
     w_mine, w_send, gains, line_loss = call(
         functools.partial(weight_kernel, batch_rows, rows),

time: 49.9 us -> 49.3 us (0.988)
  waiting for transfers between devices: 18.5 us -> 17 us
  starting transfers between devices: 22 us -> 23 us
    ppermute x15, waiting for transfers between devices: 16.7 us -> 15.6 us  [send_pieces(): out[k] = lax.ppermute(pieces[k], axes, [(i, i ^ k) for i in range(count)])]
    ppermute x15, starting transfers between devices: 21.3 us -> 22.2 us  [send_pieces(): out[k] = lax.ppermute(pieces[k], axes, [(i, i ^ k) for i in range(count)])]
    pallas_call x7 -> x8, Pallas kernels: 4.42 us -> 4.71 us  [call(): pl.pallas_call(kernel, out_shape=[jax.ShapeDtypeStruct(shape, dtype) for...]
  transfers between devices with their start and end apart: 19 -> 19, of which waited for: 7 -> 8; matrix products, arithmetic and copies ran while one was open for 0% -> 0% of each run, Pallas kernels for 7% -> 8%
where the time goes in v6:
time: 49.3 us; the launch traced here: 49.1 us
  starting transfers between devices  23 us (47%)
  waiting for transfers between devices  17 us (34%)
  Pallas kernels  4.71 us (10%)
  local copies, waits for them, and re-layouts  3.53 us (7%)
  between operations  0.83 us (2%)
    ppermute x15, starting transfers between devices, send_pieces(): out[k] = lax.ppermute(pieces[k], axes, [(i, i ^ k) for i in range(count)])  22.2 us
    ppermute x15, waiting for transfers between devices, send_pieces(): out[k] = lax.ppermute(pieces[k], axes, [(i, i ^ k) for i in range(count)])  15.6 us
    pallas_call x8, Pallas kernels, call(): pl.pallas_call(kernel, out_shape=[jax.ShapeDtypeStruct(shape, dtype) for...  4.71 us
    unnamed x16, local copies, waits for them, and re-layouts  3.51 us
    ppermute x4, waiting for transfers between devices, swap_cores(): return lax.ppermute(array, 'core', [(0, 1), (1, 0)])  1.43 us
  transfers between devices with their start and end apart: 19, of which 8 were waited for; matrix products, arithmetic and copies ran while one was open for 0% of the time, Pallas kernels for 8%

profile of v6, /device:TPU:0, one launch (start us, length us, event | category | flops | bytes accessed | tf_op | source)
XLA Modules:
  0.0 49.1 jit_solution(12670266397253899454)
XLA Ops:
  0.6 4.0 %collective-permute-start = (bf16[64,1024]{1,0:T(8,128)(2,1)}, bf16[64,1024]{1,0:T(8,128)(2,1)S(1)}, u32[]{:S(2)}, u32[]{:S(2)}) collective-permute-start(bf16[64,1024]{1,0:T(8,128)(2,1)} %documents.1), channel_id=1, source_target_pairs={{0,6},{2,4},{4,2},{6,0},{1,7},{3,5},{5,3},{7,1},{8,14},{10,12},{12... | collective-permute-start | bytes 393224 | tf_op jit(solution)/shard_map/ppermute | solution.py:26
  4.6 0.5 %collective-permute-start.1 = (bf16[64,1024]{1,0:T(8,128)(2,1)}, bf16[64,1024]{1,0:T(8,128)(2,1)S(1)}, u32[]{:S(2)}, u32[]{:S(2)}) collective-permute-start(bf16[64,1024]{1,0:T(8,128)(2,1)} %documents.1), channel_id=1, source_target_pairs={{0,4},{2,6},{4,0},{6,2},{1,5},{3,7},{5,1},{7,3},{8,12},{10,14},{12... | collective-permute-start | bytes 393224 | tf_op jit(solution)/shard_map/ppermute | solution.py:26
  5.1 0.1 collective-permute-start.2
  5.3 2.0 %collective-permute-start.5 = (bf16[64,1024]{1,0:T(8,128)(2,1)}, bf16[64,1024]{1,0:T(8,128)(2,1)S(1)}, u32[]{:S(2)}, u32[]{:S(2)}) collective-permute-start(bf16[64,1024]{1,0:T(8,128)(2,1)} %queries.1), channel_id=1, source_target_pairs={{0,8},{8,0},{16,24},{24,16},{1,9},{9,1},{17,25},{25,17},{2,10},{10... | collective-permute-start | bytes 393224 | tf_op jit(solution)/shard_map/ppermute | solution.py:26
  7.2 2.6 %collective-permute-start.6 = (bf16[64,1024]{1,0:T(8,128)(2,1)}, bf16[64,1024]{1,0:T(8,128)(2,1)S(1)}, u32[]{:S(2)}, u32[]{:S(2)}) collective-permute-start(bf16[64,1024]{1,0:T(8,128)(2,1)} %queries.1), channel_id=1, source_target_pairs={{0,16},{8,24},{16,0},{24,8},{1,17},{9,25},{17,1},{25,9},{2,18},{10... | collective-permute-start | bytes 393224 | tf_op jit(solution)/shard_map/ppermute | solution.py:26
  9.8 0.0 copy-start
  9.8 0.9 %copy-done = bf16[64,1024]{1,0:T(8,128)(2,1)S(1)} copy-done((bf16[64,1024]{1,0:T(8,128)(2,1)S(1)}, bf16[64,1024]{1,0:T(8,128)(2,1)}, u32[]{:S(2)}) %copy-start) | copy-done | bytes 131096
  10.8 0.0 copy-start.2
  10.8 0.9 %copy-done.2 = bf16[64,1024]{1,0:T(8,128)(2,1)S(1)} copy-done((bf16[64,1024]{1,0:T(8,128)(2,1)S(1)}, bf16[64,1024]{1,0:T(8,128)(2,1)}, u32[]{:S(2)}) %copy-start.2) | copy-done | bytes 131096
  11.7 0.0 copy-start.3
  11.7 0.7 %copy-done.3 = s32[2048]{0:T(1024)S(1)} copy-done((s32[2048]{0:T(1024)S(1)}, s32[2048]{0:T(1024)}, u32[]{:S(2)}) %copy-start.3) | copy-done | bytes 8216
  12.4 1.3 %shard_map.58 = (f32[1,256]{1,0:T(1,128)S(1)}, f32[8,256]{1,0:T(8,128)S(1)}, f32[512,64]{1,0:T(8,128)S(1)}, bf16[64,1024]{1,0:T(8,128)(2,1)S(1)}, bf16[64,1024]{1,0:T(8,128)(2,1)S(1)}) custom-call(s32[16,128]{1,0:T(8,128)S(1)} %bitcast.3, bf16[64,1024]{1,0:T(8,128)(2,1)S(1)} %copy-done, bf16[64,1024]{1,0:T(8,128)(2,1)S(1)} %copy-done.2), custom_call_target="tpu_custom_call" | custom-call | tf_op jit(solution)/shard_map/pallas_call | solution.py:56
  13.7 0.0 copy-start.1
  13.8 0.0 collective-permute-done
  13.8 0.9 %copy-done.1 = bf16[64,1024]{1,0:T(8,128)(2,1)S(1)} copy-done((bf16[64,1024]{1,0:T(8,128)(2,1)S(1)}, bf16[64,1024]{1,0:T(8,128)(2,1)}, u32[]{:S(2)}) %copy-start.1) | copy-done | bytes 131096
  14.6 0.0 collective-permute-start.7
  14.6 0.0 collective-permute-done.1
  14.7 0.1 collective-permute-start.3
  14.8 0.0 collective-permute-done.5
  14.8 0.5 %collective-permute-done.6 = bf16[64,1024]{1,0:T(8,128)(2,1)S(1)} collective-permute-done((bf16[64,1024]{1,0:T(8,128)(2,1)}, bf16[64,1024]{1,0:T(8,128)(2,1)S(1)}, u32[]{:S(2)}, u32[]{:S(2)}) %collective-permute-start.6) | collective-permute-done | bytes 131104 | tf_op jit(solution)/shard_map/ppermute | solution.py:26
  15.4 6.2 %collective-permute-done.7 = bf16[64,1024]{1,0:T(8,128)(2,1)S(1)} collective-permute-done((bf16[64,1024]{1,0:T(8,128)(2,1)S(1)}, bf16[64,1024]{1,0:T(8,128)(2,1)S(1)}, u32[]{:S(2)}, u32[]{:S(2)}) %collective-permute-start.7) | collective-permute-done | bytes 131104 | tf_op jit(solution)/shard_map/ppermute | solution.py:26
  21.5 0.1 collective-permute-start.12
  21.6 0.0 collective-permute-done.2
  21.7 0.6 %collective-permute-start.4 = (bf16[64,1024]{1,0:T(8,128)(2,1)S(1)}, bf16[64,1024]{1,0:T(8,128)(2,1)S(1)}, u32[]{:S(2)}, u32[]{:S(2)}) collective-permute-start(bf16[64,1024]{1,0:T(8,128)(2,1)S(1)} %collective-permute-done.2), channel_id=1, source_target_pairs={{0,1},{1,0},{2,3},{3,2},{4,5},{5,4},{6,7},{7,6},{8,9},{9,8},{10,11... | collective-permute-start | bytes 393224 | tf_op jit(solution)/shard_map/ppermute | solution.py:35
  22.2 0.0 collective-permute-done.3
  22.3 1.4 %collective-permute-done.4 = bf16[64,1024]{1,0:T(8,128)(2,1)S(1)} collective-permute-done((bf16[64,1024]{1,0:T(8,128)(2,1)S(1)}, bf16[64,1024]{1,0:T(8,128)(2,1)S(1)}, u32[]{:S(2)}, u32[]{:S(2)}) %collective-permute-start.4) | collective-permute-done | bytes 131104 | tf_op jit(solution)/shard_map/ppermute | solution.py:35
  23.7 0.6 %shard_map.59 = (f32[512,256]{1,0:T(8,128)S(1)}, f32[1,384]{1,0:T(1,128)S(1)}) custom-call(bf16[512,1024]{1,0:T(8,128)(2,1)S(1)} %constant_dynamic-update-slice_fusion.docs, bf16[256,1024]{1,0:T(8,128)(2,1)S(1)} %constant_dynamic-update-slice_fusion.6.queries.q_mine, f32[512,64]{1,0:T(8,128)S(1)} %get-tuple-element.26.positive), custom_call_target="tpu_custom_call" | custom-call | tf_op jit(solution)/shard_map/pallas_call | solution.py:56
  24.3 0.2 collective-permute-start.10
  24.5 1.6 %collective-permute-start.8 = (f32[1,384]{1,0:T(1,128)S(1)}, f32[1,384]{1,0:T(1,128)S(1)}, u32[]{:S(2)}, u32[]{:S(2)}) collective-permute-start(f32[1,384]{1,0:T(1,128)S(1)} %get-tuple-element.28.s0.stats), channel_id=1, source_target_pairs={{0,8},{8,0},{16,24},{24,16},{1,9},{9,1},{17,25},{25,17},{2,10},{10... | collective-permute-start | bytes 4616 | tf_op jit(solution)/shard_map/ppermute | solution.py:26
  26.1 2.6 %collective-permute-start.9 = (f32[1,384]{1,0:T(1,128)S(1)}, f32[1,384]{1,0:T(1,128)S(1)}, u32[]{:S(2)}, u32[]{:S(2)}) collective-permute-start(f32[1,384]{1,0:T(1,128)S(1)} %get-tuple-element.28.s0.stats), channel_id=1, source_target_pairs={{0,16},{8,24},{16,0},{24,8},{1,17},{9,25},{17,1},{25,9},{2,18},{10... | collective-permute-start | bytes 4616 | tf_op jit(solution)/shard_map/ppermute | solution.py:26
  28.8 1.0 %collective-permute-done.10.s3 = f32[1,384]{1,0:T(1,128)S(1)} collective-permute-done((f32[1,384]{1,0:T(1,128)S(1)}, f32[1,384]{1,0:T(1,128)S(1)}, u32[]{:S(2)}, u32[]{:S(2)}) %collective-permute-start.10) | collective-permute-done | bytes 1568 | tf_op jit(solution)/shard_map/ppermute | solution.py:26
  29.7 0.0 collective-permute-done.8.s1
  29.8 0.9 %collective-permute-done.9.s2 = f32[1,384]{1,0:T(1,128)S(1)} collective-permute-done((f32[1,384]{1,0:T(1,128)S(1)}, f32[1,384]{1,0:T(1,128)S(1)}, u32[]{:S(2)}, u32[]{:S(2)}) %collective-permute-start.9) | collective-permute-done | bytes 1568 | tf_op jit(solution)/shard_map/ppermute | solution.py:26
  30.6 0.4 shard_map.60
  31.0 0.1 collective-permute-start.11
  31.0 0.4 shard_map.64
  31.4 2.7 %collective-permute-start.14 = (bf16[64,1024]{1,0:T(8,128)(2,1)S(1)}, bf16[64,1024]{1,0:T(8,128)(2,1)S(1)}, u32[]{:S(2)}, u32[]{:S(2)}) collective-permute-start(bf16[64,1024]{1,0:T(8,128)(2,1)S(1)} %shard_map.64), channel_id=1, source_target_pairs={{0,16},{8,24},{16,0},{24,8},{1,17},{9,25},{17,1},{25,9},{2,18},{10... | collective-permute-start | bytes 393224 | tf_op jit(solution)/shard_map/ppermute | solution.py:26
  34.1 0.0 collective-permute-done.12.q_other
  34.1 0.0 collective-permute-done.11.w_in
  34.1 0.4 shard_map.62
  34.5 1.6 %collective-permute-start.16 = (bf16[520,128]{1,0:T(8,128)(2,1)S(1)}, bf16[520,128]{1,0:T(8,128)(2,1)S(1)}, u32[]{:S(2)}, u32[]{:S(2)}) collective-permute-start(bf16[520,128]{1,0:T(8,128)(2,1)S(1)} %get-tuple-element.39), channel_id=1, source_target_pairs={{0,2},{2,0},{4,6},{6,4},{1,3},{3,1},{5,7},{7,5},{8,10},{10,8},{12,... | collective-permute-start | bytes 399368 | tf_op jit(solution)/shard_map/ppermute | solution.py:26
  36.1 1.5 %collective-permute-start.17 = (bf16[520,128]{1,0:T(8,128)(2,1)S(1)}, bf16[520,128]{1,0:T(8,128)(2,1)S(1)}, u32[]{:S(2)}, u32[]{:S(2)}) collective-permute-start(bf16[520,128]{1,0:T(8,128)(2,1)S(1)} %get-tuple-element.40), channel_id=1, source_target_pairs={{0,4},{2,6},{4,0},{6,2},{1,5},{3,7},{5,1},{7,3},{8,12},{10,14},{12... | collective-permute-start | bytes 399368 | tf_op jit(solution)/shard_map/ppermute | solution.py:26
  37.6 0.5 collective-permute-start.18
  38.1 0.4 shard_map.63
  38.5 0.1 collective-permute-start.13
  38.6 2.4 %collective-permute-done.14.refs_1_ = bf16[64,1024]{1,0:T(8,128)(2,1)S(1)} collective-permute-done((bf16[64,1024]{1,0:T(8,128)(2,1)S(1)}, bf16[64,1024]{1,0:T(8,128)(2,1)S(1)}, u32[]{:S(2)}, u32[]{:S(2)}) %collective-permute-start.14) | collective-permute-done | bytes 131104 | tf_op jit(solution)/shard_map/ppermute | solution.py:26
  41.0 2.3 %collective-permute-start.15 = (bf16[64,1024]{1,0:T(8,128)(2,1)S(1)}, bf16[64,1024]{1,0:T(8,128)(2,1)S(1)}, u32[]{:S(2)}, u32[]{:S(2)}) collective-permute-start(bf16[64,1024]{1,0:T(8,128)(2,1)S(1)} %get-tuple-element.38), channel_id=1, source_target_pairs={{0,24},{8,16},{16,8},{24,0},{1,25},{9,17},{17,9},{25,1},{2,26},{10... | collective-permute-start | bytes 393224 | tf_op jit(solution)/shard_map/ppermute | solution.py:26
  43.2 0.3 shard_map.61.own_query
  43.6 0.2 collective-permute-done.13.refs_0_
  43.7 4.5 %collective-permute-done.15.refs_2_ = bf16[64,1024]{1,0:T(8,128)(2,1)S(1)} collective-permute-done((bf16[64,1024]{1,0:T(8,128)(2,1)S(1)}, bf16[64,1024]{1,0:T(8,128)(2,1)S(1)}, u32[]{:S(2)}, u32[]{:S(2)}) %collective-permute-start.15) | collective-permute-done | bytes 131104 | tf_op jit(solution)/shard_map/ppermute | solution.py:26
  48.2 0.0 collective-permute-done.16.refs_3_
  48.2 0.0 collective-permute-done.17.refs_4_
  48.2 0.0 collective-permute-done.18.refs_5_
  48.2 0.9 %shard_map.65 = (bf16[64,1024]{1,0:T(8,128)(2,1)}, bf16[64,1024]{1,0:T(8,128)(2,1)}, f32[1,128]{1,0:T(1,128)}) custom-call(f32[64,1024]{1,0:T(8,128)S(1)} %shard_map.61.own_query, f32[64,8]{1,0:T(8,128)S(1)} %get-tuple-element.33.gains, f32[64,1024]{1,0:T(8,128)S(1)} %get-tuple-element.35.own, f32[8,128]{1,0:T(8,128)S(1)} %get-tuple-element.36.chip_loss, ...), custom_call_target="tpu_custom_call" | custom-call | tf_op jit(solution)/shard_map/pallas_call | solution.py:56
  (11 shorter events, 0.1 us)
Async XLA Ops:
  0.6 13.1 %collective-permute-start = (bf16[64,1024]{1,0:T(8,128)(2,1)}, bf16[64,1024]{1,0:T(8,128)(2,1)S(1)}, u32[]{:S(2)}, u32[]{:S(2)}) collective-permute-start(bf16[64,1024]{1,0:T(8,128)(2,1)} %documents.1), channel_id=1, source_target_pairs={{0,6},{2,4},{4,2},{6,0},{1,7},{3,5},{5,3},{7,1},{8,14},{10,12},{12... | collective-permute-start | bytes 393224 | tf_op jit(solution)/shard_map/ppermute | solution.py:26
  4.6 10.0 %collective-permute-start.1 = (bf16[64,1024]{1,0:T(8,128)(2,1)}, bf16[64,1024]{1,0:T(8,128)(2,1)S(1)}, u32[]{:S(2)}, u32[]{:S(2)}) collective-permute-start(bf16[64,1024]{1,0:T(8,128)(2,1)} %documents.1), channel_id=1, source_target_pairs={{0,4},{2,6},{4,0},{6,2},{1,5},{3,7},{5,1},{7,3},{8,12},{10,14},{12... | collective-permute-start | bytes 393224 | tf_op jit(solution)/shard_map/ppermute | solution.py:26
  5.1 16.5 %collective-permute-start.2 = (bf16[64,1024]{1,0:T(8,128)(2,1)}, bf16[64,1024]{1,0:T(8,128)(2,1)S(1)}, u32[]{:S(2)}, u32[]{:S(2)}) collective-permute-start(bf16[64,1024]{1,0:T(8,128)(2,1)} %documents.1), channel_id=1, source_target_pairs={{0,2},{2,0},{4,6},{6,4},{1,3},{3,1},{5,7},{7,5},{8,10},{10,8},{12,... | collective-permute-start | bytes 393224 | tf_op jit(solution)/shard_map/ppermute | solution.py:26
  5.3 9.5 %collective-permute-start.5 = (bf16[64,1024]{1,0:T(8,128)(2,1)}, bf16[64,1024]{1,0:T(8,128)(2,1)S(1)}, u32[]{:S(2)}, u32[]{:S(2)}) collective-permute-start(bf16[64,1024]{1,0:T(8,128)(2,1)} %queries.1), channel_id=1, source_target_pairs={{0,8},{8,0},{16,24},{24,16},{1,9},{9,1},{17,25},{25,17},{2,10},{10... | collective-permute-start | bytes 393224 | tf_op jit(solution)/shard_map/ppermute | solution.py:26
  7.2 8.1 %collective-permute-start.6 = (bf16[64,1024]{1,0:T(8,128)(2,1)}, bf16[64,1024]{1,0:T(8,128)(2,1)S(1)}, u32[]{:S(2)}, u32[]{:S(2)}) collective-permute-start(bf16[64,1024]{1,0:T(8,128)(2,1)} %queries.1), channel_id=1, source_target_pairs={{0,16},{8,24},{16,0},{24,8},{1,17},{9,25},{17,1},{25,9},{2,18},{10... | collective-permute-start | bytes 393224 | tf_op jit(solution)/shard_map/ppermute | solution.py:26
  9.8 0.9 %copy-start = (bf16[64,1024]{1,0:T(8,128)(2,1)S(1)}, bf16[64,1024]{1,0:T(8,128)(2,1)}, u32[]{:S(2)}) copy-start(bf16[64,1024]{1,0:T(8,128)(2,1)} %queries.1) | copy-start | bytes 393220
  10.8 0.9 %copy-start.2 = (bf16[64,1024]{1,0:T(8,128)(2,1)S(1)}, bf16[64,1024]{1,0:T(8,128)(2,1)}, u32[]{:S(2)}) copy-start(bf16[64,1024]{1,0:T(8,128)(2,1)} %documents.1) | copy-start | bytes 393220
  11.7 0.7 %copy-start.3 = (s32[2048]{0:T(1024)S(1)}, s32[2048]{0:T(1024)}, u32[]{:S(2)}) copy-start(s32[2048]{0:T(1024)} %param.5) | copy-start | bytes 24580
  13.7 0.9 %copy-start.1 = (bf16[64,1024]{1,0:T(8,128)(2,1)S(1)}, bf16[64,1024]{1,0:T(8,128)(2,1)}, u32[]{:S(2)}) copy-start(bf16[64,1024]{1,0:T(8,128)(2,1)} %queries.1) | copy-start | bytes 393220
  14.6 6.9 %collective-permute-start.7 = (bf16[64,1024]{1,0:T(8,128)(2,1)S(1)}, bf16[64,1024]{1,0:T(8,128)(2,1)S(1)}, u32[]{:S(2)}, u32[]{:S(2)}) collective-permute-start(bf16[64,1024]{1,0:T(8,128)(2,1)S(1)} %copy-done.1), channel_id=1, source_target_pairs={{0,24},{8,16},{16,8},{24,0},{1,25},{9,17},{17,9},{25,1},{2,26},{10... | collective-permute-start | bytes 393224 | tf_op jit(solution)/shard_map/ppermute | solution.py:26
  14.7 7.5 %collective-permute-start.3 = (bf16[192,1024]{1,0:T(8,128)(2,1)S(1)}, bf16[192,1024]{1,0:T(8,128)(2,1)S(1)}, u32[]{:S(2)}, u32[]{:S(2)}) collective-permute-start(bf16[192,1024]{1,0:T(8,128)(2,1)S(1)} %pad_maximum_fusion), channel_id=1, source_target_pairs={{0,1},{1,0},{2,3},{3,2},{4,5},{5,4},{6,7},{7,6},{8,9},{9,8},{10,11... | collective-permute-start | bytes 1179656 | tf_op jit(solution)/shard_map/ppermute | solution.py:35
  21.5 12.6 %collective-permute-start.12 = (bf16[256,1024]{1,0:T(8,128)(2,1)S(1)}, bf16[256,1024]{1,0:T(8,128)(2,1)S(1)}, u32[]{:S(2)}, u32[]{:S(2)}) collective-permute-start(bf16[256,1024]{1,0:T(8,128)(2,1)S(1)} %constant_dynamic-update-slice_fusion.6.queries.q_mine), channel_id=1, source_target_pairs={{0,1},{1,0},{2,3},{3,2},{4,5},{5,4},{6,7},{7,6},{8,9},{9,8},{10,11... | collective-permute-start | bytes 1572872 | tf_op jit(solution)/shard_map/ppermute | solution.py:35
  21.7 2.0 %collective-permute-start.4 = (bf16[64,1024]{1,0:T(8,128)(2,1)S(1)}, bf16[64,1024]{1,0:T(8,128)(2,1)S(1)}, u32[]{:S(2)}, u32[]{:S(2)}) collective-permute-start(bf16[64,1024]{1,0:T(8,128)(2,1)S(1)} %collective-permute-done.2), channel_id=1, source_target_pairs={{0,1},{1,0},{2,3},{3,2},{4,5},{5,4},{6,7},{7,6},{8,9},{9,8},{10,11... | collective-permute-start | bytes 393224 | tf_op jit(solution)/shard_map/ppermute | solution.py:35
  24.3 5.4 %collective-permute-start.10 = (f32[1,384]{1,0:T(1,128)S(1)}, f32[1,384]{1,0:T(1,128)S(1)}, u32[]{:S(2)}, u32[]{:S(2)}) collective-permute-start(f32[1,384]{1,0:T(1,128)S(1)} %get-tuple-element.28.s0.stats), channel_id=1, source_target_pairs={{0,24},{8,16},{16,8},{24,0},{1,25},{9,17},{17,9},{25,1},{2,26},{10... | collective-permute-start | bytes 4616 | tf_op jit(solution)/shard_map/ppermute | solution.py:26
  24.5 5.2 %collective-permute-start.8 = (f32[1,384]{1,0:T(1,128)S(1)}, f32[1,384]{1,0:T(1,128)S(1)}, u32[]{:S(2)}, u32[]{:S(2)}) collective-permute-start(f32[1,384]{1,0:T(1,128)S(1)} %get-tuple-element.28.s0.stats), channel_id=1, source_target_pairs={{0,8},{8,0},{16,24},{24,16},{1,9},{9,1},{17,25},{25,17},{2,10},{10... | collective-permute-start | bytes 4616 | tf_op jit(solution)/shard_map/ppermute | solution.py:26
  26.1 4.5 %collective-permute-start.9 = (f32[1,384]{1,0:T(1,128)S(1)}, f32[1,384]{1,0:T(1,128)S(1)}, u32[]{:S(2)}, u32[]{:S(2)}) collective-permute-start(f32[1,384]{1,0:T(1,128)S(1)} %get-tuple-element.28.s0.stats), channel_id=1, source_target_pairs={{0,16},{8,24},{16,0},{24,8},{1,17},{9,25},{17,1},{25,9},{2,18},{10... | collective-permute-start | bytes 4616 | tf_op jit(solution)/shard_map/ppermute | solution.py:26
  31.0 3.1 %collective-permute-start.11 = (bf16[264,256]{1,0:T(8,128)(2,1)S(1)}, bf16[264,256]{1,0:T(8,128)(2,1)S(1)}, u32[]{:S(2)}, u32[]{:S(2)}) collective-permute-start(bf16[264,256]{1,0:T(8,128)(2,1)S(1)} %get-tuple-element.32.w_send), channel_id=1, source_target_pairs={{0,1},{1,0},{2,3},{3,2},{4,5},{5,4},{6,7},{7,6},{8,9},{9,8},{10,11... | collective-permute-start | bytes 405512 | tf_op jit(solution)/shard_map/ppermute | solution.py:35
  31.4 9.6 %collective-permute-start.14 = (bf16[64,1024]{1,0:T(8,128)(2,1)S(1)}, bf16[64,1024]{1,0:T(8,128)(2,1)S(1)}, u32[]{:S(2)}, u32[]{:S(2)}) collective-permute-start(bf16[64,1024]{1,0:T(8,128)(2,1)S(1)} %shard_map.64), channel_id=1, source_target_pairs={{0,16},{8,24},{16,0},{24,8},{1,17},{9,25},{17,1},{25,9},{2,18},{10... | collective-permute-start | bytes 393224 | tf_op jit(solution)/shard_map/ppermute | solution.py:26
  34.5 13.7 %collective-permute-start.16 = (bf16[520,128]{1,0:T(8,128)(2,1)S(1)}, bf16[520,128]{1,0:T(8,128)(2,1)S(1)}, u32[]{:S(2)}, u32[]{:S(2)}) collective-permute-start(bf16[520,128]{1,0:T(8,128)(2,1)S(1)} %get-tuple-element.39), channel_id=1, source_target_pairs={{0,2},{2,0},{4,6},{6,4},{1,3},{3,1},{5,7},{7,5},{8,10},{10,8},{12,... | collective-permute-start | bytes 399368 | tf_op jit(solution)/shard_map/ppermute | solution.py:26
  36.1 12.1 %collective-permute-start.17 = (bf16[520,128]{1,0:T(8,128)(2,1)S(1)}, bf16[520,128]{1,0:T(8,128)(2,1)S(1)}, u32[]{:S(2)}, u32[]{:S(2)}) collective-permute-start(bf16[520,128]{1,0:T(8,128)(2,1)S(1)} %get-tuple-element.40), channel_id=1, source_target_pairs={{0,4},{2,6},{4,0},{6,2},{1,5},{3,7},{5,1},{7,3},{8,12},{10,14},{12... | collective-permute-start | bytes 399368 | tf_op jit(solution)/shard_map/ppermute | solution.py:26
  37.6 10.6 %collective-permute-start.18 = (bf16[520,128]{1,0:T(8,128)(2,1)S(1)}, bf16[520,128]{1,0:T(8,128)(2,1)S(1)}, u32[]{:S(2)}, u32[]{:S(2)}) collective-permute-start(bf16[520,128]{1,0:T(8,128)(2,1)S(1)} %get-tuple-element.41), channel_id=1, source_target_pairs={{0,6},{2,4},{4,2},{6,0},{1,7},{3,5},{5,3},{7,1},{8,14},{10,12},{12... | collective-permute-start | bytes 399368 | tf_op jit(solution)/shard_map/ppermute | solution.py:26
  38.5 5.3 %collective-permute-start.13 = (bf16[64,1024]{1,0:T(8,128)(2,1)S(1)}, bf16[64,1024]{1,0:T(8,128)(2,1)S(1)}, u32[]{:S(2)}, u32[]{:S(2)}) collective-permute-start(bf16[64,1024]{1,0:T(8,128)(2,1)S(1)} %get-tuple-element.37), channel_id=1, source_target_pairs={{0,8},{8,0},{16,24},{24,16},{1,9},{9,1},{17,25},{25,17},{2,10},{10... | collective-permute-start | bytes 393224 | tf_op jit(solution)/shard_map/ppermute | solution.py:26
  41.0 7.2 %collective-permute-start.15 = (bf16[64,1024]{1,0:T(8,128)(2,1)S(1)}, bf16[64,1024]{1,0:T(8,128)(2,1)S(1)}, u32[]{:S(2)}, u32[]{:S(2)}) collective-permute-start(bf16[64,1024]{1,0:T(8,128)(2,1)S(1)} %get-tuple-element.38), channel_id=1, source_target_pairs={{0,24},{8,16},{16,8},{24,0},{1,25},{9,17},{17,9},{25,1},{2,26},{10... | collective-permute-start | bytes 393224 | tf_op jit(solution)/shard_map/ppermute | solution.py:26
